TPU v7x, 32 devices: a whole 2x2x4 slice. The times are simulated.
32 devices in a mesh: dp: 8 (over z, y), tensor: 4 (over x, core).
Axes of the slice: x: 2, y: 2, z: 4, core: 2. Of those that a mesh axis runs over, the one named last changes fastest.
Arguments:
- tokens: bfloat16 [16384, 768], P(('dp', 'tensor')), may hold values from -6 to 6
- cotangent: bfloat16 [16384, 768], P(('dp', 'tensor')), may hold values from -6 to 6
- seq_lengths: int32 [8], P('dp'), may hold values from 1 to 2048, 8192 in all
- norm1_gain: float32 [768], replicated, may hold values from 0.5 to 1.5
- norm1_bias: float32 [768], replicated, may hold values from -1.75 to 1.75
- norm2_gain: float32 [768], replicated, may hold values from 0.5 to 1.5
- norm2_bias: float32 [768], replicated, may hold values from -1.75 to 1.75
- w_qkv: bfloat16 [768, 3, 768], P('dp', None, 'tensor'), may hold values from -3 to 3
- b_qkv: float32 [3, 768], P(None, 'tensor'), may hold values from -1.75 to 1.75
- w_attn_out: bfloat16 [768, 768], P('tensor', 'dp'), may hold values from -0.875 to 0.875
- w_in: bfloat16 [768, 3072], P('dp', 'tensor'), may hold values from -0.21875 to 0.21875
- b_in: float32 [3072], P('tensor'), may hold values from -3 to 3
- w_down: bfloat16 [3072, 768], P('tensor', 'dp'), may hold values from -0.109375 to 0.109375
- b_out: float32 [768], replicated, may hold values from -3 to 3
- b_down: float32 [768], replicated, may hold values from -3 to 3
Outputs:
- output: float32 [16384, 768], P(('dp', 'tensor'))
- grad_tokens: float32 [16384, 768], P(('dp', 'tensor'))
- grad_w_qkv: float32 [768, 3, 768], P('dp', None, 'tensor')
- grad_b_qkv: float32 [3, 768], P(None, 'tensor')
- grad_w_attn_out: float32 [768, 768], P('tensor', 'dp')
- grad_w_in: float32 [768, 3072], P('dp', 'tensor')
- grad_b_in: float32 [3072], P('tensor')
- grad_w_down: float32 [3072, 768], P('tensor', 'dp')
- grad_small: float32 [5, 768], replicated
Inputs may be any that keep to these rules, and one draw needn't show every extreme that they name: `seq_lengths`: the longest sequence has exactly 2048.
All inputs are finite; a program needn't handle non-finite values. No bound on the sum of `seq_lengths` on one device may be relied on, other than what follows from the above.
Results may differ from a plain program's by a relative error of at most 0.0062.
Values may be sent and summed in bfloat16 or wider, within the bound.
A program may use at most 128 MiB of HBM per device.

v0:
```python
import math

import jax
import jax.numpy as jnp
from jax import lax
from jax.sharding import PartitionSpec as P

D = 768
HD = 64
ROT = 16
LMAX = 2048


eps_norm = 1e-05
neg_large = -1e30
inv_root_two = 1.0 / math.sqrt(2.0)
inv_root_tau = 1.0 / math.sqrt(2.0 * math.pi)
query_block = 512


def layer_norm(values):
    centre = jnp.mean(values, axis=-1, keepdims=True)
    shifted = values - centre
    variance = jnp.mean(shifted * shifted, axis=-1, keepdims=True)
    inv_std = lax.rsqrt(variance + eps_norm)
    return (shifted * inv_std, inv_std)


def rotary_tables(positions):
    head_dims = jnp.arange(HD)
    half_rot = ROT // 2
    freq_index = (head_dims % half_rot).astype(jnp.float32)
    inverse = jnp.exp(freq_index * (-2.0 * math.log(10000.0) / ROT))
    angles = positions.astype(jnp.float32)[:, None] * inverse[None, :]
    inside = (head_dims < ROT)[None, :]
    return (jnp.where(inside, jnp.cos(angles), 1.0), jnp.where(inside, jnp.sin(angles), 0.0))


def rotate(values, cosine, sine_part):
    half_rot = ROT // 2
    turned = jnp.concatenate(
        [-values[..., half_rot:ROT], values[..., :half_rot], jnp.zeros_like(values[..., ROT:])],
        axis=-1,
    )
    return values * cosine[:, None, :] + turned * sine_part[:, None, :]


def gelu_with_slope(inputs):
    normal_cdf = 0.5 * (1.0 + jax.scipy.special.erf(inputs * inv_root_two))
    density = jnp.exp(-0.5 * inputs * inputs) * inv_root_tau
    return (inputs * normal_cdf, normal_cdf + inputs * density)


def per_device(
    tokens,
    cotangent,
    seq_lengths,
    norm1_gain,
    norm1_bias,
    norm2_gain,
    norm2_bias,
    w_qkv,
    b_qkv,
    w_attn_out,
    w_in,
    b_in,
    w_down,
    b_out,
    b_down,
):
    f32 = jnp.float32
    low = jnp.bfloat16
    local_rows = tokens.shape[0]
    group_rows = local_rows * lax.axis_size("tensor")
    slot_count = seq_lengths.shape[0]
    width_local = w_qkv.shape[2]
    heads_local = width_local // HD
    block_rows = min(query_block, LMAX)
    blocks_per_slot = LMAX // block_rows
    block_count = group_rows // block_rows
    scale = HD ** (-0.5)
    slot_ids = jnp.arange(slot_count)
    local_index = lax.axis_index("tensor") * local_rows + jnp.arange(local_rows)
    local_slot = local_index // LMAX
    local_length = jnp.sum(
        jnp.where(local_slot[:, None] == slot_ids[None, :], seq_lengths[None, :], 0), axis=1
    )
    row_mask = (local_index % LMAX < local_length).astype(f32)[:, None]
    cosine, sine_part = rotary_tables(jnp.arange(group_rows) % LMAX)
    qkv_full, attn_out_full, in_full, down_full = (
        lax.all_gather(w_qkv, "dp", axis=0, tiled=True),
        lax.all_gather(w_attn_out, "dp", axis=1, tiled=True),
        lax.all_gather(w_in, "dp", axis=0, tiled=True),
        lax.all_gather(w_down, "dp", axis=1, tiled=True),
    )
    x_float = tokens.astype(f32)
    normed, inv_std = layer_norm(x_float)
    first_in, second_in = (
        lax.all_gather(
            (normed * norm1_gain + norm1_bias).astype(low), "tensor", axis=0, tiled=True
        ),
        lax.all_gather(
            (normed * norm2_gain + norm2_bias).astype(low), "tensor", axis=0, tiled=True
        ),
    )
    projected = jnp.dot(
        first_in, qkv_full.reshape(D, 3 * width_local), preferred_element_type=f32
    ).reshape(group_rows, 3, heads_local, HD) + b_qkv.reshape(1, 3, heads_local, HD)
    queries = (
        rotate(projected[:, 0], cosine, sine_part).astype(low).reshape(group_rows, width_local)
    )
    key_rows = (
        rotate(projected[:, 1], cosine, sine_part).astype(low).reshape(group_rows, width_local)
    )
    value_rows = projected[:, 2].astype(low).reshape(group_rows, width_local)

    def block_place(block_id):
        first_row = block_id * block_rows
        slot_index = block_id // blocks_per_slot
        slot_first = slot_index * LMAX
        length = seq_lengths[slot_index]
        return (first_row, slot_first, length)

    def block_scores(block_id, key_count):
        first_row, slot_first, length = block_place(block_id)
        query_pos = first_row - slot_first + jnp.arange(block_rows)
        key_pos = jnp.arange(key_count)
        allowed = (key_pos[None, :] <= query_pos[:, None]) & (key_pos[None, :] < length)
        block_query = lax.dynamic_slice_in_dim(queries, first_row, block_rows, 0).reshape(
            block_rows, heads_local, HD
        )
        block_key = key_rows.reshape(key_count, heads_local, HD)
        block_value = value_rows.reshape(key_count, heads_local, HD)
        scores = (
            jnp.einsum("qhd,khd->hqk", block_query, block_key, preferred_element_type=f32) * scale
        )
        scores = jnp.where(allowed[None], scores, neg_large)
        return (block_query, block_key, block_value, scores)

    def attend(block_id, key_count):
        block_query, block_key, block_value, scores = block_scores(block_id, key_count)
        top = jnp.max(scores, axis=-1, keepdims=True)
        log_total = top + jnp.log(jnp.sum(jnp.exp(scores - top), axis=-1, keepdims=True))
        probs_low = jnp.exp(scores - log_total).astype(low)
        mixed = jnp.einsum("hqk,khd->qhd", probs_low, block_value, preferred_element_type=f32)
        return (mixed.astype(low).reshape(block_rows, width_local), log_total[:, :, 0])

    def attend_block(block_id):
        return attend(block_id, LMAX)

    context_blocks, log_totals = lax.map(attend_block, jnp.arange(block_count))
    context = context_blocks.reshape(group_rows, width_local)
    hidden_pre = jnp.dot(second_in, in_full, preferred_element_type=f32) + b_in
    activated, slope = gelu_with_slope(hidden_pre)
    act_low = activated.astype(low)
    branches = lax.psum_scatter(
        jnp.dot(context, attn_out_full, preferred_element_type=f32)
        + jnp.dot(act_low, down_full, preferred_element_type=f32),
        "tensor",
        scatter_dimension=0,
        tiled=True,
    )
    output = x_float + row_mask * (branches + b_out + b_down)
    grad_rows = row_mask * cotangent.astype(f32)
    grad_low = lax.all_gather(grad_rows.astype(low), "tensor", axis=0, tiled=True)
    qkv_back, attn_out_back, in_back, down_back = (
        lax.all_gather(w_qkv, "dp", axis=0, tiled=True),
        lax.all_gather(w_attn_out, "dp", axis=1, tiled=True),
        lax.all_gather(w_in, "dp", axis=0, tiled=True),
        lax.all_gather(w_down, "dp", axis=1, tiled=True),
    )
    grad_attn_out = jnp.einsum("rc,rd->cd", context, grad_low, preferred_element_type=f32)
    grad_down = jnp.einsum("rf,rd->fd", act_low, grad_low, preferred_element_type=f32)
    grad_context = jnp.einsum(
        "rd,cd->rc", grad_low, attn_out_back, preferred_element_type=f32
    ).astype(low)
    grad_hidden = jnp.einsum("rd,fd->rf", grad_low, down_back, preferred_element_type=f32) * slope
    grad_hidden_low = grad_hidden.astype(low)
    grad_in_bias = jnp.sum(grad_hidden, axis=0)
    grad_in = jnp.einsum("rc,rf->cf", second_in, grad_hidden_low, preferred_element_type=f32)

    def back_compute(block_id, key_count):
        first_row, slot_first, length = block_place(block_id)
        block_query, block_key, block_value, scores = block_scores(block_id, key_count)
        probs = jnp.exp(scores - log_totals[block_id][:, :, None])
        probs_low = probs.astype(low)
        out_grad = lax.dynamic_slice_in_dim(grad_context, first_row, block_rows, 0).reshape(
            block_rows, heads_local, HD
        )
        out_rows = lax.dynamic_slice_in_dim(context, first_row, block_rows, 0).reshape(
            block_rows, heads_local, HD
        )
        grad_probs = jnp.einsum("qhd,khd->hqk", out_grad, block_value, preferred_element_type=f32)
        delta = jnp.sum(out_grad.astype(f32) * out_rows.astype(f32), axis=-1).T
        grad_scores = (probs * (grad_probs - delta[:, :, None]) * scale).astype(low)
        grad_query = jnp.einsum("hqk,khd->qhd", grad_scores, block_key, preferred_element_type=f32)
        grad_key = jnp.einsum(
            "hqk,qhd->khd", grad_scores, block_query, preferred_element_type=f32
        ).reshape(key_count, width_local)
        grad_value = jnp.einsum(
            "hqk,qhd->khd", probs_low, out_grad, preferred_element_type=f32
        ).reshape(key_count, width_local)
        return (grad_query.reshape(block_rows, width_local), grad_key, grad_value)

    def back_block(carry, block_id):
        key_total, value_total = carry
        grad_query, grad_key, grad_value = back_compute(block_id, LMAX)
        first_row, slot_first, length = block_place(block_id)
        key_total = key_total + grad_key
        value_total = value_total + grad_value
        return ((key_total, value_total), grad_query)

    start_carry = (
        jnp.zeros((group_rows, width_local), f32),
        jnp.zeros((group_rows, width_local), f32),
    )
    carry_out, query_blocks = lax.scan(back_block, start_carry, jnp.arange(block_count))
    grad_keys, grad_values = carry_out
    grad_queries = query_blocks.reshape(group_rows, heads_local, HD)
    grad_projected = jnp.stack(
        [
            rotate(grad_queries, cosine, -sine_part),
            rotate(grad_keys.reshape(group_rows, heads_local, HD), cosine, -sine_part),
            grad_values.reshape(group_rows, heads_local, HD),
        ],
        axis=1,
    )
    grad_qkv_bias = jnp.sum(grad_projected, axis=0).reshape(3, width_local)
    grad_proj_low = grad_projected.astype(low).reshape(group_rows, 3 * width_local)
    grad_qkv = jnp.einsum("rc,rk->ck", first_in, grad_proj_low, preferred_element_type=f32).reshape(
        D, 3, width_local
    )
    qkv_flat = qkv_back.reshape(D, 3 * width_local)
    first_part = jnp.einsum("rk,ck->rc", grad_proj_low, qkv_flat, preferred_element_type=f32)
    second_part = jnp.einsum("rf,cf->rc", grad_hidden_low, in_back, preferred_element_type=f32)
    grad_inputs = lax.psum_scatter(
        jnp.stack([first_part, second_part], axis=1), "tensor", scatter_dimension=0, tiled=True
    )
    grad_first = grad_inputs[:, 0]
    grad_second = grad_inputs[:, 1]
    norm_terms = [
        jnp.sum(grad_first * normed, axis=0),
        jnp.sum(grad_first, axis=0),
        jnp.sum(grad_second * normed, axis=0),
        jnp.sum(grad_second, axis=0),
    ]
    grad_normed = grad_first * norm1_gain + grad_second * norm2_gain
    small_terms = jnp.stack(norm_terms + [jnp.sum(grad_rows, axis=0)])
    grad_x = cotangent.astype(f32) + inv_std * (
        grad_normed
        - jnp.mean(grad_normed, axis=-1, keepdims=True)
        - normed * jnp.mean(grad_normed * normed, axis=-1, keepdims=True)
    )
    qkv_shard, attn_out_shard, in_shard, down_shard = (
        lax.psum_scatter(grad_qkv, "dp", scatter_dimension=0, tiled=True),
        lax.psum_scatter(grad_attn_out, "dp", scatter_dimension=1, tiled=True),
        lax.psum_scatter(grad_in, "dp", scatter_dimension=0, tiled=True),
        lax.psum_scatter(grad_down, "dp", scatter_dimension=1, tiled=True),
    )
    bias_qkv_total, bias_in_total, small_partial = lax.psum(
        (grad_qkv_bias, grad_in_bias, small_terms), "dp"
    )
    small_total = lax.psum(small_partial, "tensor")
    return (
        output,
        grad_x,
        qkv_shard,
        bias_qkv_total,
        attn_out_shard,
        in_shard,
        bias_in_total,
        down_shard,
        small_total,
    )


def solution(mesh):
    placed = (
        P(("dp", "tensor"), None),
        P(("dp", "tensor"), None),
        P("dp"),
        P(),
        P(),
        P(),
        P(),
        P("dp", None, "tensor"),
        P(None, "tensor"),
        P("tensor", "dp"),
        P("dp", "tensor"),
        P("tensor"),
        P("tensor", "dp"),
        P(),
        P(),
    )
    return jax.shard_map(
        per_device,
        mesh=mesh,
        in_specs=placed,
        out_specs=(
            P(("dp", "tensor"), None),
            P(("dp", "tensor"), None),
            P("dp", None, "tensor"),
            P(None, "tensor"),
            P("tensor", "dp"),
            P("dp", "tensor"),
            P("tensor"),
            P("tensor", "dp"),
            P(),
        ),
        check_vma=False,
    )
```

profile of v0, /device:TPU:0, one launch (start us, length us, event | category | flops | bytes accessed | tf_op | source)
XLA Modules:
  0.0 822.7 jit_solution(14073815493402586671)
XLA Ops:
  10.2 2.8 fusion.40
  17.9 35.1 %all_gather.27 = bf16[192,768]{0,1:T(8,128)(2,1)} all-gather(bf16[192,96]{0,1:T(8,128)(2,1)S(1)} %copy.34), channel_id=1, replica_groups=mesh['dp'=8,'tensor'=4] {'dp'}, dimensions={1}, use_global_device_ids=true | all-gather | bytes 331776 | tf_op jit(solution)/shard_map/all_gather | solution.py:92
  53.1 39.8 %all_gather.26 = bf16[768,3,192]{2,1,0:T(4,128)(2,1)S(1)} all-gather(bf16[96,3,192]{2,1,0:T(4,128)(2,1)S(1)} %copy.31), channel_id=1, replica_groups=mesh['dp'=8,'tensor'=4] {'dp'}, dimensions={0}, use_global_device_ids=true | all-gather | bytes 995328 | tf_op jit(solution)/shard_map/all_gather | solution.py:91
  92.9 2.1 copy.32
  95.1 3.0 fusion.63
  98.0 4.3 fusion.26
  105.9 102.6 %while.31 = (s32[]{:T(128)}, bf16[4,512,192]{1,2,0:T(8,128)(2,1)}, f32[4,3,512]{2,1,0:T(4,128)}, s32[4]{0:T(128)S(1)}, s32[1]{0:T(128)}, /*index=5*/bf16[2048,19...) while((s32[]{:T(128)}, bf16[4,512,192]{1,2,0:T(8,128)(2,1)}, ...), condition=%wide.region_5.6_spmd, body=%wide.region_2.5_spmd.sunk | while | flops 842105856 | bytes 47901100 | solution.py:151
  110.8 6.0 fusion.144
  116.8 6.8 exponential_reduce_fusion.2
  124.2 7.3 fusion.145
  137.1 6.0 fusion.144
  143.1 6.9 exponential_reduce_fusion.2
  150.6 6.4 fusion.145
  162.6 6.0 fusion.144
  168.6 6.8 exponential_reduce_fusion.2
  176.0 6.5 fusion.145
  188.0 6.0 fusion.144
  194.0 6.8 exponential_reduce_fusion.2
  201.4 6.4 fusion.145
  208.6 2.1 copy.56
  210.7 4.0 convolution_convert_fusion
  214.7 143.1 %while.32 = (s32[]{:T(128)}, f32[2048,192]{0,1:T(8,128)}, f32[2048,192]{0,1:T(8,128)S(1)}, f32[4,512,192]{1,0,2:T(4,128)}, s32[4]{0:T(128)S(1)}, /*index=5*/bf16...) while((s32[]{:T(128)}, f32[2048,192]{0,1:T(8,128)}, ...), condition=%wide.region_9.10_spmd.clone, body=%wide.region_7.9_spmd.clone.sunk | while | flops 2051933184 | bytes 101102168 | solution.py:217
  226.3 4.6 fusion.158
  230.9 5.0 multiply_convert_fusion.3
  235.9 2.0 fusion.161
  242.2 8.6 %dynamic_update_slice.29 = f32[4,512,192]{1,0,2:T(4,128)} dynamic-update-slice(f32[4,512,192]{1,0,2:T(4,128)} %get-tuple-element.600, f32[1,512,192]{1,0,2:T(1,128)S(1)} %copy.58, s32[]{:T(128)S(6)} %copy.75, s32[]{:T(128)} %constant.214.clone.1..sunk.1, s32[]{:T(128)} %constant.214.clone.1..sunk.1) | dynamic-update-slice | bytes 786436 | tf_op jit(solution)/shard_map/while/body/jit(dynamic_update_index_in_dim)/dynamic_update_slice | solution.py:217
  261.9 4.6 fusion.158
  266.5 5.0 multiply_convert_fusion.3
  271.5 2.0 fusion.161
  277.8 8.6 %dynamic_update_slice.29 = f32[4,512,192]{1,0,2:T(4,128)} dynamic-update-slice(f32[4,512,192]{1,0,2:T(4,128)} %get-tuple-element.600, f32[1,512,192]{1,0,2:T(1,128)S(1)} %copy.58, s32[]{:T(128)S(6)} %copy.75, s32[]{:T(128)} %constant.214.clone.1..sunk.1, s32[]{:T(128)} %constant.214.clone.1..sunk.1) | dynamic-update-slice | bytes 786436 | tf_op jit(solution)/shard_map/while/body/jit(dynamic_update_index_in_dim)/dynamic_update_slice | solution.py:217
  297.5 4.6 fusion.158
  302.1 5.0 multiply_convert_fusion.3
  307.1 2.0 fusion.161
  313.4 8.6 %dynamic_update_slice.29 = f32[4,512,192]{1,0,2:T(4,128)} dynamic-update-slice(f32[4,512,192]{1,0,2:T(4,128)} %get-tuple-element.600, f32[1,512,192]{1,0,2:T(1,128)S(1)} %copy.58, s32[]{:T(128)S(6)} %copy.75, s32[]{:T(128)} %constant.214.clone.1..sunk.1, s32[]{:T(128)} %constant.214.clone.1..sunk.1) | dynamic-update-slice | bytes 786436 | tf_op jit(solution)/shard_map/while/body/jit(dynamic_update_index_in_dim)/dynamic_update_slice | solution.py:217
  333.1 4.6 fusion.158
  337.7 5.0 multiply_convert_fusion.3
  342.8 2.0 fusion.161
  349.0 8.6 %dynamic_update_slice.29 = f32[4,512,192]{1,0,2:T(4,128)} dynamic-update-slice(f32[4,512,192]{1,0,2:T(4,128)} %get-tuple-element.600, f32[1,512,192]{1,0,2:T(1,128)S(1)} %copy.58, s32[]{:T(128)S(6)} %copy.75, s32[]{:T(128)} %constant.214.clone.1..sunk.1, s32[]{:T(128)} %constant.214.clone.1..sunk.1) | dynamic-update-slice | bytes 786436 | tf_op jit(solution)/shard_map/while/body/jit(dynamic_update_index_in_dim)/dynamic_update_slice | solution.py:217
  357.8 3.3 reshape.527
  361.1 2.2 reshape.526
  363.3 4.5 convolution_bitcast_fusion.2
  369.7 2.5 fusion.51
  373.8 1.9 fusion.21
  375.7 7.1 multiply_convert_fusion.1
  382.8 7.0 fusion.78
  389.9 4.5 convolution_bitcast_fusion
  394.5 4.5 convolution_bitcast_fusion.1
  399.0 10.0 %pad_maximum_fusion = f32[2048,2,768]{2,0,1:T(8,128)} fusion(f32[2048,1,768]{2,0,1:T(8,128)} %convolution_bitcast_fusion.1, f32[2048,1,768]{2,0,1:T(8,128)} %convolution_bitcast_fusion), kind=kLoop, calls=%fused_computation.36 | loop fusion | flops 3145728 | bytes 25165824 | tf_op jit(solution)/shard_map/stack | solution.py:237
  410.3 4.7 fusion.82
  415.0 3.7 convolution_add_fusion
  418.7 6.7 fusion.24
  425.5 7.0 fusion.55
  432.8 6.9 fusion.83
  443.5 2.0 copy.42
  445.5 89.0 %reduce-scatter.11.cloned.1.call-done = f32[512,2,768]{2,0,1:T(8,128)} async-done(((f32[2048,2,768]{2,0,1:T(8,128)}), f32[512,2,768]{2,0,1:T(8,128)}) %reduce-scatter.11.cloned.1.call-update) | async-done | bytes 3145744 | tf_op jit(solution)/shard_map/reduce_scatter | solution.py:236
  534.5 2.1 slice_reduce_fusion
  536.7 2.9 fusion.76
  539.6 37.1 %all-reduce = (f32[3,192]{1,0:T(4,128)}, f32[768]{0:T(1024)}, f32[5,768]{1,0:T(8,128)S(1)}) all-reduce(f32[3,192]{1,0:T(4,128)S(1)} %reshape.530, f32[768]{0:T(1024)S(1)} %get-tuple-element.392, f32[5,768]{1,0:T(8,128)S(1)} %stack.41), channel_id=1, replica_groups=mesh['dp'=8,'tensor'=4] {'dp'}, use_global_device_ids=true, to_apply=%region_15.16 | all-reduce | flops 5184 | bytes 41472 | tf_op jit(solution)/shard_map/psum | solution.py:260
  576.7 12.7 %psum.31 = f32[5,768]{1,0:T(8,128)} all-reduce(f32[5,768]{1,0:T(8,128)S(1)} %get-tuple-element.358), channel_id=1, replica_groups=mesh['dp'=8,'tensor'=4] {'tensor'}, use_global_device_ids=true, to_apply=%region_27.28 | all-reduce | flops 3840 | bytes 30720 | tf_op jit(solution)/shard_map/psum | solution.py:263
  589.4 7.0 reduce-scatter.9.cloned.1.call-done
  596.5 3.8 convert_add_fusion.1
  600.3 69.9 %reduce-scatter.13.cloned.1.call-done = f32[96,3,192]{2,0,1:T(8,128)} async-done(((f32[768,3,192]{2,0,1:T(8,128)}), f32[96,3,192]{2,0,1:T(8,128)}) %reduce-scatter.13.cloned.1.call-update) | async-done | bytes 221200 | tf_op jit(solution)/shard_map/reduce_scatter | solution.py:255
  670.1 72.7 %reduce-scatter.15.cloned.1.call-done = f32[96,768]{1,0:T(8,128)} async-done(((f32[768,768]{1,0:T(8,128)}), f32[96,768]{1,0:T(8,128)}) %reduce-scatter.15.cloned.1.call-update) | async-done | bytes 294928 | tf_op jit(solution)/shard_map/reduce_scatter | solution.py:257
  742.9 72.9 %reduce-scatter.17.cloned.1.call-done = f32[768,96]{0,1:T(8,128)} async-done(((f32[768,768]{0,1:T(8,128)}), f32[768,96]{0,1:T(8,128)}) %reduce-scatter.17.cloned.1.call-update) | async-done | bytes 294928 | tf_op jit(solution)/shard_map/reduce_scatter | solution.py:258
  (252 shorter events, 75.8 us)
Async XLA Ops:
  7.2 6.6 copy-start.12
  7.2 90.8 %all-gather.6.cloned.1.call-start = ((), (), s32[]{:S(2)}) async-start(), calls=%async_computation.6 | async-start | bytes 3932160 | tf_op jit(solution)/shard_map/all_gather | solution.py:99
  8.6 1.5 copy-start.19
  10.1 2.8 copy-start.22
  13.0 4.6 copy-start.31
  13.0 4.7 copy-start.21
  13.0 4.8 copy-start.18
  13.0 197.7 %all-gather.14.cloned.1.call-start = ((), (), s32[]{:S(2)}) async-start(), calls=%async_computation.11 | async-start | bytes 3932160 | tf_op jit(solution)/shard_map/all_gather | solution.py:165
  13.8 3.7 copy-start.24
  15.5 360.2 %all-gather.10.cloned.1.call-start = ((), (), s32[]{:S(2)}) async-start(), calls=%async_computation.8 | async-start | bytes 1327104 | tf_op jit(solution)/shard_map/all_gather | solution.py:93
  16.3 359.4 %all-gather.8.cloned.1.call-start = ((), (), s32[]{:S(2)}) async-start(), calls=%async_computation.7 | async-start | bytes 3932160 | tf_op jit(solution)/shard_map/all_gather | solution.py:102
  16.8 366.0 %all-gather.12.cloned.1.call-start = ((), (), s32[]{:S(2)}) async-start(), calls=%async_computation.9 | async-start | bytes 1327104 | tf_op jit(solution)/shard_map/all_gather | solution.py:94
  17.4 426.1 %reduce-scatter.19.cloned.1.call-start = ((), (), s32[]{:S(2)}) async-start(), calls=%async_computation.16 | async-start | bytes 884736
  95.1 9.0 %copy-start.32 = (f32[64]{0:T(128)}, f32[64]{0:T(128)S(1)}, u32[]{:S(2)}) copy-start(f32[64]{0:T(128)S(1)} %pad.16.clone) | copy-start | bytes 772
  98.0 6.0 copy-start.8
  116.8 7.4 copy-start.16
  143.1 7.5 copy-start.16
  168.6 7.4 copy-start.16
  194.0 7.4 copy-start.16
  226.2 4.6 copy-start.17
  237.9 1.4 copy-start
  238.0 1.9 copy-start.3
  240.6 1.1 copy-start.1
  261.9 4.6 copy-start.17
  273.6 1.4 copy-start
  273.6 1.9 copy-start.3
  276.3 1.1 copy-start.1
  297.5 4.6 copy-start.17
  309.2 1.4 copy-start
  309.2 1.9 copy-start.3
  311.9 1.1 copy-start.1
  333.1 4.6 copy-start.17
  344.8 1.4 copy-start
  344.8 1.9 copy-start.3
  347.5 1.1 copy-start.1
  357.8 3.3 copy-start.10
  363.3 4.5 copy-start.2
  367.7 1.9 copy-start.33
  369.6 164.9 %reduce-scatter.11.cloned.1.call-start = ((), (), s32[]{:S(2)}) async-start(), calls=%async_computation.12 | async-start | bytes 15728640 | tf_op jit(solution)/shard_map/reduce_scatter | solution.py:236
  372.1 1.1 copy-start.5
  372.1 1.7 copy-start.7
  373.8 1.9 copy-start.36
  382.8 7.1 copy-start.14
  382.8 7.1 copy-start.15
  389.9 4.6 copy-start.37
  389.9 4.6 copy-start.34
  409.0 1.3 copy-start.35
  409.0 187.4 %reduce-scatter.9.cloned.1.call-start = ((), (), s32[]{:S(2)}) async-start(), calls=%async_computation.10 | async-start | bytes 7864320 | tf_op jit(solution)/shard_map/reduce_scatter | solution.py:156
  410.3 4.7 copy-start.9
  410.3 4.7 copy-start.11
  418.7 251.5 %reduce-scatter.13.cloned.1.call-start = ((), (), s32[]{:S(2)}) async-start(), calls=%async_computation.13 | async-start | bytes 2654208 | tf_op jit(solution)/shard_map/reduce_scatter | solution.py:255
  425.5 317.4 %reduce-scatter.15.cloned.1.call-start = ((), (), s32[]{:S(2)}) async-start(), calls=%async_computation.14 | async-start | bytes 2654208 | tf_op jit(solution)/shard_map/reduce_scatter | solution.py:257
  432.5 383.2 %reduce-scatter.17.cloned.1.call-start = ((), (), s32[]{:S(2)}) async-start(), calls=%async_computation.15 | async-start | bytes 2654208 | tf_op jit(solution)/shard_map/reduce_scatter | solution.py:258
  439.7 0.7 copy-start.26
  439.7 1.9 copy-start.6
  443.4 93.2 %copy-start.4 = (bf16[512,768]{1,0:T(8,128)(2,1)S(1)}, bf16[512,768]{1,0:T(8,128)(2,1)}, u32[]{:S(2)}) copy-start(bf16[512,768]{1,0:T(8,128)(2,1)} %param.19) | copy-start | bytes 2359300
  443.4 93.2 %copy-start.20 = (f32[512]{0:T(512)S(1)}, f32[512]{0:T(512)}, u32[]{:S(2)}) copy-start(f32[512]{0:T(512)} %copy-done.19) | copy-start | bytes 6148
  443.4 93.2 %copy-start.23 = (f32[512]{0:T(512)S(1)}, f32[512]{0:T(512)}, u32[]{:S(2)}) copy-start(f32[512]{0:T(512)} %copy-done.22) | copy-start | bytes 6148
  443.4 93.2 %copy-start.27 = (f32[768]{0:T(1024)S(1)}, f32[768]{0:T(1024)}, u32[]{:S(2)}) copy-start(f32[768]{0:T(1024)} %param.22) | copy-start | bytes 9220
  443.4 93.2 %copy-start.28 = (f32[768]{0:T(1024)S(1)}, f32[768]{0:T(1024)}, u32[]{:S(2)}) copy-start(f32[768]{0:T(1024)} %param.24) | copy-start | bytes 9220
  536.6 59.8 %copy-start.13 = (bf16[512,768]{1,0:T(8,128)(2,1)S(1)}, bf16[512,768]{1,0:T(8,128)(2,1)}, u32[]{:S(2)}) copy-start(bf16[512,768]{1,0:T(8,128)(2,1)} %param.20) | copy-start | bytes 2359300
  536.6 59.8 %copy-start.25 = (f32[512]{0:T(512)S(1)}, f32[512]{0:T(512)}, u32[]{:S(2)}) copy-start(f32[512]{0:T(512)} %copy-done.24) | copy-start | bytes 6148
  536.7 59.8 %copy-start.29 = (f32[768]{0:T(1024)S(1)}, f32[768]{0:T(1024)}, u32[]{:S(2)}) copy-start(f32[768]{0:T(1024)} %param.33) | copy-start | bytes 9220
  536.7 59.8 %copy-start.30 = (f32[768]{0:T(1024)S(1)}, f32[768]{0:T(1024)}, u32[]{:S(2)}) copy-start(f32[768]{0:T(1024)} %param.32) | copy-start | bytes 9220
Sparse Core Ops, SparseCore 0:
  13.1 31.2 all-gather.5
  46.0 28.4 all-gather.13
  76.7 41.6 all-gather.9
  119.8 27.1 all-gather.7
  149.0 41.0 all-gather.11
  369.7 63.3 reduce-scatter.18
  435.7 98.7 reduce-scatter.10
  537.0 59.3 reduce-scatter.8
  600.5 69.5 reduce-scatter.12
  674.1 68.7 reduce-scatter.14
  747.0 68.7 reduce-scatter.16
where the time goes:
time: 833 us; the launch traced here: 823 us
  waiting for transfers between devices  313 us (38%)
  matrix products  174 us (21%)
  blocking collectives  125 us (15%)
  other arithmetic  83.5 us (10%)
  local copies, waits for them, and re-layouts  79.7 us (10%)
  loops' own time  30.7 us (4%)
  between operations  15.5 us (2%)
    reduce_scatter x1, waiting for transfers between devices, per_device(): lax.psum_scatter(jnp.stack([first_part, second_part], axis=1), 'tensor',...  89 us
    reduce_scatter x1, waiting for transfers between devices, per_device(): lax.psum_scatter(grad_down, 'dp', scatter_dimension=1, tiled=True)  72.9 us
    reduce_scatter x1, waiting for transfers between devices, per_device(): lax.psum_scatter(grad_in, 'dp', scatter_dimension=0, tiled=True)  72.7 us
    reduce_scatter x1, waiting for transfers between devices, per_device(): lax.psum_scatter(grad_qkv, 'dp', scatter_dimension=0, tiled=True)  69.9 us
    all_gather x1, blocking collectives, per_device(): lax.all_gather(w_qkv, 'dp', axis=0, tiled=True)  39.8 us
    psum x1, blocking collectives, per_device(): lax.psum((grad_qkv_bias, grad_in_bias, small_terms), 'dp')  37.1 us
    dynamic_update_slice x8, local copies, waits for them, and re-layouts, per_device(): lax.scan(back_block, start_carry, jnp.arange(block_count))  35.9 us
    all_gather x1, blocking collectives, per_device(): lax.all_gather(w_attn_out, 'dp', axis=1, tiled=True)  35.1 us
  transfers between devices with their start and end apart: 11, of which 5 were waited for; matrix products, arithmetic and copies ran while one was open for 39% of the time, Pallas kernels for 0%

commit v1 on v0

v1 whole, which is shorter than its diff:
```python
import functools
import math

import jax
import jax.numpy as jnp
import numpy as np
from jax import lax
from jax.experimental import pallas as pl
from jax.experimental.pallas import tpu as pltpu
from jax.sharding import PartitionSpec as P

HD = 64
ROT = 16
LMAX = 2048
LANES = 128
EPS = 1e-05
BLOCK = 256
FAST = 64
VMEM = 66 * 1024 * 1024

f32 = jnp.float32
low = jnp.bfloat16

NN = (((1,), (0,)), ((), ()))
NT = (((1,), (1,)), ((), ()))
TN = (((0,), (0,)), ((), ()))


def dot(a, b, dims):
    return lax.dot_general(a, b, dims, preferred_element_type=f32)


def round_up(n, m):
    return (n + m - 1) // m * m


def rotary_base():
    d = np.arange(LANES) % HD
    half = ROT // 2
    inverse = np.where(d < ROT, np.exp((d % half) * (-2.0 * math.log(10000.0) / ROT)), 0.0)
    slow = np.arange(0, LMAX, FAST)[:, None] * inverse
    fast = np.arange(FAST)[:, None] * inverse
    return np.concatenate([np.cos(slow), np.sin(slow), np.cos(fast), np.sin(fast)]).astype(
        np.float32
    )


def rotary_rows(table_ref, block):
    slow_rows = LMAX // FAST
    fast_cos = table_ref[2 * slow_rows : 2 * slow_rows + FAST, :]
    fast_sin = table_ref[2 * slow_rows + FAST :, :]
    cosines, sines = [], []
    for part in range(BLOCK // FAST):
        row = block * (BLOCK // FAST) + part
        slow_cos = table_ref[pl.ds(row, 1), :]
        slow_sin = table_ref[pl.ds(row + slow_rows, 1), :]
        cosines.append(slow_cos * fast_cos - slow_sin * fast_sin)
        sines.append(slow_sin * fast_cos + slow_cos * fast_sin)
    cosine, sine = jnp.concatenate(cosines), jnp.concatenate(sines)
    d = lax.broadcasted_iota(jnp.int32, cosine.shape, 1) % HD
    return (
        cosine,
        jnp.where(d < ROT // 2, -sine, 0.0),
        jnp.where((d >= ROT // 2) & (d < ROT), sine, 0.0),
    )


def rotate(values, tables, sign):
    cosine, from_right, from_left = tables
    half = ROT // 2
    turned = []
    for first in range(0, values.shape[1], LANES):
        t = values[:, first : first + LANES]
        side = (
            pltpu.roll(t, LANES - half, axis=1) * from_right
            + pltpu.roll(t, half, axis=1) * from_left
        )
        turned.append(t * cosine + side if sign > 0 else t * cosine - side)
    return jnp.concatenate(turned, axis=1)


def three_terms(value):
    first = value.astype(low).astype(f32)
    second = (value - first).astype(low).astype(f32)
    return first, second, value - first - second


def front_kernel(width, x_ref, norm_ref, wq_ref, bq_ref, table_ref, first_ref, second_ref, qkv_ref):
    padded = qkv_ref.shape[1] // 3
    x = x_ref[...].astype(f32)
    shifted = x - jnp.mean(x, axis=1, keepdims=True)
    inv_std = lax.rsqrt(jnp.mean(shifted * shifted, axis=1, keepdims=True) + EPS)
    normed = shifted * inv_std
    first = (normed * norm_ref[0:1, :] + norm_ref[1:2, :]).astype(low)
    first_ref[...] = first
    second_ref[...] = (normed * norm_ref[2:3, :] + norm_ref[3:4, :]).astype(low)
    projected = dot(first, wq_ref[...], NN) + bq_ref[...]
    tables = rotary_rows(table_ref, pl.program_id(0))
    lane = lax.broadcasted_iota(jnp.int32, (BLOCK, padded), 1)
    extra = (lane >= width) & (lane < width + 3)
    qkv_ref[:, :padded] = rotate(projected[:, :padded], tables, 1).astype(low)
    keys = rotate(projected[:, padded : 2 * padded], tables, 1)
    qkv_ref[:, padded : 2 * padded] = jnp.where(extra, 1.0, keys).astype(low)
    qkv_ref[:, 2 * padded :] = jnp.where(extra, 1.0, projected[:, 2 * padded :]).astype(low)


def front(width, x, norms, wq, bq, table):
    rows, d = x.shape
    full = lambda a: pl.BlockSpec(a.shape, lambda r: (0,) * a.ndim)
    block = lambda w: pl.BlockSpec((BLOCK, w), lambda r: (r, 0))
    return pl.pallas_call(
        functools.partial(front_kernel, width),
        name="front",
        grid=(rows // BLOCK,),
        in_specs=[block(d), full(norms), full(wq), full(bq), full(table)],
        out_specs=[block(d), block(d), block(wq.shape[1])],
        out_shape=[
            jax.ShapeDtypeStruct((rows, d), low),
            jax.ShapeDtypeStruct((rows, d), low),
            jax.ShapeDtypeStruct((rows, wq.shape[1]), low),
        ],
        compiler_params=pltpu.CompilerParams(vmem_limit_bytes=VMEM),
    )(x, norms, wq, bq, table)


def attend_kernel(width, qkv_ref, context_ref, qx_ref, vm_ref, scores_ref):
    heads = width // HD
    rows = qkv_ref.shape[0]
    padded = qkv_ref.shape[1] // 3
    blocks = rows // BLOCK
    scale = HD ** (-0.5)
    step = pl.program_id(0)
    lane = lax.broadcasted_iota(jnp.int32, (BLOCK, padded), 1)
    of_head = [(lane >= h * HD) & (lane < (h + 1) * HD) for h in range(heads)]

    @pl.when(step == 0)
    def _():
        @pl.loop(0, blocks)
        def _(j):
            v = qkv_ref[pl.ds(pl.multiple_of(j * BLOCK, BLOCK), BLOCK), 2 * padded :].astype(f32)
            for h in range(heads):
                vm_ref[j, h * BLOCK : (h + 1) * BLOCK, :] = jnp.where(
                    of_head[h], v, jnp.where(lane == width + h, 1.0, 0.0)
                ).astype(low)

    q = qkv_ref[pl.ds(pl.multiple_of(step * BLOCK, BLOCK), BLOCK), :padded].astype(f32)
    query = jnp.concatenate([jnp.where(of_head[h], q, 0.0).astype(low) for h in range(heads)])

    def keys(j):
        return qkv_ref[pl.ds(pl.multiple_of(j * BLOCK, BLOCK), BLOCK), padded : 2 * padded]

    def widest(s):
        return functools.reduce(
            jnp.maximum, [s[:, c : c + LANES] for c in range(0, BLOCK, LANES)]
        )

    own = dot(query, keys(step), NT)
    row = lax.broadcasted_iota(jnp.int32, own.shape, 0) % BLOCK
    col = lax.broadcasted_iota(jnp.int32, own.shape, 1)
    own = jnp.where(col <= row, own, -1e30)

    def first_pass(j, top):
        s = dot(query, keys(j), NT)
        scores_ref[j] = s
        return jnp.maximum(top, widest(s))

    top = lax.fori_loop(0, step, first_pass, widest(own))
    top = jnp.max(top, axis=1, keepdims=True)

    def weigh(s, j):
        p = jnp.exp((s - top) * scale).astype(low)
        return functools.reduce(
            jnp.add,
            [
                dot(
                    p[h * BLOCK : (h + 1) * BLOCK],
                    vm_ref[j, h * BLOCK : (h + 1) * BLOCK, :],
                    NN,
                )
                for h in range(heads)
            ],
        )

    def second_pass(j, total):
        return total + weigh(scores_ref[j], j)

    mixed = lax.fori_loop(0, step, second_pass, weigh(own, step))
    inverse = jnp.zeros((BLOCK, padded), f32)
    for h in range(heads):
        total = mixed[:, width + h : width + h + 1]
        inverse = jnp.where(of_head[h], 1.0 / total, inverse)
        log_total = top[h * BLOCK : (h + 1) * BLOCK] + jnp.log(total) / scale
        extended = query[h * BLOCK : (h + 1) * BLOCK].astype(f32)
        for k, term in enumerate(three_terms(-log_total)):
            extended = jnp.where(lane == width + k, term, extended)
        qx_ref[0, h * BLOCK : (h + 1) * BLOCK, :] = extended.astype(low)
    context_ref[...] = (mixed * inverse).astype(low)


def attend(width, qkv):
    rows = qkv.shape[0]
    padded = qkv.shape[1] // 3
    heads = width // HD
    blocks = rows // BLOCK
    return pl.pallas_call(
        functools.partial(attend_kernel, width),
        name="attend",
        grid=(blocks,),
        in_specs=[pl.BlockSpec(qkv.shape, lambda r: (0, 0))],
        out_specs=[
            pl.BlockSpec((BLOCK, padded), lambda r: (r, 0)),
            pl.BlockSpec((1, heads * BLOCK, padded), lambda r: (r, 0, 0)),
        ],
        out_shape=[
            jax.ShapeDtypeStruct((rows, padded), low),
            jax.ShapeDtypeStruct((blocks, heads * BLOCK, padded), low),
        ],
        scratch_shapes=[
            pltpu.VMEM((blocks, heads * BLOCK, padded), low),
            pltpu.VMEM((blocks, heads * BLOCK, BLOCK), f32),
        ],
        compiler_params=pltpu.CompilerParams(vmem_limit_bytes=VMEM),
    )(qkv)


def feed_kernel(
    width, length_ref, second_ref, context_ref, cot_ref, wi_ref, wd_ref, bias_ref, norm_ref,
    branch_ref, dox_ref, back_ref, gwi_ref, gwd_ref, gbias_ref, gsmall_ref, gwi_sum, gwd_sum,
):
    heads = width // HD
    padded = context_ref.shape[1]
    hidden = wi_ref.shape[1]
    step = pl.program_id(0)

    @pl.when(step == 0)
    def _():
        gwi_sum[...] = jnp.zeros_like(gwi_sum)
        gwd_sum[...] = jnp.zeros_like(gwd_sum)
        gbias_ref[...] = jnp.zeros_like(gbias_ref)
        gsmall_ref[...] = jnp.zeros_like(gsmall_ref)

    second = second_ref[...]
    context = context_ref[...]
    row = lax.broadcasted_iota(jnp.int32, cot_ref.shape, 0) + step * BLOCK
    grad = jnp.where(row < length_ref[0], cot_ref[...].astype(f32), 0.0).astype(low)

    u = dot(second, wi_ref[...], NN) + bias_ref[...]
    cdf = 0.5 * (1.0 + lax.erf(u * (1.0 / math.sqrt(2.0))))
    act = (u * cdf).astype(low)
    slope = cdf + u * (jnp.exp(-0.5 * u * u) * (1.0 / math.sqrt(2.0 * math.pi)))
    both = jnp.concatenate([act, context], axis=1)
    branch_ref[...] = dot(both, wd_ref[...], NT).astype(low)

    back = dot(grad, wd_ref[...], NN)
    grad_hidden = back[:, :hidden] * slope
    gbias_ref[...] += jnp.sum(grad_hidden, axis=0, keepdims=True)
    hidden_low = grad_hidden.astype(low)
    gwi_sum[...] += dot(second, hidden_low, TN)
    gwd_sum[...] += dot(grad, both, TN)

    grad_context = back[:, hidden:].astype(low).astype(f32)
    lane = lax.broadcasted_iota(jnp.int32, grad_context.shape, 1)
    product = grad_context * context.astype(f32)
    for h in range(heads):
        inside = (lane >= h * HD) & (lane < (h + 1) * HD)
        extended = jnp.where(inside, grad_context, 0.0)
        delta = jnp.sum(jnp.where(inside, product, 0.0), axis=1, keepdims=True)
        for k, term in enumerate(three_terms(-delta)):
            extended = jnp.where(lane == width + k, term, extended)
        dox_ref[0, h * BLOCK : (h + 1) * BLOCK, :] = extended.astype(low)

    part = dot(hidden_low, wi_ref[...], NT)
    gsmall_ref[0:1, :] += jnp.sum(part * second.astype(f32), axis=0, keepdims=True)
    gsmall_ref[1:2, :] += jnp.sum(part, axis=0, keepdims=True)
    back_ref[...] = (part * norm_ref[2:3, :]).astype(low)

    @pl.when(step == pl.num_programs(0) - 1)
    def _():
        gwi_ref[...] = gwi_sum[...].astype(low)
        gwd_ref[...] = gwd_sum[...].astype(low)


def feed(width, length, second, context, cot, wi, wd, bias, norms):
    rows, d = second.shape
    padded = context.shape[1]
    heads = width // HD
    blocks = rows // BLOCK
    full = lambda a: pl.BlockSpec(a.shape, lambda r: (0,) * a.ndim)
    block = lambda w: pl.BlockSpec((BLOCK, w), lambda r: (r, 0))
    outs = [
        jax.ShapeDtypeStruct((rows, d), low),
        jax.ShapeDtypeStruct((blocks, heads * BLOCK, padded), low),
        jax.ShapeDtypeStruct((rows, d), low),
        jax.ShapeDtypeStruct(wi.shape, low),
        jax.ShapeDtypeStruct(wd.shape, low),
        jax.ShapeDtypeStruct(bias.shape, f32),
        jax.ShapeDtypeStruct((8, d), f32),
    ]
    return pl.pallas_call(
        functools.partial(feed_kernel, width),
        name="feed",
        grid=(blocks,),
        in_specs=[
            pl.BlockSpec(memory_space=pltpu.SMEM),
            block(d), block(padded), block(d), full(wi), full(wd), full(bias), full(norms),
        ],
        out_specs=[
            block(d),
            pl.BlockSpec((1, heads * BLOCK, padded), lambda r: (r, 0, 0)),
            block(d), full(outs[3]), full(outs[4]), full(outs[5]), full(outs[6]),
        ],
        out_shape=outs,
        scratch_shapes=[pltpu.VMEM(wi.shape, f32), pltpu.VMEM(wd.shape, f32)],
        compiler_params=pltpu.CompilerParams(vmem_limit_bytes=VMEM),
    )(length, second, context, cot, wi, wd, bias, norms)


def back_kernel(
    width, qkv_ref, qx_ref, dox_ref, first_ref, part_ref, wq_ref, norm_ref, table_ref,
    gn_ref, gwq_ref, gbias_ref, gsmall_ref, keyt_ref, dqt_ref, gwq_sum,
):
    heads = width // HD
    rows = qkv_ref.shape[0]
    padded = qkv_ref.shape[1] // 3
    blocks = rows // BLOCK
    scale = HD ** (-0.5)
    step = pl.program_id(0)

    @pl.when(step == 0)
    def _():
        dqt_ref[...] = jnp.zeros_like(dqt_ref)
        gwq_sum[...] = jnp.zeros_like(gwq_sum)
        gbias_ref[...] = jnp.zeros_like(gbias_ref)
        gsmall_ref[...] = jnp.zeros_like(gsmall_ref)

    here = pl.ds(pl.multiple_of(step * BLOCK, BLOCK), BLOCK)
    keys = qkv_ref[here, padded : 2 * padded]
    values = qkv_ref[here, 2 * padded :]
    keyt_ref[...] = keys.astype(f32).T[:width].astype(low)

    def pair(i, own):
        query, dout = qx_ref[i], dox_ref[i]
        p = jnp.exp(dot(keys, query, NT) * scale)
        if own:
            key_at = lax.broadcasted_iota(jnp.int32, p.shape, 0)
            query_at = lax.broadcasted_iota(jnp.int32, p.shape, 1) % BLOCK
            p = jnp.where(key_at <= query_at, p, 0.0)
        ds = (p * dot(values, dout, NT)).astype(low)
        grad_value = dot(p.astype(low), dout, NN)
        grad_key = dot(ds, query, NN)
        for h in range(heads):
            dqt_ref[i, h * HD : (h + 1) * HD, :] += dot(
                keyt_ref[h * HD : (h + 1) * HD, :], ds[:, h * BLOCK : (h + 1) * BLOCK], NN
            )
        return grad_key, grad_value

    def later(i, carry):
        grad_key, grad_value = pair(i, False)
        return carry[0] + grad_key, carry[1] + grad_value

    grad_key, grad_value = lax.fori_loop(step + 1, blocks, later, pair(step, True))

    tables = rotary_rows(table_ref, step)
    inside = lax.broadcasted_iota(jnp.int32, (BLOCK, padded), 1) < width
    grad_query = jnp.concatenate(
        [dqt_ref[step].T, jnp.zeros((BLOCK, padded - width), f32)], axis=1
    )
    projected = jnp.concatenate(
        [
            rotate(grad_query * scale, tables, -1),
            rotate(jnp.where(inside, grad_key * scale, 0.0), tables, -1),
            jnp.where(inside, grad_value, 0.0),
        ],
        axis=1,
    )
    gbias_ref[...] += jnp.sum(projected, axis=0, keepdims=True)
    proj_low = projected.astype(low)
    first = first_ref[...]
    gwq_sum[...] += dot(first, proj_low, TN)
    part = dot(proj_low, wq_ref[...], NT)
    gsmall_ref[0:1, :] += jnp.sum(part * first.astype(f32), axis=0, keepdims=True)
    gsmall_ref[1:2, :] += jnp.sum(part, axis=0, keepdims=True)
    gn_ref[...] = (part * norm_ref[0:1, :] + part_ref[...].astype(f32)).astype(low)

    @pl.when(step == blocks - 1)
    def _():
        gwq_ref[...] = gwq_sum[...].astype(low)


def back(width, qkv, qx, dox, first, part, wq, norms, table):
    rows, d = first.shape
    padded = qkv.shape[1] // 3
    blocks = rows // BLOCK
    full = lambda a: pl.BlockSpec(a.shape, lambda r: (0,) * a.ndim)
    block = lambda w: pl.BlockSpec((BLOCK, w), lambda r: (r, 0))
    outs = [
        jax.ShapeDtypeStruct((rows, d), low),
        jax.ShapeDtypeStruct(wq.shape, low),
        jax.ShapeDtypeStruct((1, wq.shape[1]), f32),
        jax.ShapeDtypeStruct((8, d), f32),
    ]
    return pl.pallas_call(
        functools.partial(back_kernel, width),
        name="back",
        grid=(blocks,),
        in_specs=[
            full(qkv), full(qx), full(dox), block(d), block(d), full(wq), full(norms), full(table),
        ],
        out_specs=[block(d)] + [full(o) for o in outs[1:]],
        out_shape=outs,
        scratch_shapes=[
            pltpu.VMEM((width, BLOCK), low),
            pltpu.VMEM((blocks, width, BLOCK), f32),
            pltpu.VMEM(wq.shape, f32),
        ],
        compiler_params=pltpu.CompilerParams(vmem_limit_bytes=VMEM),
    )(qkv, qx, dox, first, part, wq, norms, table)


def layer_norm(values):
    shifted = values - jnp.mean(values, axis=-1, keepdims=True)
    inv_std = lax.rsqrt(jnp.mean(shifted * shifted, axis=-1, keepdims=True) + EPS)
    return shifted * inv_std, inv_std


def per_device(
    tokens, cotangent, seq_lengths, norm1_gain, norm1_bias, norm2_gain, norm2_bias,
    w_qkv, b_qkv, w_attn_out, w_in, b_in, w_down, b_out, b_down,
):
    local_rows, d = tokens.shape
    width = w_qkv.shape[2]
    padded = round_up(width + 3, LANES)
    extra = padded - width
    assert local_rows * lax.axis_size("tensor") == LMAX and seq_lengths.shape[0] == 1
    hidden = w_in.shape[1]

    gather = lambda a, axis: lax.all_gather(a, axis, axis=0, tiled=True)
    wq = jnp.pad(w_qkv, ((0, 0), (0, 0), (0, extra))).reshape(-1, 3 * padded)
    bq = jnp.pad(b_qkv, ((0, 0), (0, extra))).reshape(1, 3 * padded)
    wd = jnp.concatenate([w_down.T, jnp.pad(w_attn_out.T, ((0, 0), (0, extra)))], axis=1)
    norms = jnp.stack([norm1_gain, norm1_bias, norm2_gain, norm2_bias])
    table = jnp.asarray(rotary_base())

    x_full = gather(tokens, "tensor")
    wq_full = gather(wq, "dp")
    cot_full = gather(cotangent, "tensor")
    wi_full, wd_full = gather(w_in, "dp"), gather(wd, "dp")

    first, second, qkv = front(width, x_full, norms, wq_full, bq, table)
    context, qx = attend(width, qkv)
    branch, dox, part, gwi, gwd, gb_in, small2 = feed(
        width, seq_lengths, second, context, cot_full, wi_full, wd_full, b_in.reshape(1, -1), norms
    )
    scatter = lambda a, axis: lax.psum_scatter(a, axis, scatter_dimension=0, tiled=True).astype(f32)
    branches = scatter(branch, "tensor")
    gn, gwq, gb_qkv, small1 = back(width, qkv, qx, dox, first, part, wq_full, norms, table)
    grad_normed = scatter(gn, "tensor")
    gwi, gwd, gwq = scatter(gwi, "dp"), scatter(gwd, "dp"), scatter(gwq, "dp")

    row = lax.axis_index("tensor") * local_rows + jnp.arange(local_rows)
    row_mask = (row < seq_lengths[0]).astype(f32)[:, None]
    x = tokens.astype(f32)
    cot = cotangent.astype(f32)
    output = x + row_mask * (branches + b_out + b_down)
    normed, inv_std = layer_norm(x)
    grad_x = cot + inv_std * (
        grad_normed
        - jnp.mean(grad_normed, axis=-1, keepdims=True)
        - normed * jnp.mean(grad_normed * normed, axis=-1, keepdims=True)
    )
    gb_qkv = gb_qkv.reshape(3, padded)[:, :width]
    small = jnp.concatenate(
        [small1[:2], small2[:2], jnp.sum(row_mask * cot, axis=0, keepdims=True)]
    )
    gb_qkv, gb_in, small = lax.psum((gb_qkv, gb_in, small), "dp")
    small = lax.psum(small, "tensor")
    small = jnp.stack(
        [
            (small[0] - norm1_bias * small[1]) / norm1_gain,
            small[1],
            (small[2] - norm2_bias * small[3]) / norm2_gain,
            small[3],
            small[4],
        ]
    )
    return (
        output,
        grad_x,
        gwq.reshape(-1, 3, padded)[:, :, :width],
        gb_qkv,
        gwd[:, hidden : hidden + width].T,
        gwi,
        gb_in.reshape(-1),
        gwd[:, :hidden].T,
        small,
    )


def solution(mesh):
    rows = P(("dp", "tensor"), None)
    placed = (
        rows, rows, P("dp"), P(), P(), P(), P(), P("dp", None, "tensor"), P(None, "tensor"),
        P("tensor", "dp"), P("dp", "tensor"), P("tensor"), P("tensor", "dp"), P(), P(),
    )
    return jax.shard_map(
        per_device,
        mesh=mesh,
        in_specs=placed,
        out_specs=(
            rows, rows, P("dp", None, "tensor"), P(None, "tensor"), P("tensor", "dp"),
            P("dp", "tensor"), P("tensor"), P("tensor", "dp"), P(),
        ),
        check_vma=False,
    )
```

time: 833 us -> 610 us (0.73); the launches traced: 823 us -> 609 us
  matrix products: 174 us -> 0 us
  Pallas kernels: 0 us -> 108 us
  waiting for transfers between devices: 313 us -> 419 us
  blocking collectives: 125 us -> 47.5 us
  other arithmetic: 83.5 us -> 10.8 us
  local copies, waits for them, and re-layouts: 79.7 us -> 8.74 us
  loops' own time: 30.7 us -> 0 us
    dot_general x39 -> x0, matrix products: 170 us -> none  [the longest x8 31.2 us: block_scores(): jnp.einsum('qhd,khd->hqk', block_query, block_key, preferred_element_type...]
    all_gather x5, waiting for transfers between devices: 0.01 us -> 147 us  [per_device(): gather = lambda a, axis: lax.all_gather(a, axis, axis=0, tiled=True)]
    pallas_call x0 -> x4, Pallas kernels: none -> 108 us  [the longest x1 42.2 us: back(): pl.pallas_call(functools.partial(back_kernel, width), name='back', grid=(...]
    all_gather x2 -> x0, blocking collectives: 75 us -> none  [the longest x1 39.8 us: per_device(): lax.all_gather(w_qkv, 'dp', axis=0, tiled=True)]
    reduce_scatter x5, waiting for transfers between devices: 311 us -> 268 us  [per_device(): lax.psum_scatter(a, axis, scatter_dimension=0, tiled=True).astype(f32)]
    dynamic_update_slice x12 -> x0, local copies, waits for them, and re-layouts: 38.7 us -> none  [the longest x8 35.9 us: per_device(): lax.scan(back_block, start_carry, jnp.arange(block_count))]
    reduce_sum x13 -> x3, other arithmetic: 36 us -> 4.22 us  [the longest x1 3.69 us: per_device(): jnp.sum(row_mask * cot, axis=0, keepdims=True)]
    another operation x2 -> x0, loops' own time: 30.7 us -> none  [the longest x1 19.2 us: per_device(): lax.scan(back_block, start_carry, jnp.arange(block_count))]
  transfers between devices with their start and end apart: 11 -> 10, of which waited for: 5 -> 10; matrix products, arithmetic and copies ran while one was open for 39% -> 2% of each run, Pallas kernels for 0% -> 6%
where the time goes in v1:
time: 610 us; the launch traced here: 609 us
  waiting for transfers between devices  419 us (69%)
  Pallas kernels  108 us (18%)
  blocking collectives  47.5 us (8%)
  between operations  15.2 us (2%)
  other arithmetic  10.8 us (2%)
  local copies, waits for them, and re-layouts  8.74 us (1%)
    reduce_scatter x5, waiting for transfers between devices, per_device(): lax.psum_scatter(a, axis, scatter_dimension=0, tiled=True).astype(f32)  268 us
    all_gather x5, waiting for transfers between devices, per_device(): gather = lambda a, axis: lax.all_gather(a, axis, axis=0, tiled=True)  147 us
    pallas_call x1, Pallas kernels, back(): pl.pallas_call(functools.partial(back_kernel, width), name='back', grid=(...  42.2 us
    psum x1, blocking collectives, per_device(): gb_qkv, gb_in, small = lax.psum((gb_qkv, gb_in, small), 'dp')  37.1 us
    pallas_call x1, Pallas kernels, attend(): pl.pallas_call(functools.partial(attend_kernel, width), name='attend', gr...  29.1 us
    pallas_call x1, Pallas kernels, feed(): pl.pallas_call(functools.partial(feed_kernel, width), name='feed', grid=(...  26.3 us
  transfers between devices with their start and end apart: 10, of which 10 were waited for; matrix products, arithmetic and copies ran while one was open for 2% of the time, Pallas kernels for 6%

profile of v1, /device:TPU:0, one launch (start us, length us, event | category | flops | bytes accessed | tf_op | source)
XLA Modules:
  0.0 609.2 jit_solution(17280283200593634092)
XLA Ops:
  7.2 0.0 all-gather.8.cloned.1.call-start
  7.2 1.1 copy.33
  8.3 0.0 copy-start.5
  8.3 0.0 copy-start.11
  8.4 0.0 copy-start.16
  8.4 0.1 pad.12.clone
  8.5 0.7 copy.34
  9.2 0.0 all-gather.8.cloned.1.call-update
  9.2 0.0 all-gather.6.cloned.1.call-start
  9.2 0.7 all-gather.6.cloned.1.call-update
  9.9 0.0 all-gather.12.cloned.1.call-start
  10.0 0.7 all-gather.12.cloned.1.call-update
  10.7 0.0 all-gather.14.cloned.1.call-start
  10.7 0.1 copy.30
  10.9 0.7 fusion.9
  11.6 0.0 all-gather.14.cloned.1.call-update
  11.6 0.0 all-gather.10.cloned.1.call-start
  11.6 0.5 all-gather.10.cloned.1.call-update
  12.2 0.0 reduce-scatter.10.cloned.1.call-start
  12.3 0.6 copy.35
  13.6 0.6 reshape.67.bias_ref
  14.2 0.6 pad_maximum_fusion.2.norm_ref
  14.8 39.9 %all-gather.8.cloned.1.call-done.wq_ref = bf16[768,768]{1,0:T(8,128)(2,1)} async-done(((bf16[96,768]{1,0:T(8,128)(2,1)}), bf16[768,768]{1,0:T(8,128)(2,1)}) %all-gather.8.cloned.1.call-update) | async-done | bytes 1179664 | tf_op jit(solution)/shard_map/all_gather | solution.py:437
  54.6 28.8 %all-gather.6.cloned.1.call-done.x_ref = bf16[2048,768]{1,0:T(8,128)(2,1)} async-done(((bf16[512,768]{1,0:T(8,128)(2,1)}), bf16[2048,768]{1,0:T(8,128)(2,1)}) %all-gather.6.cloned.1.call-update) | async-done | bytes 3145744 | tf_op jit(solution)/shard_map/all_gather | solution.py:437
  83.4 10.1 %front.1 = (bf16[2048,768]{1,0:T(8,128)(2,1)}, bf16[2048,768]{1,0:T(8,128)(2,1)}, bf16[2048,768]{1,0:T(8,128)(2,1)}) custom-call(bf16[2048,768]{1,0:T(8,128)(2,1)} %all-gather.6.cloned.1.call-done.x_ref, f32[4,768]{1,0:T(4,128)} %pad_maximum_fusion.2.norm_ref, bf16[768,768]{1,0:T(8,128)(2,1)} %all-gather.8.cloned.1.call-done.wq_ref, f32[1,768]{1,0:T(1,128)} %bitcast.20, ...), custom_call_target="tpu_custom_call" | custom-call | tf_op jit(solution)/shard_map/front/pallas_call | solution.py:111
  93.5 29.1 %attend.1 = (bf16[2048,256]{1,0:T(8,128)(2,1)}, bf16[8,768,256]{2,1,0:T(8,128)(2,1)}) custom-call(bf16[2048,768]{1,0:T(8,128)(2,1)} %get-tuple-element.26.qkv_ref), custom_call_target="tpu_custom_call" | custom-call | tf_op jit(solution)/shard_map/attend/pallas_call | solution.py:205
  122.5 4.2 all-gather.12.cloned.1.call-done.wi_ref
  126.8 45.5 %all-gather.14.cloned.1.call-done.wd_ref = bf16[768,1024]{1,0:T(8,128)(2,1)} async-done(((bf16[96,1024]{1,0:T(8,128)(2,1)}), bf16[768,1024]{1,0:T(8,128)(2,1)}) %all-gather.14.cloned.1.call-update) | async-done | bytes 1572880 | tf_op jit(solution)/shard_map/all_gather | solution.py:437
  172.3 28.3 %all-gather.10.cloned.1.call-done.cot_ref = bf16[2048,768]{1,0:T(8,128)(2,1)} async-done(((bf16[512,768]{1,0:T(8,128)(2,1)}), bf16[2048,768]{1,0:T(8,128)(2,1)}) %all-gather.10.cloned.1.call-update) | async-done | bytes 3145744 | tf_op jit(solution)/shard_map/all_gather | solution.py:437
  200.6 26.3 %feed.1 = (bf16[2048,768]{1,0:T(8,128)(2,1)}, bf16[8,768,256]{2,1,0:T(8,128)(2,1)}, bf16[2048,768]{1,0:T(8,128)(2,1)}, bf16[768,768]{1,0:T(8,128)(2,1)}, bf16[76...) custom-call(s32[1]{0:T(128)} %copy.36.length_ref, bf16[2048,768]{1,0:T(8,128)(2,1)} %get-tuple-element.25.second_ref, ...), custom_call_target="tpu_custom_call" | custom-call | tf_op jit(solution)/shard_map/feed/pallas_call | solution.py:299
  226.9 42.2 %back.1 = (bf16[2048,768]{1,0:T(8,128)(2,1)}, bf16[768,768]{1,0:T(8,128)(2,1)}, f32[1,768]{1,0:T(1,128)}, f32[8,768]{1,0:T(8,128)}) custom-call(bf16[2048,768]{1,0:T(8,128)(2,1)} %get-tuple-element.26.qkv_ref, bf16[8,768,256]{2,1,0:T(8,128)(2,1)} %get-tuple-element.29.qx_ref, bf16[8,768,256]{2,1,0:T(8,128)(2,1)} %get-tuple-element.30.dox_ref, ...), custom_call_target="tpu_custom_call" | custom-call | tf_op jit(solution)/shard_map/back/pallas_call | solution.py:402
  269.1 0.0 reduce-scatter.10.cloned.1.call-update
  269.1 0.0 reduce-scatter.14.cloned.1.call-start
  269.2 0.7 reduce-scatter.14.cloned.1.call-update
  269.9 0.0 reduce-scatter.12.cloned.1.call-start
  269.9 0.7 reduce-scatter.12.cloned.1.call-update
  270.6 0.0 reduce-scatter.8.cloned.1.call-start
  270.7 0.7 reduce-scatter.8.cloned.1.call-update
  271.4 0.2 reduce-scatter.6.cloned.1.call-start
  271.6 0.0 copy-start
  271.6 0.3 reduce-scatter.6.cloned.1.call-update
  272.0 0.0 copy-start.18
  272.0 0.7 copy-done
  272.7 0.2 convert_reduce_fusion.1
  272.9 0.4 fusion.5
  273.3 0.7 slice.44
  274.0 0.7 slice.45
  274.8 59.4 %reduce-scatter.10.cloned.1.call-done = bf16[96,768]{1,0:T(8,128)(2,1)} async-done(((bf16[768,768]{1,0:T(8,128)(2,1)}), bf16[96,768]{1,0:T(8,128)(2,1)}) %reduce-scatter.10.cloned.1.call-update) | async-done | bytes 147472 | tf_op jit(solution)/shard_map/reduce_scatter | solution.py:454
  334.2 1.0 reshape.68
  335.2 0.1 slice_convert_fusion
  335.3 0.8 copy.31
  336.0 66.0 %reduce-scatter.14.cloned.1.call-done = bf16[96,768]{1,0:T(8,128)(2,1)} async-done(((bf16[768,768]{1,0:T(8,128)(2,1)}), bf16[96,768]{1,0:T(8,128)(2,1)}) %reduce-scatter.14.cloned.1.call-update) | async-done | bytes 147472 | tf_op jit(solution)/shard_map/reduce_scatter | solution.py:454
  402.1 1.6 convert_element_type.38
  403.7 67.0 %reduce-scatter.12.cloned.1.call-done = bf16[96,1024]{1,0:T(8,128)(2,1)} async-done(((bf16[768,1024]{1,0:T(8,128)(2,1)}), bf16[96,1024]{1,0:T(8,128)(2,1)}) %reduce-scatter.12.cloned.1.call-update) | async-done | bytes 196624 | tf_op jit(solution)/shard_map/reduce_scatter | solution.py:454
  470.7 1.0 convert_element_type.37
  471.7 0.7 copy.32
  472.4 0.7 slice_bitcast_fusion
  473.2 36.8 %reduce-scatter.8.cloned.1.call-done = bf16[512,768]{1,0:T(8,128)(2,1)} async-done(((bf16[2048,768]{1,0:T(8,128)(2,1)}), bf16[512,768]{1,0:T(8,128)(2,1)}) %reduce-scatter.8.cloned.1.call-update) | async-done | bytes 786448 | tf_op jit(solution)/shard_map/reduce_scatter | solution.py:454
  510.0 1.9 convert_reduce_fusion
  511.9 38.3 %reduce-scatter.6.cloned.1.call-done = bf16[512,768]{1,0:T(8,128)(2,1)} async-done(((bf16[2048,768]{1,0:T(8,128)(2,1)}), bf16[512,768]{1,0:T(8,128)(2,1)}) %reduce-scatter.6.cloned.1.call-update) | async-done | bytes 786448 | tf_op jit(solution)/shard_map/reduce_scatter | solution.py:454
  550.3 3.7 fusion.6
  554.1 37.1 %all-reduce.3 = (f32[3,192]{1,0:T(4,128)}, f32[768]{0:T(1024)}, f32[5,768]{1,0:T(8,128)S(1)}) all-reduce(f32[3,192]{1,0:T(4,128)S(1)} %bitcast.19, f32[768]{0:T(1024)S(1)} %reduce.1, f32[5,768]{1,0:T(8,128)S(1)} %pad_maximum_fusion), channel_id=1, replica_groups=mesh['dp'=8,'tensor'=4] {'dp'}, use_global_device_ids=true, to_apply=%region_7.8 | all-reduce | flops 5184 | bytes 41472 | tf_op jit(solution)/shard_map/psum | solution.py:475
  591.2 10.4 %psum.31 = f32[5,768]{1,0:T(8,128)S(1)} all-reduce(f32[5,768]{1,0:T(8,128)S(1)} %get-tuple-element.67), channel_id=1, replica_groups=mesh['dp'=8,'tensor'=4] {'tensor'}, use_global_device_ids=true, to_apply=%region_13.14 | all-reduce | flops 3840 | bytes 30720 | tf_op jit(solution)/shard_map/psum | solution.py:476
  601.7 0.6 pad_maximum_fusion.1
  (53 shorter events, 0.3 us)
Async XLA Ops:
  7.2 3.6 copy-start.4
  7.2 3.7 copy-start.3
  7.2 47.4 %all-gather.8.cloned.1.call-start = ((), (), s32[]{:S(2)}) async-start(), calls=%async_computation.6 | async-start | bytes 1327104 | tf_op jit(solution)/shard_map/all_gather | solution.py:437
  8.3 3.9 copy-start.7
  8.3 3.9 copy-start.5
  8.3 3.9 copy-start.11
  8.4 3.9 copy-start.9
  8.4 3.9 copy-start.16
  8.5 5.1 copy-start.15
  9.2 74.2 %all-gather.6.cloned.1.call-start = ((), (), s32[]{:S(2)}) async-start(), calls=%async_computation.5 | async-start | bytes 3932160 | tf_op jit(solution)/shard_map/all_gather | solution.py:437
  9.9 116.8 %all-gather.12.cloned.1.call-start = ((), (), s32[]{:S(2)}) async-start(), calls=%async_computation.8 | async-start | bytes 1327104 | tf_op jit(solution)/shard_map/all_gather | solution.py:437
  10.7 161.6 %all-gather.14.cloned.1.call-start = ((), (), s32[]{:S(2)}) async-start(), calls=%async_computation.9 | async-start | bytes 1769472 | tf_op jit(solution)/shard_map/all_gather | solution.py:437
  11.6 189.0 %all-gather.10.cloned.1.call-start = ((), (), s32[]{:S(2)}) async-start(), calls=%async_computation.7 | async-start | bytes 3932160 | tf_op jit(solution)/shard_map/all_gather | solution.py:437
  12.2 322.0 %reduce-scatter.10.cloned.1.call-start = ((), (), s32[]{:S(2)}) async-start(), calls=%async_computation.12 | async-start | bytes 1327104 | tf_op jit(solution)/shard_map/reduce_scatter | solution.py:454
  269.1 132.9 %reduce-scatter.14.cloned.1.call-start = ((), (), s32[]{:S(2)}) async-start(), calls=%async_computation.14 | async-start | bytes 1327104 | tf_op jit(solution)/shard_map/reduce_scatter | solution.py:454
  269.9 200.8 %reduce-scatter.12.cloned.1.call-start = ((), (), s32[]{:S(2)}) async-start(), calls=%async_computation.13 | async-start | bytes 1769472 | tf_op jit(solution)/shard_map/reduce_scatter | solution.py:454
  270.6 239.3 %reduce-scatter.8.cloned.1.call-start = ((), (), s32[]{:S(2)}) async-start(), calls=%async_computation.11 | async-start | bytes 3932160 | tf_op jit(solution)/shard_map/reduce_scatter | solution.py:454
  271.4 278.9 %reduce-scatter.6.cloned.1.call-start = ((), (), s32[]{:S(2)}) async-start(), calls=%async_computation.10 | async-start | bytes 3932160 | tf_op jit(solution)/shard_map/reduce_scatter | solution.py:454
  271.6 1.1 copy-start
  272.0 2.8 copy-start.18
  272.0 2.8 copy-start.17
  403.7 146.6 %copy-start.1 = (bf16[512,768]{1,0:T(8,128)(2,1)S(1)}, bf16[512,768]{1,0:T(8,128)(2,1)}, u32[]{:S(2)}) copy-start(bf16[512,768]{1,0:T(8,128)(2,1)} %param.17) | copy-start | bytes 2359300
  403.7 146.6 %copy-start.13 = (f32[768]{0:T(1024)S(1)}, f32[768]{0:T(1024)}, u32[]{:S(2)}) copy-start(f32[768]{0:T(1024)} %param.30) | copy-start | bytes 9220
  403.7 146.6 %copy-start.14 = (f32[768]{0:T(1024)S(1)}, f32[768]{0:T(1024)}, u32[]{:S(2)}) copy-start(f32[768]{0:T(1024)} %param.29) | copy-start | bytes 9220
  510.0 40.3 %copy-start.2 = (bf16[512,768]{1,0:T(8,128)(2,1)S(1)}, bf16[512,768]{1,0:T(8,128)(2,1)}, u32[]{:S(2)}) copy-start(bf16[512,768]{1,0:T(8,128)(2,1)} %reduce-scatter.8.cloned.1.call-done) | copy-start | bytes 2359300
  550.3 51.3 %copy-start.6 = (f32[768]{0:T(1024)S(1)}, f32[768]{0:T(1024)}, u32[]{:S(2)}) copy-start(f32[768]{0:T(1024)} %param.20) | copy-start | bytes 9220
  550.3 51.3 %copy-start.8 = (f32[768]{0:T(1024)S(1)}, f32[768]{0:T(1024)}, u32[]{:S(2)}) copy-start(f32[768]{0:T(1024)} %param.19) | copy-start | bytes 9220
  550.3 51.3 %copy-start.10 = (f32[768]{0:T(1024)S(1)}, f32[768]{0:T(1024)}, u32[]{:S(2)}) copy-start(f32[768]{0:T(1024)} %param.22) | copy-start | bytes 9220
  550.3 51.3 %copy-start.12 = (f32[768]{0:T(1024)S(1)}, f32[768]{0:T(1024)}, u32[]{:S(2)}) copy-start(f32[768]{0:T(1024)} %param.21) | copy-start | bytes 9220
Sparse Core Ops, SparseCore 0:
  10.8 43.8 all-gather.7
  56.2 27.1 all-gather.5
  85.6 41.1 all-gather.11
  129.4 42.8 all-gather.13
  173.7 26.8 all-gather.9
  269.3 64.9 reduce-scatter.9
  338.2 63.8 reduce-scatter.13
  406.1 64.5 reduce-scatter.11
  473.2 36.6 reduce-scatter.7
  512.4 37.8 reduce-scatter.5

commit v2 on v1

--- a/solution.py
+++ b/solution.py
@@ -225,7 +225,7 @@
 
 def feed_kernel(
     width, length_ref, second_ref, context_ref, cot_ref, wi_ref, wd_ref, bias_ref, norm_ref,
-    branch_ref, dox_ref, back_ref, gwi_ref, gwd_ref, gbias_ref, gsmall_ref, gwi_sum, gwd_sum,
+    branch_ref, dox_ref, back_ref, gw_ref, gbias_ref, gsmall_ref, gwi_sum, gwd_sum,
 ):
     heads = width // HD
     padded = context_ref.shape[1]
@@ -276,8 +276,11 @@
 
     @pl.when(step == pl.num_programs(0) - 1)
     def _():
-        gwi_ref[...] = gwi_sum[...].astype(low)
-        gwd_ref[...] = gwd_sum[...].astype(low)
+        side = gw_ref.shape[1]
+        for block in range(gw_ref.shape[0]):
+            rows_of = slice(block * side, (block + 1) * side)
+            gw_ref[block, :, :hidden] = gwi_sum[rows_of, :].astype(low)
+            gw_ref[block, :, hidden:] = gwd_sum[rows_of, :].astype(low)
 
 
 def feed(width, length, second, context, cot, wi, wd, bias, norms):
@@ -285,14 +288,14 @@
     padded = context.shape[1]
     heads = width // HD
     blocks = rows // BLOCK
-    full = lambda a: pl.BlockSpec(a.shape, lambda r: (0,) * a.ndim)
+    n = lax.axis_size("dp")
+    full = lambda a: pl.BlockSpec(a.shape, lambda r: (0,) * len(a.shape))
     block = lambda w: pl.BlockSpec((BLOCK, w), lambda r: (r, 0))
     outs = [
         jax.ShapeDtypeStruct((rows, d), low),
         jax.ShapeDtypeStruct((blocks, heads * BLOCK, padded), low),
         jax.ShapeDtypeStruct((rows, d), low),
-        jax.ShapeDtypeStruct(wi.shape, low),
-        jax.ShapeDtypeStruct(wd.shape, low),
+        jax.ShapeDtypeStruct((n, d // n, wi.shape[1] + wd.shape[1]), low),
         jax.ShapeDtypeStruct(bias.shape, f32),
         jax.ShapeDtypeStruct((8, d), f32),
     ]
@@ -307,7 +310,7 @@
         out_specs=[
             block(d),
             pl.BlockSpec((1, heads * BLOCK, padded), lambda r: (r, 0, 0)),
-            block(d), full(outs[3]), full(outs[4]), full(outs[5]), full(outs[6]),
+            block(d), full(outs[3]), full(outs[4]), full(outs[5]),
         ],
         out_shape=outs,
         scratch_shapes=[pltpu.VMEM(wi.shape, f32), pltpu.VMEM(wd.shape, f32)],
@@ -315,30 +318,241 @@
     )(length, second, context, cot, wi, wd, bias, norms)
 
 
+MESH = pl.DeviceIdType.MESH
+
+
+class Place:
+    def __init__(self):
+        self.dp, self.t = lax.axis_index("dp"), lax.axis_index("tensor")
+        self.n, self.ways = lax.axis_size("dp"), lax.axis_size("tensor")
+        self.majors = self.n // 2
+        self.a, self.b = self.dp // 2, self.dp % 2
+        self.chip, self.core = self.t // 2, self.t % 2
+        self.near = (self.dp, self.t + 1 - 2 * self.core)
+        self.across = (self.dp, (self.t + 2) % 4)
+        self.beside = (self.dp + 1 - 2 * self.b, self.t)
+
+    def major(self, k):
+        return ((self.a + k) % self.majors, (self.a + k) % self.majors * 2 + self.b)
+
+    def greet(self, everyone):
+        barrier = pltpu.get_barrier_semaphore()
+        others = [self.near, self.across]
+        if everyone:
+            others += [(self.dp, 3 - self.t)]
+            others += [((self.dp + k) % self.n, self.t) for k in range(1, self.n)]
+        else:
+            others += [self.beside]
+            others += [(self.major(k)[1], self.t) for k in range(1, self.majors)]
+        for other in others:
+            pl.semaphore_signal(barrier, inc=1, device_id=other, device_id_type=MESH)
+        pl.semaphore_wait(barrier, len(others))
+
+
+def send(src, dst, sems, k, to):
+    return pltpu.make_async_remote_copy(
+        src_ref=src,
+        dst_ref=dst,
+        send_sem=sems.at[0, k],
+        recv_sem=sems.at[1, k],
+        device_id=to,
+        device_id_type=MESH,
+    )
+
+
+def plus(*terms):
+    return functools.reduce(jnp.add, [t.astype(f32) for t in terms])
+
+
+class Scatter:
+    def __init__(self, place, mine, got, mid, last, sems):
+        self.p, self.mine, self.got, self.mid, self.last = place, mine, got, mid, last
+        self.pairs, self.lines = sems
+
+    def first(self, k):
+        p = self.p
+        a = p.major(k)[0]
+        return send(
+            self.mine.at[a * 2 + 1 - p.b], self.got.at[k % p.majors], self.pairs, k % p.majors, p.beside
+        )
+
+    def second(self, k):
+        return send(
+            self.mid.at[k - 1], self.last.at[k - 1], self.lines, k - 1, (self.p.major(k)[1], self.p.t)
+        )
+
+    def start(self):
+        for k in range(1, self.p.majors + 1):
+            self.first(k).start()
+
+    def add(self, k):
+        self.first(k).wait_recv()
+        self.mid[k - 1] = plus(
+            self.mine[self.p.major(k)[1]], self.got[k % self.p.majors]
+        ).astype(self.mid.dtype)
+
+    def forward(self, k):
+        self.second(k).start()
+
+    def finish(self):
+        p = self.p
+        for k in range(1, p.majors + 1):
+            self.first(k).wait_send()
+        self.first(p.majors).wait_recv()
+        for k in range(1, p.majors):
+            self.second(k).wait()
+        return plus(
+            self.mine[p.dp], self.got[0], *[self.last[k] for k in range(p.majors - 1)]
+        )
+
+
+class Exchange:
+    def __init__(self, slots, sems, me, count, device):
+        self.slots, self.sems, self.me, self.count, self.device = slots, sems, me, count, device
+
+    def copy(self, k, source):
+        return pltpu.make_async_remote_copy(
+            src_ref=self.slots.at[source],
+            dst_ref=self.slots.at[source],
+            send_sem=self.sems.at[0, k],
+            recv_sem=self.sems.at[1, source],
+            device_id=self.device((self.me + k) % self.count),
+            device_id_type=MESH,
+        )
+
+    def start(self):
+        for k in range(1, self.count):
+            self.copy(k, self.me).start()
+
+    def total(self):
+        for k in range(1, self.count):
+            self.copy(k, (self.me + k) % self.count).wait_recv()
+        return functools.reduce(jnp.add, [self.slots[k] for k in range(self.count)])
+
+    def finish(self):
+        for k in range(1, self.count):
+            self.copy(k, self.me).wait_send()
+
+
+def scatter_scratch(majors, rows, columns):
+    return [
+        pltpu.VMEM((majors, rows, columns), low),
+        pltpu.VMEM((majors - 1, rows, columns), low),
+        pltpu.VMEM((majors - 1, rows, columns), low),
+        pltpu.SemaphoreType.DMA((2, majors)),
+        pltpu.SemaphoreType.DMA((2, majors - 1)),
+    ]
+
+
 def back_kernel(
-    width, qkv_ref, qx_ref, dox_ref, first_ref, part_ref, wq_ref, norm_ref, table_ref,
-    gn_ref, gwq_ref, gbias_ref, gsmall_ref, keyt_ref, dqt_ref, gwq_sum,
+    width, hidden, length_ref, qkv_ref, qx_ref, dox_ref, first_ref, part_ref, wq_ref, norm_ref,
+    table_ref, branch_ref, gw_ref, gbin_ref, gpart_ref, tokens_ref, cot_ref,
+    out_ref, gx_ref, gq_ref, gbq_ref, go_ref, gi_ref, gb_ref, gd_ref, small_ref,
+    keyt_ref, dqt_ref, dk_ref, dv_ref, gwq_sum, gbias_sum, gsmall_sum,
+    gn_ref, gn_near, gn_mid, gn_own, gn_far, gn_sem1, gn_sem2,
+    br_near, br_mid, br_far, br_sem1, br_sem2,
+    w_got, w_mid, w_last, w_sem1, w_sem2,
+    gq_low, q_got, q_mid, q_last, q_sem1, q_sem2,
+    line_ref, cross_ref, line_sem, cross_sem,
 ):
     heads = width // HD
     rows = qkv_ref.shape[0]
     padded = qkv_ref.shape[1] // 3
     blocks = rows // BLOCK
+    local = tokens_ref.shape[0]
+    per = local // BLOCK
+    d = tokens_ref.shape[1]
     scale = HD ** (-0.5)
     step = pl.program_id(0)
+    last = blocks - 1
+    here = Place()
+    weights = Scatter(here, gw_ref, w_got, w_mid, w_last, (w_sem1, w_sem2))
+    final = Scatter(here, gq_low, q_got, q_mid, q_last, (q_sem1, q_sem2))
+
+    def near_branch(chip):
+        owner = chip * 2 + 1 - here.core
+        return send(
+            branch_ref.at[pl.ds(pl.multiple_of(owner * local, local), local)], br_near.at[chip],
+            br_sem1, chip, here.near,
+        )
+
+    def far_branch():
+        return send(br_mid, br_far, br_sem2, 0, here.across)
+
+    def branch_rows(chip):
+        owner = chip * 2 + here.core
+        return branch_ref[pl.ds(pl.multiple_of(owner * local, local), local), :]
+
+    def block_of(number):
+        return number // 2 + number % 2 * (blocks - 1 - number // 2 * 2)
+
+    def near_block(r):
+        slot = r // per // 2 * per + r % per
+        return send(gn_ref.at[r], gn_near.at[slot], gn_sem1, slot, here.near)
+
+    def far_block(r):
+        return send(gn_mid.at[r % per], gn_far.at[r % per], gn_sem2, r % per, here.across)
+
+    def collect(r):
+        owner = r // per
+
+        @pl.when(owner % 2 == here.core)
+        def _():
+            near_block(r).wait_recv()
+            total = plus(gn_ref[r], gn_near[owner // 2 * per + r % per])
+
+            @pl.when(owner // 2 == here.chip)
+            def _():
+                gn_own[r % per] = total
+
+            @pl.when(owner // 2 != here.chip)
+            def _():
+                gn_mid[r % per] = total.astype(low)
+
+    def pass_on(r):
+        owner = r // per
+
+        @pl.when((owner % 2 == here.core) & (owner // 2 != here.chip))
+        def _():
+            far_block(r).start()
 
     @pl.when(step == 0)
     def _():
+        here.greet(True)
+        weights.start()
+        for chip in range(2):
+            near_branch(chip).start()
         dqt_ref[...] = jnp.zeros_like(dqt_ref)
+        dk_ref[...] = jnp.zeros_like(dk_ref)
+        dv_ref[...] = jnp.zeros_like(dv_ref)
         gwq_sum[...] = jnp.zeros_like(gwq_sum)
-        gbias_ref[...] = jnp.zeros_like(gbias_ref)
-        gsmall_ref[...] = jnp.zeros_like(gsmall_ref)
-
-    here = pl.ds(pl.multiple_of(step * BLOCK, BLOCK), BLOCK)
-    keys = qkv_ref[here, padded : 2 * padded]
-    values = qkv_ref[here, 2 * padded :]
-    keyt_ref[...] = keys.astype(f32).T[:width].astype(low)
-
-    def pair(i, own):
+        gbias_sum[...] = jnp.zeros_like(gbias_sum)
+        gsmall_sum[...] = jnp.zeros_like(gsmall_sum)
+
+        @pl.loop(0, blocks)
+        def _(j):
+            k = qkv_ref[pl.ds(pl.multiple_of(j * BLOCK, BLOCK), BLOCK), padded : 2 * padded]
+            keyt_ref[j] = k.astype(f32).T[:width].astype(low)
+
+    @pl.when(step == 1)
+    def _():
+        for chip in range(2):
+            near_branch(chip).wait_recv()
+        br_mid[...] = plus(branch_rows(1 - here.chip), br_near[1 - here.chip]).astype(low)
+
+    for k in range(1, here.majors):
+
+        @pl.when(step == min(k, last - 2))
+        def _():
+            weights.add(k)
+
+    @pl.when(step > 0)
+    def _():
+        collect(block_of(step - 1))
+
+    def pair(i, j, own):
+        at = pl.ds(pl.multiple_of(j * BLOCK, BLOCK), BLOCK)
+        keys, values = qkv_ref[at, padded : 2 * padded], qkv_ref[at, 2 * padded :]
         query, dout = qx_ref[i], dox_ref[i]
         p = jnp.exp(dot(keys, query, NT) * scale)
         if own:
@@ -346,81 +560,202 @@
             query_at = lax.broadcasted_iota(jnp.int32, p.shape, 1) % BLOCK
             p = jnp.where(key_at <= query_at, p, 0.0)
         ds = (p * dot(values, dout, NT)).astype(low)
-        grad_value = dot(p.astype(low), dout, NN)
-        grad_key = dot(ds, query, NN)
+        dv_ref[j] += dot(p.astype(low), dout, NN)
+        dk_ref[j] += dot(ds, query, NN)
         for h in range(heads):
             dqt_ref[i, h * HD : (h + 1) * HD, :] += dot(
-                keyt_ref[h * HD : (h + 1) * HD, :], ds[:, h * BLOCK : (h + 1) * BLOCK], NN
+                keyt_ref[j, h * HD : (h + 1) * HD, :], ds[:, h * BLOCK : (h + 1) * BLOCK], NN
             )
-        return grad_key, grad_value
-
-    def later(i, carry):
-        grad_key, grad_value = pair(i, False)
-        return carry[0] + grad_key, carry[1] + grad_value
-
-    grad_key, grad_value = lax.fori_loop(step + 1, blocks, later, pair(step, True))
-
-    tables = rotary_rows(table_ref, step)
+
+    turn = step // 2
+    odd = step % 2
+    now = block_of(step)
+
+    @pl.loop(0, last - step)
+    def _(number):
+        other = turn + 1 + number
+        pair(other + odd * (last - turn - other), turn + odd * (other - turn), False)
+
+    @pl.when(step == 1)
+    def _():
+        far_branch().start()
+
+    for k in range(1, here.majors):
+
+        @pl.when(step == min(k, last - 2))
+        def _():
+            weights.forward(k)
+
+    @pl.when(step > 0)
+    def _():
+        pass_on(block_of(step - 1))
+
+    pair(now, now, True)
+
+    tables = rotary_rows(table_ref, now)
     inside = lax.broadcasted_iota(jnp.int32, (BLOCK, padded), 1) < width
-    grad_query = jnp.concatenate(
-        [dqt_ref[step].T, jnp.zeros((BLOCK, padded - width), f32)], axis=1
-    )
+    grad_query = jnp.concatenate([dqt_ref[now].T, jnp.zeros((BLOCK, padded - width), f32)], axis=1)
     projected = jnp.concatenate(
         [
             rotate(grad_query * scale, tables, -1),
-            rotate(jnp.where(inside, grad_key * scale, 0.0), tables, -1),
-            jnp.where(inside, grad_value, 0.0),
+            rotate(jnp.where(inside, dk_ref[now] * scale, 0.0), tables, -1),
+            jnp.where(inside, dv_ref[now], 0.0),
         ],
         axis=1,
     )
-    gbias_ref[...] += jnp.sum(projected, axis=0, keepdims=True)
+    gbias_sum[...] += jnp.sum(projected, axis=0, keepdims=True)
     proj_low = projected.astype(low)
-    first = first_ref[...]
+    at = pl.ds(pl.multiple_of(now * BLOCK, BLOCK), BLOCK)
+    first = first_ref[at, :]
     gwq_sum[...] += dot(first, proj_low, TN)
     part = dot(proj_low, wq_ref[...], NT)
-    gsmall_ref[0:1, :] += jnp.sum(part * first.astype(f32), axis=0, keepdims=True)
-    gsmall_ref[1:2, :] += jnp.sum(part, axis=0, keepdims=True)
-    gn_ref[...] = (part * norm_ref[0:1, :] + part_ref[...].astype(f32)).astype(low)
-
-    @pl.when(step == blocks - 1)
-    def _():
-        gwq_ref[...] = gwq_sum[...].astype(low)
-
-
-def back(width, qkv, qx, dox, first, part, wq, norms, table):
+    gsmall_sum[0:1, :] += jnp.sum(part * first.astype(f32), axis=0, keepdims=True)
+    gsmall_sum[1:2, :] += jnp.sum(part, axis=0, keepdims=True)
+    gn_ref[now] = (part * norm_ref[0:1, :] + part_ref[at, :].astype(f32)).astype(low)
+
+    @pl.when(now // per % 2 != here.core)
+    def _():
+        near_block(now).start()
+
+    row = lax.broadcasted_iota(jnp.int32, (local, d), 0) + here.t * local
+    kept = row < length_ref[0]
+
+    @pl.when(step == last - 1)
+    def _():
+        far_branch().wait()
+        for chip in range(2):
+            near_branch(chip).wait_send()
+        total = plus(branch_rows(here.chip), br_near[here.chip], br_far[...])
+        total = total + (norm_ref[4:5, :] + norm_ref[5:6, :])
+        out_ref[...] = tokens_ref[...].astype(f32) + jnp.where(kept, total, 0.0)
+
+    @pl.when(step == last)
+    def _():
+        side = gwq_sum.shape[0] // here.n
+        for block in range(here.n):
+            rows_of = slice(block * side, (block + 1) * side)
+            gq_low[block] = jnp.concatenate(
+                [gwq_sum[rows_of, k * padded : k * padded + width] for k in range(3)], axis=1
+            ).astype(low)
+        cot = cot_ref[...].astype(f32)
+        dense = jnp.sum(jnp.where(kept, cot, 0.0), axis=0, keepdims=True)
+        line_ref[here.dp] = jnp.concatenate(
+            [gbias_sum[...], gbin_ref[...], gsmall_sum[0:2, :], gpart_ref[0:2, :], dense, dense]
+        )
+        final.start()
+
+        line = Exchange(line_ref, line_sem, here.dp, here.n, lambda to: (to, here.t))
+        cross = Exchange(cross_ref, cross_sem, here.t, here.ways, lambda to: (here.dp, to))
+        line.start()
+        collect(now)
+        x = tokens_ref[...].astype(f32)
+        shifted = x - jnp.mean(x, axis=1, keepdims=True)
+        inv_std = lax.rsqrt(jnp.mean(shifted * shifted, axis=1, keepdims=True) + EPS)
+        normed = shifted * inv_std
+        pass_on(now)
+
+        total = weights.finish()
+        gi_ref[...] = total[:, :hidden]
+        gd_ref[...] = total[:, hidden : 2 * hidden].T
+        go_ref[...] = total[:, 2 * hidden : 2 * hidden + width].T
+
+        for k in range(1, here.majors):
+            final.add(k)
+            final.forward(k)
+        summed = line.total()
+        gbq_ref[...] = summed[0:1, :]
+        gb_ref[...] = summed[1:2, :]
+        cross_ref[here.t] = summed
+        for k in range(per):
+            far_block(k).wait()
+        for slot in range(2 * per):
+            near_block(slot // per * 2 * per + (1 - here.core) * per + slot % per).wait_send()
+        grad_normed = jnp.concatenate([gn_own[k] + gn_far[k].astype(f32) for k in range(per)])
+        cross.start()
+        gx_ref[...] = cot + inv_std * (
+            grad_normed
+            - jnp.mean(grad_normed, axis=1, keepdims=True)
+            - normed * jnp.mean(grad_normed * normed, axis=1, keepdims=True)
+        )
+        summed = cross.total()
+        for k in range(2):
+            product, plain = summed[2 + 2 * k : 3 + 2 * k, :], summed[3 + 2 * k : 4 + 2 * k, :]
+            gain, bias = norm_ref[2 * k : 2 * k + 1, :], norm_ref[2 * k + 1 : 2 * k + 2, :]
+            small_ref[2 * k : 2 * k + 1, :] = (product - bias * plain) / gain
+            small_ref[2 * k + 1 : 2 * k + 2, :] = plain
+        small_ref[4:5, :] = summed[6:7, :]
+        line.finish()
+        cross.finish()
+        gq_ref[...] = final.finish()
+
+
+def back(width, length, qkv, qx, dox, first, part, wq, norms, table, branch, gw, gb_in, gpart, tokens, cot):
     rows, d = first.shape
     padded = qkv.shape[1] // 3
     blocks = rows // BLOCK
-    full = lambda a: pl.BlockSpec(a.shape, lambda r: (0,) * a.ndim)
-    block = lambda w: pl.BlockSpec((BLOCK, w), lambda r: (r, 0))
+    local = tokens.shape[0]
+    per = local // BLOCK
+    n, side, columns = gw.shape
+    hidden = gb_in.shape[1]
+    majors = n // 2
+    ways = lax.axis_size("tensor")
+    assert ways == 4 and 3 * padded == d == hidden and side * n == d
+    full = lambda a: pl.BlockSpec(
+        a.shape, lambda r: (0,) * len(a.shape), pipeline_mode=pl.Buffered(1)
+    )
     outs = [
-        jax.ShapeDtypeStruct((rows, d), low),
-        jax.ShapeDtypeStruct(wq.shape, low),
-        jax.ShapeDtypeStruct((1, wq.shape[1]), f32),
-        jax.ShapeDtypeStruct((8, d), f32),
+        jax.ShapeDtypeStruct((local, d), f32),
+        jax.ShapeDtypeStruct((local, d), f32),
+        jax.ShapeDtypeStruct((side, 3 * width), f32),
+        jax.ShapeDtypeStruct((1, 3 * padded), f32),
+        jax.ShapeDtypeStruct((width, side), f32),
+        jax.ShapeDtypeStruct((side, hidden), f32),
+        jax.ShapeDtypeStruct((1, hidden), f32),
+        jax.ShapeDtypeStruct((hidden, side), f32),
+        jax.ShapeDtypeStruct((5, d), f32),
     ]
+    args = (qkv, qx, dox, first, part, wq, norms, table, branch, gw, gb_in, gpart, tokens, cot)
     return pl.pallas_call(
-        functools.partial(back_kernel, width),
+        functools.partial(back_kernel, width, hidden),
         name="back",
         grid=(blocks,),
-        in_specs=[
-            full(qkv), full(qx), full(dox), block(d), block(d), full(wq), full(norms), full(table),
-        ],
-        out_specs=[block(d)] + [full(o) for o in outs[1:]],
+        in_specs=[pl.BlockSpec(memory_space=pltpu.SMEM)] + [full(a) for a in args],
+        out_specs=[pl.BlockSpec(memory_space=pltpu.VMEM)] * len(outs),
         out_shape=outs,
         scratch_shapes=[
-            pltpu.VMEM((width, BLOCK), low),
+            pltpu.VMEM((blocks, width, BLOCK), low),
             pltpu.VMEM((blocks, width, BLOCK), f32),
+            pltpu.VMEM((blocks, BLOCK, padded), f32),
+            pltpu.VMEM((blocks, BLOCK, padded), f32),
             pltpu.VMEM(wq.shape, f32),
+            pltpu.VMEM((1, 3 * padded), f32),
+            pltpu.VMEM((8, d), f32),
+            pltpu.VMEM((blocks, BLOCK, d), low),
+            pltpu.VMEM((2 * per, BLOCK, d), low),
+            pltpu.VMEM((per, BLOCK, d), low),
+            pltpu.VMEM((per, BLOCK, d), f32),
+            pltpu.VMEM((per, BLOCK, d), low),
+            pltpu.SemaphoreType.DMA((2, 2 * per)),
+            pltpu.SemaphoreType.DMA((2, per)),
+            pltpu.VMEM((2, local, d), low),
+            pltpu.VMEM((local, d), low),
+            pltpu.VMEM((local, d), low),
+            pltpu.SemaphoreType.DMA((2, 2)),
+            pltpu.SemaphoreType.DMA((2, 1)),
+        ]
+        + scatter_scratch(majors, side, columns)
+        + [pltpu.VMEM((n, side, 3 * width), low)]
+        + scatter_scratch(majors, side, 3 * width)
+        + [
+            pltpu.VMEM((n, 8, d), f32),
+            pltpu.VMEM((ways, 8, d), f32),
+            pltpu.SemaphoreType.DMA((2, n)),
+            pltpu.SemaphoreType.DMA((2, ways)),
         ],
-        compiler_params=pltpu.CompilerParams(vmem_limit_bytes=VMEM),
-    )(qkv, qx, dox, first, part, wq, norms, table)
-
-
-def layer_norm(values):
-    shifted = values - jnp.mean(values, axis=-1, keepdims=True)
-    inv_std = lax.rsqrt(jnp.mean(shifted * shifted, axis=-1, keepdims=True) + EPS)
-    return shifted * inv_std, inv_std
+        compiler_params=pltpu.CompilerParams(
+            vmem_limit_bytes=VMEM, collective_id=2, has_side_effects=True
+        ),
+    )(length, *args)
 
 
 def per_device(
@@ -438,7 +773,7 @@
     wq = jnp.pad(w_qkv, ((0, 0), (0, 0), (0, extra))).reshape(-1, 3 * padded)
     bq = jnp.pad(b_qkv, ((0, 0), (0, extra))).reshape(1, 3 * padded)
     wd = jnp.concatenate([w_down.T, jnp.pad(w_attn_out.T, ((0, 0), (0, extra)))], axis=1)
-    norms = jnp.stack([norm1_gain, norm1_bias, norm2_gain, norm2_bias])
+    norms = jnp.stack([norm1_gain, norm1_bias, norm2_gain, norm2_bias, b_out, b_down])
     table = jnp.asarray(rotary_base())
 
     x_full = gather(tokens, "tensor")
@@ -448,50 +783,22 @@
 
     first, second, qkv = front(width, x_full, norms, wq_full, bq, table)
     context, qx = attend(width, qkv)
-    branch, dox, part, gwi, gwd, gb_in, small2 = feed(
+    branch, dox, part, gw, gb_in, gpart = feed(
         width, seq_lengths, second, context, cot_full, wi_full, wd_full, b_in.reshape(1, -1), norms
     )
-    scatter = lambda a, axis: lax.psum_scatter(a, axis, scatter_dimension=0, tiled=True).astype(f32)
-    branches = scatter(branch, "tensor")
-    gn, gwq, gb_qkv, small1 = back(width, qkv, qx, dox, first, part, wq_full, norms, table)
-    grad_normed = scatter(gn, "tensor")
-    gwi, gwd, gwq = scatter(gwi, "dp"), scatter(gwd, "dp"), scatter(gwq, "dp")
-
-    row = lax.axis_index("tensor") * local_rows + jnp.arange(local_rows)
-    row_mask = (row < seq_lengths[0]).astype(f32)[:, None]
-    x = tokens.astype(f32)
-    cot = cotangent.astype(f32)
-    output = x + row_mask * (branches + b_out + b_down)
-    normed, inv_std = layer_norm(x)
-    grad_x = cot + inv_std * (
-        grad_normed
-        - jnp.mean(grad_normed, axis=-1, keepdims=True)
-        - normed * jnp.mean(grad_normed * normed, axis=-1, keepdims=True)
-    )
-    gb_qkv = gb_qkv.reshape(3, padded)[:, :width]
-    small = jnp.concatenate(
-        [small1[:2], small2[:2], jnp.sum(row_mask * cot, axis=0, keepdims=True)]
-    )
-    gb_qkv, gb_in, small = lax.psum((gb_qkv, gb_in, small), "dp")
-    small = lax.psum(small, "tensor")
-    small = jnp.stack(
-        [
-            (small[0] - norm1_bias * small[1]) / norm1_gain,
-            small[1],
-            (small[2] - norm2_bias * small[3]) / norm2_gain,
-            small[3],
-            small[4],
-        ]
+    output, grad_x, gq, gb_qkv, g_out, g_in, gb_in, g_down, small = back(
+        width, seq_lengths, qkv, qx, dox, first, part, wq_full, norms, table, branch, gw, gb_in, gpart,
+        tokens, cotangent,
     )
     return (
         output,
         grad_x,
-        gwq.reshape(-1, 3, padded)[:, :, :width],
-        gb_qkv,
-        gwd[:, hidden : hidden + width].T,
-        gwi,
+        gq.reshape(-1, 3, width),
+        gb_qkv.reshape(3, padded)[:, :width],
+        g_out,
+        g_in,
         gb_in.reshape(-1),
-        gwd[:, :hidden].T,
+        g_down,
         small,
     )
 

time: 610 us -> 327 us (0.54)
  waiting for transfers between devices: 419 us -> 147 us
  blocking collectives: 47.5 us -> 0 us
  Pallas kernels: 108 us -> 146 us
  other arithmetic: 10.8 us -> 3.7 us
    reduce_scatter x5 -> x0, waiting for transfers between devices: 268 us -> none  [per_device(): lax.psum_scatter(a, axis, scatter_dimension=0, tiled=True).astype(f32)]
    psum x2 -> x0, blocking collectives: 47.5 us -> none  [the longest x1 37.1 us: per_device(): gb_qkv, gb_in, small = lax.psum((gb_qkv, gb_in, small), 'dp')]
    pallas_call x1, Pallas kernels: 42.2 us -> 80.2 us  [back(): pl.pallas_call(functools.partial(back_kernel, width, hidden), name='back'...]
    unnamed x45 -> x36, local copies, waits for them, and re-layouts: 4.78 us -> 11.8 us
    reduce_sum x4 -> x0, other arithmetic: 6.16 us -> none  [the longest x1 3.69 us: per_device(): jnp.sum(row_mask * cot, axis=0, keepdims=True)]
  transfers between devices with their start and end apart: 10 -> 5, of which waited for: 10 -> 5; matrix products, arithmetic and copies ran while one was open for 2% -> 1% of each run, Pallas kernels for 6% -> 12%
where the time goes in v2:
time: 327 us; the launch traced here: 326 us
  waiting for transfers between devices  147 us (45%)
  Pallas kernels  146 us (45%)
  local copies, waits for them, and re-layouts  14.8 us (5%)
  between operations  14.7 us (4%)
  other arithmetic  3.7 us (1%)
    all_gather x5, waiting for transfers between devices, per_device(): gather = lambda a, axis: lax.all_gather(a, axis, axis=0, tiled=True)  145 us
    pallas_call x1, Pallas kernels, back(): pl.pallas_call(functools.partial(back_kernel, width, hidden), name='back'...  80.2 us
    pallas_call x1, Pallas kernels, attend(): pl.pallas_call(functools.partial(attend_kernel, width), name='attend', gr...  29.1 us
    pallas_call x1, Pallas kernels, feed(): pl.pallas_call(functools.partial(feed_kernel, width), name='feed', grid=(...  26.4 us
    unnamed x36, local copies, waits for them, and re-layouts  11.8 us
    pallas_call x1, Pallas kernels, front(): pl.pallas_call(functools.partial(front_kernel, width), name='front', grid...  10.1 us
  transfers between devices with their start and end apart: 5, of which 5 were waited for; matrix products, arithmetic and copies ran while one was open for 1% of the time, Pallas kernels for 12%

profile of v2, /device:TPU:0, one launch (start us, length us, event | category | flops | bytes accessed | tf_op | source)
XLA Modules:
  0.0 326.2 jit_solution(5621711427877963189)
XLA Ops:
  7.2 0.0 copy-start.4
  7.2 0.0 copy-start.5
  7.2 0.0 copy-start.6
  7.2 0.0 copy-start.7
  7.2 0.0 copy-start.8
  7.2 0.0 copy-start.9
  7.2 0.0 copy-start.10
  7.2 0.0 copy-start.11
  7.3 0.0 all-gather.8.cloned.1.call-start
  7.3 1.0 copy.34
  8.3 0.1 pad.12.clone
  8.4 0.7 copy.35
  9.1 0.0 all-gather.8.cloned.1.call-update
  9.2 0.0 all-gather.6.cloned.1.call-start
  9.2 0.7 all-gather.6.cloned.1.call-update
  9.9 0.0 all-gather.12.cloned.1.call-start
  10.0 0.7 all-gather.12.cloned.1.call-update
  10.6 0.0 all-gather.14.cloned.1.call-start
  10.7 0.9 copy.30
  11.6 1.6 fusion.1
  13.2 0.0 all-gather.14.cloned.1.call-update
  13.2 0.0 all-gather.10.cloned.1.call-start
  13.3 0.5 all-gather.10.cloned.1.call-update
  14.5 0.0 copy-done.4
  14.5 0.0 copy-done.5
  14.5 0.0 copy-done.6
  14.5 0.0 copy-done.7
  14.5 0.0 copy-done.8
  14.6 0.6 reshape.38.bias_ref
  15.1 0.0 copy-done.9
  15.1 0.0 copy-done.10
  15.2 0.0 copy-done.11
  15.2 0.6 copy.36
  15.8 0.6 stack.27.norm_ref
  16.4 38.3 %all-gather.8.cloned.1.call-done.wq_ref = bf16[768,768]{1,0:T(8,128)(2,1)} async-done(((bf16[96,768]{1,0:T(8,128)(2,1)}), bf16[768,768]{1,0:T(8,128)(2,1)}) %all-gather.8.cloned.1.call-update) | async-done | bytes 1179664 | tf_op jit(solution)/shard_map/all_gather | solution.py:772
  54.7 28.8 %all-gather.6.cloned.1.call-done.x_ref = bf16[2048,768]{1,0:T(8,128)(2,1)} async-done(((bf16[512,768]{1,0:T(8,128)(2,1)}), bf16[2048,768]{1,0:T(8,128)(2,1)}) %all-gather.6.cloned.1.call-update) | async-done | bytes 3145744 | tf_op jit(solution)/shard_map/all_gather | solution.py:772
  83.5 10.1 %front.1 = (bf16[2048,768]{1,0:T(8,128)(2,1)}, bf16[2048,768]{1,0:T(8,128)(2,1)}, bf16[2048,768]{1,0:T(8,128)(2,1)}) custom-call(bf16[2048,768]{1,0:T(8,128)(2,1)} %all-gather.6.cloned.1.call-done.x_ref, f32[6,768]{1,0:T(8,128)} %stack.27.norm_ref, bf16[768,768]{1,0:T(8,128)(2,1)} %all-gather.8.cloned.1.call-done.wq_ref, f32[1,768]{1,0:T(1,128)} %bitcast.15, ...), custom_call_target="tpu_custom_call" | custom-call | tf_op jit(solution)/shard_map/front/pallas_call | solution.py:111
  93.5 29.1 %attend.1 = (bf16[2048,256]{1,0:T(8,128)(2,1)}, bf16[8,768,256]{2,1,0:T(8,128)(2,1)}) custom-call(bf16[2048,768]{1,0:T(8,128)(2,1)} %get-tuple-element.29.qkv_ref), custom_call_target="tpu_custom_call" | custom-call | tf_op jit(solution)/shard_map/attend/pallas_call | solution.py:205
  122.6 4.2 %all-gather.12.cloned.1.call-done.wi_ref = bf16[768,768]{1,0:T(8,128)(2,1)} async-done(((bf16[96,768]{1,0:T(8,128)(2,1)}), bf16[768,768]{1,0:T(8,128)(2,1)}) %all-gather.12.cloned.1.call-update) | async-done | bytes 1179664 | tf_op jit(solution)/shard_map/all_gather | solution.py:772
  126.8 45.5 %all-gather.14.cloned.1.call-done.wd_ref = bf16[768,1024]{1,0:T(8,128)(2,1)} async-done(((bf16[96,1024]{1,0:T(8,128)(2,1)}), bf16[768,1024]{1,0:T(8,128)(2,1)}) %all-gather.14.cloned.1.call-update) | async-done | bytes 1572880 | tf_op jit(solution)/shard_map/all_gather | solution.py:772
  172.4 28.3 %all-gather.10.cloned.1.call-done.cot_ref = bf16[2048,768]{1,0:T(8,128)(2,1)} async-done(((bf16[512,768]{1,0:T(8,128)(2,1)}), bf16[2048,768]{1,0:T(8,128)(2,1)}) %all-gather.10.cloned.1.call-update) | async-done | bytes 3145744 | tf_op jit(solution)/shard_map/all_gather | solution.py:772
  200.7 26.4 %feed.1 = (bf16[2048,768]{1,0:T(8,128)(2,1)}, bf16[8,768,256]{2,1,0:T(8,128)(2,1)}, bf16[2048,768]{1,0:T(8,128)(2,1)}, bf16[8,96,1792]{2,1,0:T(8,128)(2,1)}, f32[1,768]{1,0:T(1,128)}, /*index=5*/f32[8,768]{1,0:T(8,128)}) custom-call(s32[1]{0:T(128)S(6)} %copy.42.length_ref, bf16[2048,768]{1,0:T(8,128)(2,1)} %get-tuple-element.31.second_ref, ...), custom_call_target="tpu_custom_call" | custom-call | tf_op jit(solution)/shard_map/feed/pallas_call | solution.py:302
  227.0 80.2 %back.1 = (f32[512,768]{1,0:T(8,128)}, f32[512,768]{1,0:T(8,128)}, f32[96,576]{1,0:T(8,128)}, f32[1,768]{1,0:T(1,128)}, f32[192,96]{1,0:T(8,128)}, /*index=5*/f3...) custom-call(s32[1]{0:T(128)S(6)} %copy.42.length_ref, ...), custom_call_target="tpu_custom_call" | custom-call | tf_op jit(solution)/shard_map/back/pallas_call | solution.py:718
  307.3 0.0 copy-start
  307.3 0.8 reduce
  308.1 0.6 reshape.40
  308.7 1.3 reduce.1
  310.0 1.1 copy.31
  311.1 0.9 copy.32
  311.9 1.9 copy.33
  313.8 0.0 copy-start.2
  313.8 0.0 copy-start.1
  313.8 0.0 copy-start.3
  313.8 2.7 copy.43
  316.5 0.0 copy-done
  316.5 1.1 copy.44
  317.7 0.0 copy-done.2
  317.7 0.6 copy.45
  318.3 0.0 copy-done.1
  318.3 0.7 copy.46
  319.0 0.0 copy-done.3
  319.0 0.6 copy.47
  (7 shorter events, 0.0 us)
Async XLA Ops:
  7.2 7.3 %copy-start.4 = (f32[768]{0:T(1024)S(1)}, f32[768]{0:T(1024)}, u32[]{:S(2)}) copy-start(f32[768]{0:T(1024)} %param.19) | copy-start | bytes 9220
  7.2 7.3 %copy-start.5 = (f32[768]{0:T(1024)S(1)}, f32[768]{0:T(1024)}, u32[]{:S(2)}) copy-start(f32[768]{0:T(1024)} %param.20) | copy-start | bytes 9220
  7.2 7.3 %copy-start.6 = (f32[768]{0:T(1024)S(1)}, f32[768]{0:T(1024)}, u32[]{:S(2)}) copy-start(f32[768]{0:T(1024)} %param.21) | copy-start | bytes 9220
  7.2 7.3 %copy-start.7 = (f32[768]{0:T(1024)S(1)}, f32[768]{0:T(1024)}, u32[]{:S(2)}) copy-start(f32[768]{0:T(1024)} %param.22) | copy-start | bytes 9220
  7.2 7.3 %copy-start.8 = (f32[768]{0:T(1024)S(1)}, f32[768]{0:T(1024)}, u32[]{:S(2)}) copy-start(f32[768]{0:T(1024)} %param.27) | copy-start | bytes 9220
  7.2 7.9 %copy-start.9 = (f32[768]{0:T(1024)S(1)}, f32[768]{0:T(1024)}, u32[]{:S(2)}) copy-start(f32[768]{0:T(1024)} %param.29) | copy-start | bytes 9220
  7.2 7.9 %copy-start.10 = (f32[768]{0:T(1024)S(1)}, f32[768]{0:T(1024)}, u32[]{:S(2)}) copy-start(f32[768]{0:T(1024)} %param.30) | copy-start | bytes 9220
  7.2 7.9 %copy-start.11 = (f32[3,192]{1,0:T(4,128)S(1)}, f32[3,192]{1,0:T(4,128)}, u32[]{:S(2)}) copy-start(f32[3,192]{1,0:T(4,128)} %param.24) | copy-start | bytes 6916
  7.3 47.4 %all-gather.8.cloned.1.call-start = ((), (), s32[]{:S(2)}) async-start(), calls=%async_computation.1 | async-start | bytes 1327104 | tf_op jit(solution)/shard_map/all_gather | solution.py:772
  9.2 74.3 %all-gather.6.cloned.1.call-start = ((), (), s32[]{:S(2)}) async-start(), calls=%async_computation | async-start | bytes 3932160 | tf_op jit(solution)/shard_map/all_gather | solution.py:772
  9.9 116.9 %all-gather.12.cloned.1.call-start = ((), (), s32[]{:S(2)}) async-start(), calls=%async_computation.3 | async-start | bytes 1327104 | tf_op jit(solution)/shard_map/all_gather | solution.py:772
  10.6 161.7 %all-gather.14.cloned.1.call-start = ((), (), s32[]{:S(2)}) async-start(), calls=%async_computation.4 | async-start | bytes 1769472 | tf_op jit(solution)/shard_map/all_gather | solution.py:772
  13.2 187.4 %all-gather.10.cloned.1.call-start = ((), (), s32[]{:S(2)}) async-start(), calls=%async_computation.2 | async-start | bytes 3932160 | tf_op jit(solution)/shard_map/all_gather | solution.py:772
  307.3 9.3 %copy-start = (f32[512,768]{1,0:T(8,128)S(1)}, f32[512,768]{1,0:T(8,128)}, u32[]{:S(2)}) copy-start(f32[512,768]{1,0:T(8,128)} %get-tuple-element.77) | copy-start | bytes 4718596
  313.8 3.9 %copy-start.2 = (f32[192,96]{1,0:T(8,128)S(1)}, f32[192,96]{1,0:T(8,128)}, u32[]{:S(2)}) copy-start(f32[192,96]{1,0:T(8,128)} %get-tuple-element.80) | copy-start | bytes 221188
  313.8 4.5 %copy-start.1 = (f32[96,768]{1,0:T(8,128)S(1)}, f32[96,768]{1,0:T(8,128)}, u32[]{:S(2)}) copy-start(f32[96,768]{1,0:T(8,128)} %get-tuple-element.81) | copy-start | bytes 884740
  313.8 5.2 %copy-start.3 = (f32[5,768]{1,0:T(8,128)S(1)}, f32[5,768]{1,0:T(8,128)}, u32[]{:S(2)}) copy-start(f32[5,768]{1,0:T(8,128)} %get-tuple-element.84) | copy-start | bytes 46084
Sparse Core Ops, SparseCore 0:
  10.8 43.8 all-gather.7
  56.3 27.1 all-gather.5
  85.7 41.1 all-gather.11
  129.4 42.8 all-gather.13
  173.8 26.8 all-gather.9

commit v3 on v2

--- a/solution.py
+++ b/solution.py
@@ -85,45 +85,359 @@
     return first, second, value - first - second
 
 
-def front_kernel(width, x_ref, norm_ref, wq_ref, bq_ref, table_ref, first_ref, second_ref, qkv_ref):
-    padded = qkv_ref.shape[1] // 3
-    x = x_ref[...].astype(f32)
-    shifted = x - jnp.mean(x, axis=1, keepdims=True)
-    inv_std = lax.rsqrt(jnp.mean(shifted * shifted, axis=1, keepdims=True) + EPS)
-    normed = shifted * inv_std
-    first = (normed * norm_ref[0:1, :] + norm_ref[1:2, :]).astype(low)
-    first_ref[...] = first
-    second_ref[...] = (normed * norm_ref[2:3, :] + norm_ref[3:4, :]).astype(low)
-    projected = dot(first, wq_ref[...], NN) + bq_ref[...]
-    tables = rotary_rows(table_ref, pl.program_id(0))
-    lane = lax.broadcasted_iota(jnp.int32, (BLOCK, padded), 1)
-    extra = (lane >= width) & (lane < width + 3)
-    qkv_ref[:, :padded] = rotate(projected[:, :padded], tables, 1).astype(low)
-    keys = rotate(projected[:, padded : 2 * padded], tables, 1)
-    qkv_ref[:, padded : 2 * padded] = jnp.where(extra, 1.0, keys).astype(low)
-    qkv_ref[:, 2 * padded :] = jnp.where(extra, 1.0, projected[:, 2 * padded :]).astype(low)
-
-
-def front(width, x, norms, wq, bq, table):
-    rows, d = x.shape
-    full = lambda a: pl.BlockSpec(a.shape, lambda r: (0,) * a.ndim)
-    block = lambda w: pl.BlockSpec((BLOCK, w), lambda r: (r, 0))
+MESH = pl.DeviceIdType.MESH
+
+
+class Place:
+    def __init__(self):
+        self.dp, self.t = lax.axis_index("dp"), lax.axis_index("tensor")
+        self.n, self.ways = lax.axis_size("dp"), lax.axis_size("tensor")
+        self.majors = self.n // 2
+        self.a, self.b = self.dp // 2, self.dp % 2
+        self.chip, self.core = self.t // 2, self.t % 2
+        self.near = (self.dp, self.t + 1 - 2 * self.core)
+        self.across = (self.dp, (self.t + 2) % 4)
+        self.beside = (self.dp + 1 - 2 * self.b, self.t)
+
+    def major(self, k):
+        return ((self.a + k) % self.majors, (self.a + k) % self.majors * 2 + self.b)
+
+    def greet(self, everyone):
+        barrier = pltpu.get_barrier_semaphore()
+        others = [self.near, self.across]
+        if everyone:
+            others += [(self.dp, 3 - self.t)]
+            others += [((self.dp + k) % self.n, self.t) for k in range(1, self.n)]
+        else:
+            others += [self.beside]
+            others += [(self.major(k)[1], self.t) for k in range(1, self.majors)]
+        for other in others:
+            pl.semaphore_signal(barrier, inc=1, device_id=other, device_id_type=MESH)
+        pl.semaphore_wait(barrier, len(others))
+
+
+def send(src, dst, sems, k, to):
+    return pltpu.make_async_remote_copy(
+        src_ref=src,
+        dst_ref=dst,
+        send_sem=sems.at[0, k],
+        recv_sem=sems.at[1, k],
+        device_id=to,
+        device_id_type=MESH,
+    )
+
+
+def plus(*terms):
+    return functools.reduce(jnp.add, [t.astype(f32) for t in terms])
+
+
+class Scatter:
+    def __init__(self, place, mine, got, mid, last, sems):
+        self.p, self.mine, self.got, self.mid, self.last = place, mine, got, mid, last
+        self.pairs, self.lines = sems
+
+    def first(self, k):
+        p = self.p
+        a = p.major(k)[0]
+        return send(
+            self.mine.at[a * 2 + 1 - p.b], self.got.at[k % p.majors], self.pairs, k % p.majors, p.beside
+        )
+
+    def second(self, k):
+        return send(
+            self.mid.at[k - 1], self.last.at[k - 1], self.lines, k - 1, (self.p.major(k)[1], self.p.t)
+        )
+
+    def start(self):
+        for k in range(1, self.p.majors + 1):
+            self.first(k).start()
+
+    def add(self, k):
+        self.first(k).wait_recv()
+        self.mid[k - 1] = plus(
+            self.mine[self.p.major(k)[1]], self.got[k % self.p.majors]
+        ).astype(self.mid.dtype)
+
+    def forward(self, k):
+        self.second(k).start()
+
+    def finish(self):
+        p = self.p
+        for k in range(1, p.majors + 1):
+            self.first(k).wait_send()
+        self.first(p.majors).wait_recv()
+        for k in range(1, p.majors):
+            self.second(k).wait()
+        return plus(
+            self.mine[p.dp], self.got[0], *[self.last[k] for k in range(p.majors - 1)]
+        )
+
+
+class Gather:
+    def __init__(self, place, mine, whole, sems):
+        self.p, self.mine, self.whole, self.lines, self.pairs = place, mine, whole, *sems
+
+    def line(self, k):
+        p = self.p
+        return send(self.mine, self.whole.at[p.dp], self.lines, k - 1, (p.major(k)[1], p.t))
+
+    def pair(self, k):
+        p = self.p
+        if k == 0:
+            return send(self.mine, self.whole.at[p.dp], self.pairs, 0, p.beside)
+        block = self.whole.at[p.major(p.majors - k)[1]]
+        return send(block, block, self.pairs, k, p.beside)
+
+    def start(self):
+        self.pair(0).start()
+        for k in range(1, self.p.majors):
+            self.line(k).start()
+
+    def forward(self, k):
+        self.line(k).wait_recv()
+        self.pair(k).start()
+
+    def arrived(self):
+        for k in range(self.p.majors):
+            self.pair(k).wait_recv()
+
+    def finish(self):
+        for k in range(self.p.majors):
+            self.pair(k).wait_send()
+        for k in range(1, self.p.majors):
+            self.line(k).wait_send()
+
+
+def gather_scratch(majors):
+    return [pltpu.SemaphoreType.DMA((2, majors - 1)), pltpu.SemaphoreType.DMA((2, majors))]
+
+
+class Rows:
+    def __init__(self, place, mine, whole, chunks, sems):
+        self.p, self.mine, self.whole, self.chunks, self.sems = place, mine, whole, chunks, sems
+        self.size = mine.shape[0] // chunks
+
+    def copy(self, kind, c):
+        p = self.p
+        at = pl.ds(c * self.size, self.size)
+        if kind == 2:
+            block = self.whole.at[p.across[1], at]
+            return send(block, block, self.sems, 2 * self.chunks + c, p.near)
+        to = p.near if kind == 0 else p.across
+        return send(self.mine.at[at], self.whole.at[p.t, at], self.sems, kind * self.chunks + c, to)
+
+    def start(self):
+        for c in range(self.chunks):
+            for kind in range(2):
+                self.copy(kind, c).start()
+
+    def arrived(self, kind, c):
+        self.copy(kind, c).wait_recv()
+
+    def forward(self, c):
+        self.copy(1, c).wait_recv()
+        self.copy(2, c).start()
+
+    def finish(self):
+        for c in range(self.chunks):
+            for kind in range(3):
+                self.copy(kind, c).wait_send()
+
+
+def rows_scratch(chunks):
+    return pltpu.SemaphoreType.DMA((2, 3 * chunks))
+
+
+class Exchange:
+    def __init__(self, slots, sems, me, count, device):
+        self.slots, self.sems, self.me, self.count, self.device = slots, sems, me, count, device
+
+    def copy(self, k, source):
+        return pltpu.make_async_remote_copy(
+            src_ref=self.slots.at[source],
+            dst_ref=self.slots.at[source],
+            send_sem=self.sems.at[0, k],
+            recv_sem=self.sems.at[1, source],
+            device_id=self.device((self.me + k) % self.count),
+            device_id_type=MESH,
+        )
+
+    def start(self):
+        for k in range(1, self.count):
+            self.copy(k, self.me).start()
+
+    def total(self):
+        for k in range(1, self.count):
+            self.copy(k, (self.me + k) % self.count).wait_recv()
+        return functools.reduce(jnp.add, [self.slots[k] for k in range(self.count)])
+
+    def finish(self):
+        for k in range(1, self.count):
+            self.copy(k, self.me).wait_send()
+
+
+def scatter_scratch(majors, rows, columns):
+    return [
+        pltpu.VMEM((majors, rows, columns), low),
+        pltpu.VMEM((majors - 1, rows, columns), low),
+        pltpu.VMEM((majors - 1, rows, columns), low),
+        pltpu.SemaphoreType.DMA((2, majors)),
+        pltpu.SemaphoreType.DMA((2, majors - 1)),
+    ]
+
+
+def flat(blocks_ref):
+    n, side, columns = blocks_ref.shape
+    if side % 16 == 0:
+        return blocks_ref[...].reshape(n * side, columns)
+    return jnp.concatenate([blocks_ref[k].astype(f32) for k in range(n)]).astype(low)
+
+
+def front_kernel(
+    width, x_ref, wq_ref, norm_ref, bq_ref, table_ref, first_out, second_out, qkv_out, wq_out,
+    x_all, wq_all, first_ref, second_ref, qkv_ref, x_sems, wq_lines, wq_pairs, own_sems, out_sems,
+):
+    padded = qkv_ref.shape[2] // 3
+    per = x_ref.shape[0] // BLOCK
+    here = Place()
+    here.greet(False)
+    rows = Rows(here, x_ref, x_all, per, x_sems)
+    weights = Gather(here, wq_ref, wq_all, (wq_lines, wq_pairs))
+    rows.start()
+    weights.start()
+    own = [
+        pltpu.make_async_copy(x_ref, x_all.at[here.t], own_sems.at[0]),
+        pltpu.make_async_copy(wq_ref, wq_all.at[here.dp], own_sems.at[1]),
+    ]
+    for copy in own:
+        copy.start()
+
+    def shard(kind):
+        return (here.chip + kind // 2) % 2 * 2 + (here.core + kind % 2) % 2
+
+    def out(ref, target, r, k):
+        at = pl.ds(pl.multiple_of(r * BLOCK, BLOCK), BLOCK)
+        return pltpu.make_async_copy(ref.at[r], target.at[at], out_sems.at[k, r])
+
+    def norm(kind, c):
+        x = x_all[shard(kind), pl.ds(pl.multiple_of(c * BLOCK, BLOCK), BLOCK), :].astype(f32)
+        shifted = x - jnp.mean(x, axis=1, keepdims=True)
+        inv_std = lax.rsqrt(jnp.mean(shifted * shifted, axis=1, keepdims=True) + EPS)
+        normed = shifted * inv_std
+        r = shard(kind) * per + c
+        first_ref[r] = (normed * norm_ref[0:1, :] + norm_ref[1:2, :]).astype(low)
+        second_ref[r] = (normed * norm_ref[2:3, :] + norm_ref[3:4, :]).astype(low)
+
+    def project(kind, c):
+        r = shard(kind) * per + c
+        projected = dot(first_ref[r], flat(wq_all), NN) + bq_ref[...]
+        tables = rotary_rows(table_ref, r)
+        lane = lax.broadcasted_iota(jnp.int32, (BLOCK, padded), 1)
+        extra = (lane >= width) & (lane < width + 3)
+        qkv_ref[r, :, :padded] = rotate(projected[:, :padded], tables, 1).astype(low)
+        keys = rotate(projected[:, padded : 2 * padded], tables, 1)
+        qkv_ref[r, :, padded : 2 * padded] = jnp.where(extra, 1.0, keys).astype(low)
+        values = projected[:, 2 * padded :]
+        qkv_ref[r, :, 2 * padded :] = jnp.where(extra, 1.0, values).astype(low)
+        out(first_ref, first_out, r, 0).start()
+        out(second_ref, second_out, r, 1).start()
+        out(qkv_ref, qkv_out, r, 2).start()
+
+    own[0].wait()
+
+    @pl.loop(0, per)
+    def _(c):
+        norm(0, c)
+
+    for c in range(per):
+        rows.arrived(0, c)
+
+    @pl.loop(0, per)
+    def _(c):
+        norm(1, c)
+
+    for c in range(per - 1):
+        rows.forward(c)
+        norm(2, c)
+    for k in range(1, here.majors):
+        weights.forward(k)
+    for c in range(per - 1):
+        rows.arrived(2, c)
+        norm(3, c)
+    own[1].wait()
+    weights.arrived()
+
+    @pl.loop(0, per)
+    def _(c):
+        project(0, c)
+
+    rows.forward(per - 1)
+
+    @pl.loop(0, per + 2 * (per - 1))
+    def _(number):
+        later = number // per
+        project(1 + later + number % per * later, number % per * (1 - later))
+
+    norm(2, per - 1)
+    project(2, per - 1)
+    rows.arrived(2, per - 1)
+    norm(3, per - 1)
+    project(3, per - 1)
+    copy = pltpu.make_async_copy(wq_all, wq_out, own_sems.at[2])
+    copy.start()
+    copy.wait()
+
+    @pl.loop(0, 4 * per)
+    def _(r):
+        out(first_ref, first_out, r, 0).wait()
+        out(second_ref, second_out, r, 1).wait()
+        out(qkv_ref, qkv_out, r, 2).wait()
+
+    rows.finish()
+    weights.finish()
+
+
+def front(width, x, wq, norms, bq, table):
+    local, d = x.shape
+    side, columns = wq.shape
+    n = lax.axis_size("dp")
+    ways = lax.axis_size("tensor")
+    rows = local * ways
+    blocks = rows // BLOCK
+    assert ways == 4 and local // BLOCK == 2
+    vmem = pl.BlockSpec(memory_space=pltpu.VMEM)
+    hbm = pl.BlockSpec(memory_space=pl.ANY)
     return pl.pallas_call(
         functools.partial(front_kernel, width),
         name="front",
-        grid=(rows // BLOCK,),
-        in_specs=[block(d), full(norms), full(wq), full(bq), full(table)],
-        out_specs=[block(d), block(d), block(wq.shape[1])],
+        in_specs=[vmem] * 5,
+        out_specs=[hbm] * 4,
         out_shape=[
             jax.ShapeDtypeStruct((rows, d), low),
             jax.ShapeDtypeStruct((rows, d), low),
-            jax.ShapeDtypeStruct((rows, wq.shape[1]), low),
+            jax.ShapeDtypeStruct((rows, columns), low),
+            jax.ShapeDtypeStruct((n, side, columns), low),
         ],
-        compiler_params=pltpu.CompilerParams(vmem_limit_bytes=VMEM),
-    )(x, norms, wq, bq, table)
-
-
-def attend_kernel(width, qkv_ref, context_ref, qx_ref, vm_ref, scores_ref):
+        scratch_shapes=[
+            pltpu.VMEM((ways, local, d), low),
+            pltpu.VMEM((n, side, columns), low),
+            pltpu.VMEM((blocks, BLOCK, d), low),
+            pltpu.VMEM((blocks, BLOCK, d), low),
+            pltpu.VMEM((blocks, BLOCK, columns), low),
+            rows_scratch(local // BLOCK),
+        ]
+        + gather_scratch(n // 2)
+        + [pltpu.SemaphoreType.DMA((3,)), pltpu.SemaphoreType.DMA((3, blocks))],
+        compiler_params=pltpu.CompilerParams(
+            vmem_limit_bytes=VMEM, collective_id=0, has_side_effects=True
+        ),
+    )(x, wq, norms, bq, table)
+
+
+def attend_kernel(
+    width, qkv_ref, wi_ref, wd_ref, cot_ref, context_ref, qx_ref, wi_out, wd_out, cot_out,
+    vm_ref, scores_ref, cot_sems, wi_lines, wi_pairs, wd_lines, wd_pairs, own_sems,
+):
     heads = width // HD
     rows = qkv_ref.shape[0]
     padded = qkv_ref.shape[1] // 3
@@ -132,9 +446,25 @@
     step = pl.program_id(0)
     lane = lax.broadcasted_iota(jnp.int32, (BLOCK, padded), 1)
     of_head = [(lane >= h * HD) & (lane < (h + 1) * HD) for h in range(heads)]
+    here = Place()
+    cots = Rows(here, cot_ref, cot_out, 2, cot_sems)
+    inner = Gather(here, wi_ref, wi_out, (wi_lines, wi_pairs))
+    down = Gather(here, wd_ref, wd_out, (wd_lines, wd_pairs))
+    copies = [
+        pltpu.make_async_copy(wi_ref, wi_out.at[here.dp], own_sems.at[0]),
+        pltpu.make_async_copy(wd_ref, wd_out.at[here.dp], own_sems.at[1]),
+        pltpu.make_async_copy(cot_ref, cot_out.at[here.t], own_sems.at[2]),
+    ]
 
     @pl.when(step == 0)
     def _():
+        here.greet(False)
+        inner.start()
+        down.start()
+        cots.start()
+        for copy in copies:
+            copy.start()
+
         @pl.loop(0, blocks)
         def _(j):
             v = qkv_ref[pl.ds(pl.multiple_of(j * BLOCK, BLOCK), BLOCK), 2 * padded :].astype(f32)
@@ -142,6 +472,22 @@
                 vm_ref[j, h * BLOCK : (h + 1) * BLOCK, :] = jnp.where(
                     of_head[h], v, jnp.where(lane == width + h, 1.0, 0.0)
                 ).astype(low)
+
+    for k in range(1, here.majors):
+
+        @pl.when(step == blocks - 3)
+        def _():
+            inner.forward(k)
+
+    @pl.when(step == blocks - 2)
+    def _():
+        cots.forward(0)
+
+    for k in range(1, here.majors - 1):
+
+        @pl.when(step == blocks - 1)
+        def _():
+            down.forward(k)
 
     q = qkv_ref[pl.ds(pl.multiple_of(step * BLOCK, BLOCK), BLOCK), :padded].astype(f32)
     query = jnp.concatenate([jnp.where(of_head[h], q, 0.0).astype(low) for h in range(heads)])
@@ -196,31 +542,64 @@
         qx_ref[0, h * BLOCK : (h + 1) * BLOCK, :] = extended.astype(low)
     context_ref[...] = (mixed * inverse).astype(low)
 
-
-def attend(width, qkv):
+    @pl.when(step == blocks - 1)
+    def _():
+        down.forward(here.majors - 1)
+        cots.forward(1)
+        for copy in copies:
+            copy.wait()
+        inner.arrived()
+        for c in range(2):
+            cots.arrived(0, c)
+            cots.arrived(2, c)
+        down.arrived()
+        inner.finish()
+        cots.finish()
+        down.finish()
+
+
+def attend(width, qkv, wi, wd, cot):
     rows = qkv.shape[0]
     padded = qkv.shape[1] // 3
     heads = width // HD
     blocks = rows // BLOCK
+    n = lax.axis_size("dp")
+    ways = lax.axis_size("tensor")
+    once = lambda a: pl.BlockSpec(
+        a.shape, lambda r: (0,) * len(a.shape), pipeline_mode=pl.Buffered(1)
+    )
+    hbm = pl.BlockSpec(memory_space=pl.ANY)
     return pl.pallas_call(
         functools.partial(attend_kernel, width),
         name="attend",
         grid=(blocks,),
-        in_specs=[pl.BlockSpec(qkv.shape, lambda r: (0, 0))],
+        in_specs=[once(qkv), once(wi), once(wd), once(cot)],
         out_specs=[
             pl.BlockSpec((BLOCK, padded), lambda r: (r, 0)),
             pl.BlockSpec((1, heads * BLOCK, padded), lambda r: (r, 0, 0)),
+            hbm,
+            hbm,
+            hbm,
         ],
         out_shape=[
             jax.ShapeDtypeStruct((rows, padded), low),
             jax.ShapeDtypeStruct((blocks, heads * BLOCK, padded), low),
+            jax.ShapeDtypeStruct((n,) + wi.shape, low),
+            jax.ShapeDtypeStruct((n,) + wd.shape, low),
+            jax.ShapeDtypeStruct((ways,) + cot.shape, low),
         ],
         scratch_shapes=[
             pltpu.VMEM((blocks, heads * BLOCK, padded), low),
             pltpu.VMEM((blocks, heads * BLOCK, BLOCK), f32),
-        ],
-        compiler_params=pltpu.CompilerParams(vmem_limit_bytes=VMEM),
-    )(qkv)
+            rows_scratch(2),
+        ]
+        + gather_scratch(n // 2)
+        + gather_scratch(n // 2)
+        + [pltpu.SemaphoreType.DMA((3,))],
+        compiler_params=pltpu.CompilerParams(
+            vmem_limit_bytes=VMEM, collective_id=1, has_side_effects=True
+        ),
+    )(qkv, wi, wd, cot)
 
 
 def feed_kernel(
@@ -316,132 +695,6 @@
         scratch_shapes=[pltpu.VMEM(wi.shape, f32), pltpu.VMEM(wd.shape, f32)],
         compiler_params=pltpu.CompilerParams(vmem_limit_bytes=VMEM),
     )(length, second, context, cot, wi, wd, bias, norms)
-
-
-MESH = pl.DeviceIdType.MESH
-
-
-class Place:
-    def __init__(self):
-        self.dp, self.t = lax.axis_index("dp"), lax.axis_index("tensor")
-        self.n, self.ways = lax.axis_size("dp"), lax.axis_size("tensor")
-        self.majors = self.n // 2
-        self.a, self.b = self.dp // 2, self.dp % 2
-        self.chip, self.core = self.t // 2, self.t % 2
-        self.near = (self.dp, self.t + 1 - 2 * self.core)
-        self.across = (self.dp, (self.t + 2) % 4)
-        self.beside = (self.dp + 1 - 2 * self.b, self.t)
-
-    def major(self, k):
-        return ((self.a + k) % self.majors, (self.a + k) % self.majors * 2 + self.b)
-
-    def greet(self, everyone):
-        barrier = pltpu.get_barrier_semaphore()
-        others = [self.near, self.across]
-        if everyone:
-            others += [(self.dp, 3 - self.t)]
-            others += [((self.dp + k) % self.n, self.t) for k in range(1, self.n)]
-        else:
-            others += [self.beside]
-            others += [(self.major(k)[1], self.t) for k in range(1, self.majors)]
-        for other in others:
-            pl.semaphore_signal(barrier, inc=1, device_id=other, device_id_type=MESH)
-        pl.semaphore_wait(barrier, len(others))
-
-
-def send(src, dst, sems, k, to):
-    return pltpu.make_async_remote_copy(
-        src_ref=src,
-        dst_ref=dst,
-        send_sem=sems.at[0, k],
-        recv_sem=sems.at[1, k],
-        device_id=to,
-        device_id_type=MESH,
-    )
-
-
-def plus(*terms):
-    return functools.reduce(jnp.add, [t.astype(f32) for t in terms])
-
-
-class Scatter:
-    def __init__(self, place, mine, got, mid, last, sems):
-        self.p, self.mine, self.got, self.mid, self.last = place, mine, got, mid, last
-        self.pairs, self.lines = sems
-
-    def first(self, k):
-        p = self.p
-        a = p.major(k)[0]
-        return send(
-            self.mine.at[a * 2 + 1 - p.b], self.got.at[k % p.majors], self.pairs, k % p.majors, p.beside
-        )
-
-    def second(self, k):
-        return send(
-            self.mid.at[k - 1], self.last.at[k - 1], self.lines, k - 1, (self.p.major(k)[1], self.p.t)
-        )
-
-    def start(self):
-        for k in range(1, self.p.majors + 1):
-            self.first(k).start()
-
-    def add(self, k):
-        self.first(k).wait_recv()
-        self.mid[k - 1] = plus(
-            self.mine[self.p.major(k)[1]], self.got[k % self.p.majors]
-        ).astype(self.mid.dtype)
-
-    def forward(self, k):
-        self.second(k).start()
-
-    def finish(self):
-        p = self.p
-        for k in range(1, p.majors + 1):
-            self.first(k).wait_send()
-        self.first(p.majors).wait_recv()
-        for k in range(1, p.majors):
-            self.second(k).wait()
-        return plus(
-            self.mine[p.dp], self.got[0], *[self.last[k] for k in range(p.majors - 1)]
-        )
-
-
-class Exchange:
-    def __init__(self, slots, sems, me, count, device):
-        self.slots, self.sems, self.me, self.count, self.device = slots, sems, me, count, device
-
-    def copy(self, k, source):
-        return pltpu.make_async_remote_copy(
-            src_ref=self.slots.at[source],
-            dst_ref=self.slots.at[source],
-            send_sem=self.sems.at[0, k],
-            recv_sem=self.sems.at[1, source],
-            device_id=self.device((self.me + k) % self.count),
-            device_id_type=MESH,
-        )
-
-    def start(self):
-        for k in range(1, self.count):
-            self.copy(k, self.me).start()
-
-    def total(self):
-        for k in range(1, self.count):
-            self.copy(k, (self.me + k) % self.count).wait_recv()
-        return functools.reduce(jnp.add, [self.slots[k] for k in range(self.count)])
-
-    def finish(self):
-        for k in range(1, self.count):
-            self.copy(k, self.me).wait_send()
-
-
-def scatter_scratch(majors, rows, columns):
-    return [
-        pltpu.VMEM((majors, rows, columns), low),
-        pltpu.VMEM((majors - 1, rows, columns), low),
-        pltpu.VMEM((majors - 1, rows, columns), low),
-        pltpu.SemaphoreType.DMA((2, majors)),
-        pltpu.SemaphoreType.DMA((2, majors - 1)),
-    ]
 
 
 def back_kernel(
@@ -769,22 +1022,19 @@
     assert local_rows * lax.axis_size("tensor") == LMAX and seq_lengths.shape[0] == 1
     hidden = w_in.shape[1]
 
-    gather = lambda a, axis: lax.all_gather(a, axis, axis=0, tiled=True)
     wq = jnp.pad(w_qkv, ((0, 0), (0, 0), (0, extra))).reshape(-1, 3 * padded)
     bq = jnp.pad(b_qkv, ((0, 0), (0, extra))).reshape(1, 3 * padded)
     wd = jnp.concatenate([w_down.T, jnp.pad(w_attn_out.T, ((0, 0), (0, extra)))], axis=1)
     norms = jnp.stack([norm1_gain, norm1_bias, norm2_gain, norm2_bias, b_out, b_down])
     table = jnp.asarray(rotary_base())
 
-    x_full = gather(tokens, "tensor")
-    wq_full = gather(wq, "dp")
-    cot_full = gather(cotangent, "tensor")
-    wi_full, wd_full = gather(w_in, "dp"), gather(wd, "dp")
-
-    first, second, qkv = front(width, x_full, norms, wq_full, bq, table)
-    context, qx = attend(width, qkv)
+    first, second, qkv, wq_full = front(width, tokens, wq, norms, bq, table)
+    context, qx, wi_full, wd_full, cot_full = attend(width, qkv, w_in, wd, cotangent)
+    merge = lambda a: a.reshape(-1, a.shape[-1])
+    wq_full, wi_full, wd_full = merge(wq_full), merge(wi_full), merge(wd_full)
     branch, dox, part, gw, gb_in, gpart = feed(
-        width, seq_lengths, second, context, cot_full, wi_full, wd_full, b_in.reshape(1, -1), norms
+        width, seq_lengths, second, context, merge(cot_full), wi_full, wd_full,
+        b_in.reshape(1, -1), norms,
     )
     output, grad_x, gq, gb_qkv, g_out, g_in, gb_in, g_down, small = back(
         width, seq_lengths, qkv, qx, dox, first, part, wq_full, norms, table, branch, gw, gb_in, gpart,

time: 327 us -> 215 us (0.66)
  waiting for transfers between devices: 147 us -> 0 us
  Pallas kernels: 146 us -> 189 us
  between operations: 14.7 us -> 1.36 us
  local copies, waits for them, and re-layouts: 14.8 us -> 20.3 us
    all_gather x5 -> x0, waiting for transfers between devices: 145 us -> none  [per_device(): gather = lambda a, axis: lax.all_gather(a, axis, axis=0, tiled=True)]
    pallas_call x1, Pallas kernels: 10.1 us -> 35.2 us  [front(): pl.pallas_call(functools.partial(front_kernel, width), name='front', in_s...]
    pallas_call x1, Pallas kernels: 29.1 us -> 43.1 us  [attend(): pl.pallas_call(functools.partial(attend_kernel, width), name='attend', gr...]
    pallas_call x1, Pallas kernels: 80.2 us -> 84.5 us  [back(): pl.pallas_call(functools.partial(back_kernel, width, hidden), name='back'...]
    another operation x7, local copies, waits for them, and re-layouts: 0.66 us -> 4.77 us  [per_device(): jnp.stack([norm1_gain, norm1_bias, norm2_gain, norm2_bias, b_out, b_down])]
    unnamed x36 -> x20, local copies, waits for them, and re-layouts: 11.8 us -> 12.4 us
  transfers between devices with their start and end apart: 5 -> 0, of which waited for: 5 -> 0; matrix products, arithmetic and copies ran while one was open for 1% -> 0% of each run, Pallas kernels for 12% -> 0%
where the time goes in v3:
time: 215 us
  Pallas kernels  189 us (88%)
  local copies, waits for them, and re-layouts  20.3 us (9%)
  other arithmetic  3.7 us (2%)
    pallas_call x1, Pallas kernels, back(): pl.pallas_call(functools.partial(back_kernel, width, hidden), name='back'...  84.5 us
    pallas_call x1, Pallas kernels, attend(): pl.pallas_call(functools.partial(attend_kernel, width), name='attend', gr...  43.1 us
    pallas_call x1, Pallas kernels, front(): pl.pallas_call(functools.partial(front_kernel, width), name='front', in_s...  35.2 us
    pallas_call x1, Pallas kernels, feed(): pl.pallas_call(functools.partial(feed_kernel, width), name='feed', grid=(...  26.4 us
    unnamed x20, local copies, waits for them, and re-layouts  12.4 us
    another operation x7, local copies, waits for them, and re-layouts, per_device(): jnp.stack([norm1_gain, norm1_bias, norm2_gain, norm2_bias, b_out, b_down])  4.77 us

profile of v3, /device:TPU:0, one launch (start us, length us, event | category | flops | bytes accessed | tf_op | source)
XLA Modules:
  0.0 214.5 jit_solution(17838587596289327063)
XLA Ops:
  1.3 0.7 stack.21
  2.0 0.7 stack.22
  2.7 0.7 stack.23
  3.4 0.7 stack.24
  4.0 1.3 reshape.53.bias_ref
  5.3 0.7 stack.25
  6.0 0.7 stack.26
  6.7 0.7 pad_bitcast_fusion
  7.4 0.6 copy.36
  8.0 0.6 stack.27.norm_ref
  8.6 0.9 copy.30
  9.5 1.6 fusion.1.wd_ref
  11.1 1.0 copy.34
  12.2 0.1 pad.12.clone
  12.3 0.7 copy.35
  12.9 35.2 %front.1 = (bf16[2048,768]{1,0:T(8,128)(2,1)}, bf16[2048,768]{1,0:T(8,128)(2,1)}, bf16[2048,768]{1,0:T(8,128)(2,1)}, bf16[8,96,768]{2,1,0:T(8,128)(2,1)}) custom-call(bf16[512,768]{1,0:T(8,128)(2,1)} %tokens_ref.1, bf16[96,768]{1,0:T(8,128)(2,1)} %bitcast.20, f32[6,768]{1,0:T(8,128)} %stack.27.norm_ref, f32[1,768]{1,0:T(1,128)} %bitcast.23, ...), custom_call_target="tpu_custom_call" | custom-call | tf_op jit(solution)/shard_map/front/pallas_call | solution.py:410
  48.1 43.1 %attend.1 = (bf16[2048,256]{1,0:T(8,128)(2,1)}, bf16[8,768,256]{2,1,0:T(8,128)(2,1)}, bf16[8,96,768]{2,1,0:T(8,128)(2,1)}, bf16[8,96,1024]{2,1,0:T(8,128)(2,1)}, bf16[4,512,768]{2,1,0:T(8,128)(2,1)}) custom-call(bf16[2048,768]{1,0:T(8,128)(2,1)} %get-tuple-element.33.qkv_ref, bf16[96,768]{1,0:T(8,128)(2,1)} %wi_ref.1, bf16[96,1024]{1,0:T(8,128)(2,1)} %fusion.1.wd_ref, ...), custom_call_target="tpu_custom_call" | custom-call | tf_op jit(solution)/shard_map/attend/pallas_call | solution.py:572
  91.2 26.4 %feed.1 = (bf16[2048,768]{1,0:T(8,128)(2,1)}, bf16[8,768,256]{2,1,0:T(8,128)(2,1)}, bf16[2048,768]{1,0:T(8,128)(2,1)}, bf16[8,96,1792]{2,1,0:T(8,128)(2,1)}, f32[1,768]{1,0:T(1,128)}, /*index=5*/f32[8,768]{1,0:T(8,128)}) custom-call(s32[1]{0:T(128)S(6)} %copy.42.length_ref, bf16[2048,768]{1,0:T(8,128)(2,1)} %get-tuple-element.35.second_ref, ...), custom_call_target="tpu_custom_call" | custom-call | tf_op jit(solution)/shard_map/feed/pallas_call | solution.py:681
  117.6 84.5 %back.1 = (f32[512,768]{1,0:T(8,128)}, f32[512,768]{1,0:T(8,128)}, f32[96,576]{1,0:T(8,128)}, f32[1,768]{1,0:T(1,128)}, f32[192,96]{1,0:T(8,128)}, /*index=5*/f3...) custom-call(s32[1]{0:T(128)S(6)} %copy.42.length_ref, ...), custom_call_target="tpu_custom_call" | custom-call | tf_op jit(solution)/shard_map/back/pallas_call | solution.py:971
  202.2 0.0 copy-start
  202.2 0.8 reduce
  203.0 0.6 reshape.56
  203.6 1.3 reduce.1
  204.9 1.1 copy.31
  206.0 0.9 copy.32
  206.8 1.9 copy.33
  208.7 0.0 copy-start.2
  208.7 0.0 copy-start.1
  208.7 0.0 copy-start.3
  208.7 2.7 %copy.43 = f32[512,768]{1,0:T(8,128)} copy(f32[512,768]{1,0:T(8,128)} %get-tuple-element.84) | data formatting | bytes 3145728
  211.4 0.0 copy-done
  211.4 1.1 copy.44
  212.6 0.0 copy-done.2
  212.6 0.6 copy.45
  213.2 0.0 copy-done.1
  213.2 0.7 copy.46
  213.9 0.0 copy-done.3
  213.9 0.6 copy.47
Async XLA Ops:
  202.2 9.3 %copy-start = (f32[512,768]{1,0:T(8,128)S(1)}, f32[512,768]{1,0:T(8,128)}, u32[]{:S(2)}) copy-start(f32[512,768]{1,0:T(8,128)} %get-tuple-element.85) | copy-start | bytes 4718596
  208.7 3.9 %copy-start.2 = (f32[192,96]{1,0:T(8,128)S(1)}, f32[192,96]{1,0:T(8,128)}, u32[]{:S(2)}) copy-start(f32[192,96]{1,0:T(8,128)} %get-tuple-element.88) | copy-start | bytes 221188
  208.7 4.5 %copy-start.1 = (f32[96,768]{1,0:T(8,128)S(1)}, f32[96,768]{1,0:T(8,128)}, u32[]{:S(2)}) copy-start(f32[96,768]{1,0:T(8,128)} %get-tuple-element.89) | copy-start | bytes 884740
  208.7 5.2 %copy-start.3 = (f32[5,768]{1,0:T(8,128)S(1)}, f32[5,768]{1,0:T(8,128)}, u32[]{:S(2)}) copy-start(f32[5,768]{1,0:T(8,128)} %get-tuple-element.92) | copy-start | bytes 46084

commit v4 on v1

v4 whole, which is shorter than its diff:
```python
import functools
import math

import jax
import jax.numpy as jnp
import numpy as np
from jax import lax
from jax.experimental import pallas as pl
from jax.experimental.pallas import tpu as pltpu
from jax.sharding import PartitionSpec as P

HD = 64
ROT = 16
LMAX = 2048
LANES = 128
EPS = 1e-05
BLOCK = 256
FAST = 64
VMEM = 66 * 1024 * 1024

f32 = jnp.float32
low = jnp.bfloat16

NN = (((1,), (0,)), ((), ()))
NT = (((1,), (1,)), ((), ()))
TN = (((0,), (0,)), ((), ()))


def dot(a, b, dims):
    return lax.dot_general(a, b, dims, preferred_element_type=f32)


def round_up(n, m):
    return (n + m - 1) // m * m


def rotary_base():
    d = np.arange(LANES) % HD
    half = ROT // 2
    inverse = np.where(d < ROT, np.exp((d % half) * (-2.0 * math.log(10000.0) / ROT)), 0.0)
    slow = np.arange(0, LMAX, FAST)[:, None] * inverse
    fast = np.arange(FAST)[:, None] * inverse
    return np.concatenate([np.cos(slow), np.sin(slow), np.cos(fast), np.sin(fast)]).astype(
        np.float32
    )


def rotary_rows(table_ref, block):
    slow_rows = LMAX // FAST
    fast_cos = table_ref[2 * slow_rows : 2 * slow_rows + FAST, :]
    fast_sin = table_ref[2 * slow_rows + FAST :, :]
    cosines, sines = [], []
    for part in range(BLOCK // FAST):
        row = block * (BLOCK // FAST) + part
        slow_cos = table_ref[pl.ds(row, 1), :]
        slow_sin = table_ref[pl.ds(row + slow_rows, 1), :]
        cosines.append(slow_cos * fast_cos - slow_sin * fast_sin)
        sines.append(slow_sin * fast_cos + slow_cos * fast_sin)
    cosine, sine = jnp.concatenate(cosines), jnp.concatenate(sines)
    d = lax.broadcasted_iota(jnp.int32, cosine.shape, 1) % HD
    return (
        cosine,
        jnp.where(d < ROT // 2, -sine, 0.0),
        jnp.where((d >= ROT // 2) & (d < ROT), sine, 0.0),
    )


def rotate(values, tables, sign):
    cosine, from_right, from_left = tables
    half = ROT // 2
    turned = []
    for first in range(0, values.shape[1], LANES):
        t = values[:, first : first + LANES]
        side = (
            pltpu.roll(t, LANES - half, axis=1) * from_right
            + pltpu.roll(t, half, axis=1) * from_left
        )
        turned.append(t * cosine + side if sign > 0 else t * cosine - side)
    return jnp.concatenate(turned, axis=1)


def three_terms(value):
    first = value.astype(low).astype(f32)
    second = (value - first).astype(low).astype(f32)
    return first, second, value - first - second


MESH = pl.DeviceIdType.MESH


class Place:
    def __init__(self):
        self.dp, self.t = lax.axis_index("dp"), lax.axis_index("tensor")
        self.n, self.ways = lax.axis_size("dp"), lax.axis_size("tensor")
        self.majors = self.n // 2
        self.a, self.b = self.dp // 2, self.dp % 2
        self.chip, self.core = self.t // 2, self.t % 2
        self.upper = self.a * 2 // self.majors
        self.near = (self.dp, self.t + 1 - 2 * self.core)
        self.across = (self.dp, (self.t + 2) % 4)
        self.beside = (self.dp + 1 - 2 * self.b, self.t)

    def major(self, k):
        return ((self.a + k) % self.majors, (self.a + k) % self.majors * 2 + self.b)

    def shard(self, kind):
        return (self.chip + kind // 2) % 2 * 2 + (self.core + kind % 2) % 2

    def greet(self):
        barrier = pltpu.get_barrier_semaphore()
        others = [self.near, self.across, (self.dp, 3 - self.t)]
        others += [((self.dp + k) % self.n, self.t) for k in range(1, self.n)]
        for other in others:
            pl.semaphore_signal(barrier, inc=1, device_id=other, device_id_type=MESH)
        pl.semaphore_wait(barrier, len(others))


def send(src, dst, sems, k, to):
    return pltpu.make_async_remote_copy(
        src_ref=src,
        dst_ref=dst,
        send_sem=sems.at[0, k],
        recv_sem=sems.at[1, k],
        device_id=to,
        device_id_type=MESH,
    )


def plus(*terms):
    return functools.reduce(jnp.add, [t.astype(f32) for t in terms])


class Scatter:
    def __init__(self, place, mine, got, last, sems):
        self.p, self.mine, self.got, self.last, self.pairs, self.lines = place, mine, got, last, *sems

    def first(self, k):
        p = self.p
        mine = self.mine.at[p.major(k)[0] * 2 + 1 - p.b]
        return send(mine, self.got.at[k % p.majors], self.pairs, k % p.majors, p.beside)

    def second(self, k):
        to = (self.p.major(k)[1], self.p.t)
        return send(self.got.at[k], self.last.at[k - 1], self.lines, k - 1, to)

    def start(self):
        for k in range(1, self.p.majors + 1):
            self.first(k).start()

    def add(self, k):
        self.first(k).wait_recv()
        self.got[k] = plus(self.mine[self.p.major(k)[1]], self.got[k]).astype(self.got.dtype)

    def forward(self, k):
        self.second(k).start()

    def finish(self):
        p = self.p
        for k in range(1, p.majors + 1):
            self.first(k).wait_send()
        self.first(p.majors).wait_recv()
        for k in range(1, p.majors):
            self.second(k).wait()
        return plus(self.mine[p.dp], self.got[0], *[self.last[k] for k in range(p.majors - 1)])


class Gather:
    def __init__(self, place, mine, whole, sems):
        self.p, self.mine, self.whole, self.lines, self.pairs = place, mine, whole, *sems

    def line(self, k):
        p = self.p
        return send(self.mine, self.whole.at[p.dp], self.lines, k - 1, (p.major(k)[1], p.t))

    def pair(self, k):
        block = self.whole.at[self.p.major(self.p.majors - k)[1]]
        return send(block, block, self.pairs, k, self.p.beside)

    def own_pair(self):
        return send(self.mine, self.whole.at[self.p.dp], self.pairs, 0, self.p.beside)

    def start(self):
        p = self.p
        for k in range(1, p.majors):
            self.line(k + p.upper * (p.majors - 2 * k)).start()

    def forward(self, number):
        p = self.p
        k = p.majors - number + p.upper * (2 * number - p.majors)
        self.line(k).wait_recv()
        self.pair(k).start()

    def arrived(self):
        self.own_pair().wait_recv()
        for k in range(1, self.p.majors):
            self.pair(k).wait_recv()

    def finish(self):
        self.own_pair().wait_send()
        for k in range(1, self.p.majors):
            self.pair(k).wait_send()
            self.line(k).wait_send()


def gather_scratch(majors):
    return [pltpu.SemaphoreType.DMA((2, majors - 1)), pltpu.SemaphoreType.DMA((2, majors))]


class Rows:
    def __init__(self, place, mine, whole, sems):
        self.p, self.mine, self.whole, self.sems = place, mine, whole, sems
        self.per = mine.shape[0] // BLOCK

    def copy(self, kind, c):
        p = self.p
        if kind == 2:
            block = self.whole.at[p.across[1] * self.per + c]
            return send(block, block, self.sems, 2 * self.per + c, p.near)
        to = p.near if kind == 0 else p.across
        mine = self.mine.at[pl.ds(c * BLOCK, BLOCK)]
        return send(mine, self.whole.at[p.t * self.per + c], self.sems, kind * self.per + c, to)

    def start(self):
        for c in range(self.per):
            for kind in range(2):
                self.copy(kind, c).start()

    def arrived(self, kind, c):
        self.copy(kind, c).wait_recv()

    def forward(self, c):
        self.copy(1, c).wait_recv()
        self.copy(2, c).start()

    def released(self):
        for c in range(self.per):
            self.copy(2, c).wait_send()

    def finish(self):
        for c in range(self.per):
            for kind in range(2):
                self.copy(kind, c).wait_send()


class Exchange:
    def __init__(self, slots, sems, me, count, device):
        self.slots, self.sems, self.me, self.count, self.device = slots, sems, me, count, device

    def copy(self, k, source):
        return pltpu.make_async_remote_copy(
            src_ref=self.slots.at[source],
            dst_ref=self.slots.at[source],
            send_sem=self.sems.at[0, k],
            recv_sem=self.sems.at[1, source],
            device_id=self.device((self.me + k) % self.count),
            device_id_type=MESH,
        )

    def start(self):
        for k in range(1, self.count):
            self.copy(k, self.me).start()

    def total(self):
        for k in range(1, self.count):
            self.copy(k, (self.me + k) % self.count).wait_recv()
        return functools.reduce(jnp.add, [self.slots[k] for k in range(self.count)])

    def finish(self):
        for k in range(1, self.count):
            self.copy(k, self.me).wait_send()


def scatter_scratch(majors, rows, columns):
    return [
        pltpu.VMEM((majors, rows, columns), low),
        pltpu.VMEM((majors - 1, rows, columns), low),
        pltpu.SemaphoreType.DMA((2, majors)),
        pltpu.SemaphoreType.DMA((2, majors - 1)),
    ]


def flat(blocks_ref):
    n, side, columns = blocks_ref.shape
    if side % 16 == 0:
        return blocks_ref[...].reshape(n * side, columns)
    return jnp.concatenate([blocks_ref[k].astype(f32) for k in range(n)]).astype(low)


def norm_rows(x):
    shifted = x - jnp.mean(x, axis=1, keepdims=True)
    inv_std = lax.rsqrt(jnp.mean(shifted * shifted, axis=1, keepdims=True) + EPS)
    return shifted * inv_std, inv_std


def layer_kernel(
    length_ref, tokens_ref, cot_ref, g1_ref, b1_ref, g2_ref, b2_ref, wq_ref, bq_ref, wo_ref, wi_ref,
    bi_ref, wd_ref, bo_ref, bd_ref, table_ref,
    out_out, gx_out, gq_ref, gbq_ref, go_ref, gi_ref, gb_ref, gd_ref, small_ref,
    norm_ref, bias_ref, wq_mine, wd_mine, wq_all, wi_all, wd_all,
    x_all, first_ref, second_ref, cot_all, qkv_ref, qx_ref, vm_ref, context_ref, pool_ref,
    keyt_ref, gwi_sum, gwd_sum, gb_sum, gs_sum, gw_ref, own_sems, out_sems, x_sems, cot_sems,
    wq_lines, wq_pairs, wi_lines, wi_pairs, wd_lines, wd_pairs,
    gn_near, gn_own, gn_far, gn_sem1, gn_sem2,
    br_near, br_far, br_sem1, br_sem2,
    w_got, w_last, w_sem1, w_sem2,
    gq_low, q_got, q_last, q_sem1, q_sem2,
    line_ref, cross_ref, line_sem, cross_sem,
):
    here = Place()
    blocks, _, d = x_all.shape
    local = tokens_ref.shape[0]
    per = local // BLOCK
    width = wq_ref.shape[2]
    heads = width // HD
    padded = qkv_ref.shape[2] // 3
    hidden = wi_ref.shape[1]
    side = wi_ref.shape[0]
    scale = HD ** (-0.5)
    lane = lax.broadcasted_iota(jnp.int32, (BLOCK, padded), 1)
    of_head = [(lane >= h * HD) & (lane < (h + 1) * HD) for h in range(heads)]
    inside = lane < width
    extra = (lane >= width) & (lane < width + 3)

    rows = Rows(here, tokens_ref, x_all, x_sems)
    cots = Rows(here, cot_ref, cot_all, cot_sems)
    proj_w = Gather(here, wq_mine, wq_all, (wq_lines, wq_pairs))
    in_w = Gather(here, wi_ref, wi_all, (wi_lines, wi_pairs))
    down_w = Gather(here, wd_mine, wd_all, (wd_lines, wd_pairs))

    wq_mine[...] = jnp.zeros_like(wq_mine)
    wd_mine[:, hidden:] = jnp.zeros((side, padded), low)
    bias_ref[...] = jnp.zeros_like(bias_ref)
    for k in range(3):
        wq_mine[:, k * padded : k * padded + width] = wq_ref[k]
        bias_ref[0:1, k * padded : k * padded + width] = bq_ref[k : k + 1, :]
    wd_mine[:, :hidden] = wd_ref[...]
    wd_mine[:, hidden : hidden + width] = wo_ref[...].astype(f32).T.astype(low)
    for k, ref in enumerate((g1_ref, b1_ref, g2_ref, b2_ref, bo_ref, bd_ref, bi_ref)):
        norm_ref[k, :] = ref[...]

    here.greet()
    proj_w.start()
    proj_w.own_pair().start()
    rows.start()
    in_w.start()
    down_w.start()
    own = [
        pltpu.make_async_copy(tokens_ref.at[pl.ds(c * BLOCK, BLOCK)], x_all.at[here.t * per + c], own_sems.at[c])
        for c in range(per)
    ]
    own += [
        pltpu.make_async_copy(cot_ref.at[pl.ds(c * BLOCK, BLOCK)], cot_all.at[here.t * per + c], own_sems.at[per + c])
        for c in range(per)
    ]
    own += [
        pltpu.make_async_copy(mine, whole.at[here.dp], own_sems.at[2 * per + k])
        for k, (mine, whole) in enumerate(((wq_mine, wq_all), (wi_ref, wi_all), (wd_mine, wd_all)))
    ]
    for copy in own:
        copy.start()

    def norm(kind, c):
        r = here.shard(kind) * per + c
        normed, _ = norm_rows(x_all[r].astype(f32))
        first_ref[r] = (normed * norm_ref[0:1, :] + norm_ref[1:2, :]).astype(low)
        second_ref[r] = (normed * norm_ref[2:3, :] + norm_ref[3:4, :]).astype(low)

    def project(kind, c):
        r = here.shard(kind) * per + c
        projected = dot(first_ref[r], flat(wq_all), NN) + bias_ref[...]
        tables = rotary_rows(table_ref, r)
        qkv_ref[r, :, :padded] = rotate(projected[:, :padded], tables, 1).astype(low)
        keys = rotate(projected[:, padded : 2 * padded], tables, 1)
        keys = jnp.where(extra, 1.0, keys)
        keyt_ref[r] = keys.T[:width].astype(low)
        qkv_ref[r, :, padded : 2 * padded] = keys.astype(low)
        values = projected[:, 2 * padded :]
        qkv_ref[r, :, 2 * padded :] = jnp.where(extra, 1.0, values).astype(low)
        for h in range(heads):
            vm_ref[r, h * BLOCK : (h + 1) * BLOCK, :] = jnp.where(
                of_head[h], values, jnp.where(lane == width + h, 1.0, 0.0)
            ).astype(low)

    for c in range(per):
        own[c].wait()

    @pl.loop(0, per)
    def _(c):
        norm(0, c)

    for c in range(per):
        rows.arrived(0, c)
    proj_w.forward(1)

    @pl.loop(0, per)
    def _(c):
        norm(1, c)

    for k in range(2, here.majors - 1):
        proj_w.forward(k)
    for c in range(per - 1):
        rows.forward(c)
    proj_w.forward(here.majors - 1)
    in_w.own_pair().start()
    down_w.own_pair().start()
    cots.start()
    for c in range(per - 1):
        norm(2, c)
    for c in range(per - 1):
        rows.arrived(2, c)
        norm(3, c)
    own[2 * per].wait()
    proj_w.arrived()

    @pl.loop(0, per + 2 * (per - 1))
    def _(number):
        @pl.when(number == per + 1)
        def _():
            rows.forward(per - 1)

        later = number // per
        project(1 + later + number % per * later, number % per * (1 - later))

    @pl.loop(0, per)
    def _(c):
        project(0, c)

    norm(2, per - 1)
    project(2, per - 1)
    rows.arrived(2, per - 1)
    norm(3, per - 1)
    project(3, per - 1)

    @pl.loop(0, blocks)
    def _(i):
        for k in range(1, here.majors):

            @pl.when(i == min(blocks // 2 - 2 + k, blocks - 1))
            def _():
                in_w.forward(k)

        for c in range(per):

            @pl.when(i == blocks - per + c)
            def _():
                cots.forward(c)

        q = qkv_ref[i, :, :padded].astype(f32)
        for h in range(heads):
            qx_ref[i, h * BLOCK : (h + 1) * BLOCK, :] = jnp.where(of_head[h], q, 0.0).astype(low)
        query = qx_ref[i]

        def scores(j):
            return dot(query, qkv_ref[j, :, padded : 2 * padded], NT)

        def widest(s):
            return functools.reduce(
                jnp.maximum, [s[:, c : c + LANES] for c in range(0, BLOCK, LANES)]
            )

        diagonal = scores(i)
        row = lax.broadcasted_iota(jnp.int32, diagonal.shape, 0) % BLOCK
        col = lax.broadcasted_iota(jnp.int32, diagonal.shape, 1)
        diagonal = jnp.where(col <= row, diagonal, -1e30)

        def first_pass(j, top):
            s = scores(j)
            pool_ref[pl.ds(j * heads, heads)] = s.reshape(heads, BLOCK, BLOCK)
            return jnp.maximum(top, widest(s))

        top = lax.fori_loop(0, i, first_pass, widest(diagonal))
        top = jnp.max(top, axis=1, keepdims=True)

        def weigh(s, j):
            p = jnp.exp((s - top) * scale).astype(low)
            parts = [slice(h * BLOCK, (h + 1) * BLOCK) for h in range(heads)]
            return functools.reduce(jnp.add, [dot(p[at], vm_ref[j, at, :], NN) for at in parts])

        def second_pass(j, total):
            s = pool_ref[pl.ds(j * heads, heads)].reshape(heads * BLOCK, BLOCK)
            return total + weigh(s, j)

        mixed = lax.fori_loop(0, i, second_pass, weigh(diagonal, i))
        inverse = jnp.zeros((BLOCK, padded), f32)
        for h in range(heads):
            total = mixed[:, width + h : width + h + 1]
            inverse = jnp.where(of_head[h], 1.0 / total, inverse)
            log_total = top[h * BLOCK : (h + 1) * BLOCK] + jnp.log(total) / scale
            extended = jnp.where(of_head[h], q, 0.0)
            for k, term in enumerate(three_terms(-log_total)):
                extended = jnp.where(lane == width + k, term, extended)
            qx_ref[i, h * BLOCK : (h + 1) * BLOCK, :] = extended.astype(low)
        context_ref[i] = (mixed * inverse).astype(low)

    for k in range(1, here.majors):
        down_w.forward(k)
    for c in range(per):
        cots.arrived(0, c)
        cots.arrived(2, c)
    for copy in own[per : 2 * per] + own[2 * per + 1 :]:
        copy.wait()
    in_w.arrived()
    gwi_sum[...] = jnp.zeros_like(gwi_sum)
    gwd_sum[...] = jnp.zeros_like(gwd_sum)
    gb_sum[...] = jnp.zeros_like(gb_sum)
    gs_sum[...] = jnp.zeros_like(gs_sum)
    down_w.arrived()
    cots.released()
    rows.released()

    branch_ref, part_ref, dox_ref = cot_all, second_ref, vm_ref

    def near_branch(chip):
        owner = chip * 2 + 1 - here.core
        return send(
            branch_ref.at[pl.ds(owner * per, per)], br_near.at[chip], br_sem1, chip, here.near
        )

    def far_branch():
        return send(br_near.at[1 - here.chip], br_far, br_sem2, 0, here.across)

    @pl.loop(0, blocks)
    def _(number):
        r = here.shard(3 - number // per) * per + number % per

        @pl.when(number == per + 1)
        def _():
            near_branch(1 - here.chip).start()

        @pl.when(number == 2 * per + 1)
        def _():
            near_branch(1 - here.chip).wait_recv()

            @pl.loop(0, per)
            def _(c):
                mine = branch_ref[here.across[1] * per + c]
                br_near[1 - here.chip, c] = plus(mine, br_near[1 - here.chip, c]).astype(low)

        @pl.when(number == 3 * per + 1)
        def _():
            near_branch(here.chip).start()

        second = second_ref[r]
        context = context_ref[r]
        row = lax.broadcasted_iota(jnp.int32, second.shape, 0) + r * BLOCK
        grad = jnp.where(row < length_ref[0], cot_all[r].astype(f32), 0.0).astype(low)

        u = dot(second, flat(wi_all), NN) + norm_ref[6:7, :]
        cdf = 0.5 * (1.0 + lax.erf(u * (1.0 / math.sqrt(2.0))))
        act = (u * cdf).astype(low)
        slope = cdf + u * (jnp.exp(-0.5 * u * u) * (1.0 / math.sqrt(2.0 * math.pi)))
        both = jnp.concatenate([act, context], axis=1)
        back = dot(grad, flat(wd_all), NN)
        branch_ref[r] = dot(both, flat(wd_all), NT).astype(low)

        grad_hidden = back[:, :hidden] * slope
        gb_sum[1:2, :] += jnp.sum(grad_hidden, axis=0, keepdims=True)
        hidden_low = grad_hidden.astype(low)
        gwi_sum[...] += dot(second, hidden_low, TN)
        gwd_sum[...] += dot(grad, both, TN)

        @pl.when(number == 2 * per + 1)
        def _():
            far_branch().start()

        grad_context = back[:, hidden:].astype(low).astype(f32)
        product = grad_context * context.astype(f32)
        for h in range(heads):
            extended = jnp.where(of_head[h], grad_context, 0.0)
            delta = jnp.sum(jnp.where(of_head[h], product, 0.0), axis=1, keepdims=True)
            for k, term in enumerate(three_terms(-delta)):
                extended = jnp.where(lane == width + k, term, extended)
            dox_ref[r, h * BLOCK : (h + 1) * BLOCK, :] = extended.astype(low)

        part = dot(hidden_low, flat(wi_all), NT)
        gs_sum[2:3, :] += jnp.sum(part * second.astype(f32), axis=0, keepdims=True)
        gs_sum[3:4, :] += jnp.sum(part, axis=0, keepdims=True)
        part_ref[r] = (part * norm_ref[2:3, :]).astype(low)

    weights = Scatter(here, gw_ref, w_got, w_last, (w_sem1, w_sem2))
    final = Scatter(here, gq_low, q_got, q_last, (q_sem1, q_sem2))
    for block in range(here.n):
        rows_of = slice(block * side, (block + 1) * side)
        gw_ref[block, :, :hidden] = gwi_sum[rows_of, :].astype(low)
        gw_ref[block, :, hidden:] = gwd_sum[rows_of, :].astype(low)
    gwq_sum, gn_ref = gwi_sum, x_all
    gwq_sum[...] = jnp.zeros_like(gwq_sum)
    pool_ref[...] = jnp.zeros_like(pool_ref)
    weights.start()

    last = blocks - 1

    def block_of(number):
        return number // 2 + number % 2 * (last - number // 2 * 2)

    def slot_of(r):
        return r // per // 2 * per + r % per

    def near_block(r):
        return send(gn_ref.at[r], gn_near.at[slot_of(r)], gn_sem1, slot_of(r), here.near)

    def far_block(c):
        mine = gn_near.at[(1 - here.chip) * per + c]
        return send(mine, gn_far.at[c], gn_sem2, c, here.across)

    def hand_over(r):
        @pl.when(r // per % 2 != here.core)
        def _():
            near_block(r).start()

    def collect(r):
        owner = r // per

        @pl.when(owner % 2 == here.core)
        def _():
            near_block(r).wait_recv()
            total = plus(gn_ref[r], gn_near[slot_of(r)])

            @pl.when(owner // 2 == here.chip)
            def _():
                gn_own[r % per] = total

            @pl.when(owner // 2 != here.chip)
            def _():
                gn_near[slot_of(r)] = total.astype(low)

    def pass_on(r):
        owner = r // per

        @pl.when((owner % 2 == here.core) & (owner // 2 != here.chip))
        def _():
            far_block(r % per).start()

    def pair(i, j, own):
        keys, values = qkv_ref[j, :, padded : 2 * padded], qkv_ref[j, :, 2 * padded :]
        query, dout = qx_ref[i], dox_ref[i]
        p = jnp.exp(dot(keys, query, NT) * scale)
        if own:
            key_at = lax.broadcasted_iota(jnp.int32, p.shape, 0)
            query_at = lax.broadcasted_iota(jnp.int32, p.shape, 1) % BLOCK
            p = jnp.where(key_at <= query_at, p, 0.0)
        ds = (p * dot(values, dout, NT)).astype(low)
        pool_ref[blocks + j] += dot(p.astype(low), dout, NN)
        pool_ref[j] += dot(ds, query, NN)
        for h in range(heads):
            pool_ref[2 * blocks + i, h * HD : (h + 1) * HD, :] += dot(
                keyt_ref[j, h * HD : (h + 1) * HD, :], ds[:, h * BLOCK : (h + 1) * BLOCK], NN
            )

    def kept(c, values):
        row = lax.broadcasted_iota(jnp.int32, (BLOCK, d), 0) + (here.t * per + c) * BLOCK
        return jnp.where(row < length_ref[0], values, 0.0)

    def output_copy():
        return pltpu.make_async_copy(gwd_sum.at[:local, :d], out_out, out_sems.at[0])

    @pl.loop(0, blocks)
    def _(step):
        for k in range(1, here.majors):

            @pl.when(step == min(k, last - 2))
            def _():
                weights.add(k)

        @pl.when(step > 0)
        def _():
            hand_over(block_of(step - 1))

        turn = step // 2
        odd = step % 2
        now = block_of(step)
        pair(now, now, True)

        for k in range(1, here.majors):

            @pl.when(step == min(k, last - 2))
            def _():
                weights.forward(k)

        @pl.when(step > 0)
        def _():
            collect(block_of(step - 1))

        @pl.loop(0, last - step)
        def _(number):
            other = turn + 1 + number
            pair(other + odd * (last - turn - other), turn + odd * (other - turn), False)

        @pl.when(step == last // 2)
        def _():
            far_branch().wait()
            for chip in range(2):
                near_branch(chip).wait_send()
            near_branch(here.chip).wait_recv()

            @pl.loop(0, per)
            def _(c):
                total = plus(branch_ref[here.t * per + c], br_near[here.chip, c], br_far[c])
                total += norm_ref[4:5, :] + norm_ref[5:6, :]
                at = pl.ds(pl.multiple_of(c * BLOCK, BLOCK), BLOCK)
                gwd_sum[at, :d] = tokens_ref[at, :].astype(f32) + kept(c, total)

        tables = rotary_rows(table_ref, now)
        grad_query = jnp.concatenate(
            [
                pool_ref[2 * blocks + now, :width, :].T,
                jnp.zeros((BLOCK, padded - width), f32),
            ],
            axis=1,
        )
        projected = jnp.concatenate(
            [
                rotate(grad_query * scale, tables, -1),
                rotate(jnp.where(inside, pool_ref[now] * scale, 0.0), tables, -1),
                jnp.where(inside, pool_ref[blocks + now], 0.0),
            ],
            axis=1,
        )
        gb_sum[0:1, :] += jnp.sum(projected, axis=0, keepdims=True)
        proj_low = projected.astype(low)
        first = first_ref[now]
        gwq_sum[...] += dot(first, proj_low, TN)
        part = dot(proj_low, flat(wq_all), NT)
        gs_sum[0:1, :] += jnp.sum(part * first.astype(f32), axis=0, keepdims=True)
        gs_sum[1:2, :] += jnp.sum(part, axis=0, keepdims=True)
        gn_ref[now] = (part * norm_ref[0:1, :] + part_ref[now].astype(f32)).astype(low)

        @pl.when(step > 0)
        def _():
            pass_on(block_of(step - 1))

        @pl.when(step == last // 2)
        def _():
            output_copy().start()

    now = block_of(last)
    for block in range(here.n):
        rows_of = slice(block * side, (block + 1) * side)
        gq_low[block] = jnp.concatenate(
            [gwq_sum[rows_of, k * padded : k * padded + width] for k in range(3)], axis=1
        ).astype(low)
    hand_over(now)
    for c in range(per):
        cot = kept(c, cot_ref[c * BLOCK : (c + 1) * BLOCK, :].astype(f32))
        gs_sum[4:5, :] += jnp.sum(cot, axis=0, keepdims=True)
    final.start()
    line_ref[here.dp] = jnp.concatenate(
        [gb_sum[0:2, :], gs_sum[0:5, :], jnp.zeros((1, d), f32)]
    )
    line = Exchange(line_ref, line_sem, here.dp, here.n, lambda to: (to, here.t))
    cross = Exchange(cross_ref, cross_sem, here.t, here.ways, lambda to: (here.dp, to))
    collect(now)
    pass_on(now)
    line.start()
    for k in range(1, here.majors):
        final.add(k)
        if k == 1:
            total = weights.finish()
            gi_ref[...] = total[:, :hidden]
            gd_ref[...] = total[:, hidden : 2 * hidden]
            go_ref[...] = total[:, 2 * hidden : 2 * hidden + width].T
        final.forward(k)
    summed = line.total()
    for k in range(3):
        gbq_ref[k : k + 1, :] = summed[0:1, k * padded : k * padded + width]
    gb_ref[...] = summed[1, :]
    cross_ref[here.t] = summed
    cross.start()

    def grad_copy(c):
        return pltpu.make_async_copy(gn_own.at[c], gx_out.at[pl.ds(c * BLOCK, BLOCK)], out_sems.at[1 + c])

    for c in range(per):
        far_block(c).wait()
    for c in range(per):
        at = slice(c * BLOCK, (c + 1) * BLOCK)
        normed, inv_std = norm_rows(tokens_ref[at, :].astype(f32))
        grad_normed = gn_own[c] + gn_far[c].astype(f32)
        gn_own[c] = cot_ref[at, :].astype(f32) + inv_std * (
            grad_normed
            - jnp.mean(grad_normed, axis=1, keepdims=True)
            - normed * jnp.mean(grad_normed * normed, axis=1, keepdims=True)
        )
        grad_copy(c).start()
    summed = cross.total()
    for k in range(2):
        product, plain = summed[2 + 2 * k : 3 + 2 * k, :], summed[3 + 2 * k : 4 + 2 * k, :]
        gain, bias = norm_ref[2 * k : 2 * k + 1, :], norm_ref[2 * k + 1 : 2 * k + 2, :]
        small_ref[2 * k : 2 * k + 1, :] = (product - bias * plain) / gain
        small_ref[2 * k + 1 : 2 * k + 2, :] = plain
    small_ref[4:5, :] = summed[6:7, :]
    for slot in range(2 * per):
        near_block(slot // per * 2 * per + (1 - here.core) * per + slot % per).wait_send()
    for one in (rows, cots, proj_w, in_w, down_w, line, cross):
        one.finish()
    output_copy().wait()
    for c in range(per):
        grad_copy(c).wait()
    total = final.finish()
    for k in range(3):
        gq_ref[k] = total[:, k * width : (k + 1) * width]


def layer(length, tokens, cot, norms, wq, bq, wo, wi, bi, wd, biases, table):
    local, d = tokens.shape
    _, side, width = wq.shape
    hidden = wi.shape[1]
    heads = width // HD
    padded = round_up(width + 3, LANES)
    n, ways = lax.axis_size("dp"), lax.axis_size("tensor")
    majors = n // 2
    rows = local * ways
    blocks, per = rows // BLOCK, local // BLOCK
    assert rows == LMAX and length.shape[0] == 1
    assert ways == 4 and per == 2 and n % 4 == 0 and padded == BLOCK and heads == 3
    assert 3 * padded == d == hidden == side * n
    vmem = pl.BlockSpec(memory_space=pltpu.VMEM)
    hbm = pl.BlockSpec(memory_space=pl.ANY)
    row_blocks = pltpu.VMEM((blocks, BLOCK, d), low)
    head_blocks = pltpu.VMEM((blocks, heads * BLOCK, padded), low)
    columns = hidden + wd.shape[1] + padded
    outs = [
        jax.ShapeDtypeStruct((local, d), f32),
        jax.ShapeDtypeStruct((local, d), f32),
        jax.ShapeDtypeStruct((3, side, width), f32),
        jax.ShapeDtypeStruct((3, width), f32),
        jax.ShapeDtypeStruct((width, side), f32),
        jax.ShapeDtypeStruct((side, hidden), f32),
        jax.ShapeDtypeStruct((hidden,), f32),
        jax.ShapeDtypeStruct((side, hidden), f32),
        jax.ShapeDtypeStruct((5, d), f32),
    ]
    args = (tokens, cot, *norms, wq, bq, wo, wi, bi, wd, *biases, table)
    return pl.pallas_call(
        layer_kernel,
        name="layer",
        in_specs=[pl.BlockSpec(memory_space=pltpu.SMEM)] + [vmem] * len(args),
        out_specs=[hbm, hbm] + [vmem] * (len(outs) - 2),
        out_shape=outs,
        scratch_shapes=[
            pltpu.VMEM((8, d), f32),
            pltpu.VMEM((1, 3 * padded), f32),
            pltpu.VMEM((side, 3 * padded), low),
            pltpu.VMEM((side, hidden + padded), low),
            pltpu.VMEM((n, side, 3 * padded), low),
            pltpu.VMEM((n, side, hidden), low),
            pltpu.VMEM((n, side, hidden + padded), low),
            row_blocks, row_blocks, row_blocks, row_blocks,
            pltpu.VMEM((blocks, BLOCK, 3 * padded), low),
            head_blocks, head_blocks,
            pltpu.VMEM((blocks, BLOCK, padded), low),
            pltpu.VMEM((blocks * heads, BLOCK, BLOCK), f32),
            pltpu.VMEM((blocks, width, BLOCK), low),
            pltpu.VMEM((d, hidden), f32),
            pltpu.VMEM((d, hidden + padded), f32),
            pltpu.VMEM((8, d), f32),
            pltpu.VMEM((8, d), f32),
            pltpu.VMEM((n, side, columns), low),
            pltpu.SemaphoreType.DMA((2 * per + 3,)),
            pltpu.SemaphoreType.DMA((1 + per,)),
            pltpu.SemaphoreType.DMA((2, 3 * per)),
            pltpu.SemaphoreType.DMA((2, 3 * per)),
            *gather_scratch(majors), *gather_scratch(majors), *gather_scratch(majors),
            pltpu.VMEM((2 * per, BLOCK, d), low),
            pltpu.VMEM((per, BLOCK, d), f32),
            pltpu.VMEM((per, BLOCK, d), low),
            pltpu.SemaphoreType.DMA((2, 2 * per)),
            pltpu.SemaphoreType.DMA((2, per)),
            pltpu.VMEM((2, per, BLOCK, d), low),
            pltpu.VMEM((per, BLOCK, d), low),
            pltpu.SemaphoreType.DMA((2, 2)),
            pltpu.SemaphoreType.DMA((2, 1)),
            *scatter_scratch(majors, side, columns),
            pltpu.VMEM((n, side, 3 * width), low),
            *scatter_scratch(majors, side, 3 * width),
            pltpu.VMEM((n, 8, d), f32),
            pltpu.VMEM((ways, 8, d), f32),
            pltpu.SemaphoreType.DMA((2, n)),
            pltpu.SemaphoreType.DMA((2, ways)),
        ],
        compiler_params=pltpu.CompilerParams(
            vmem_limit_bytes=VMEM, collective_id=0, has_side_effects=True
        ),
    )(length, *args)


def per_device(
    tokens, cotangent, seq_lengths, norm1_gain, norm1_bias, norm2_gain, norm2_bias,
    w_qkv, b_qkv, w_attn_out, w_in, b_in, w_down, b_out, b_down,
):
    output, grad_x, g_qkv, gb_qkv, g_out, g_in, gb_in, g_down, small = layer(
        seq_lengths, tokens, cotangent, (norm1_gain, norm1_bias, norm2_gain, norm2_bias),
        w_qkv.transpose(1, 0, 2), b_qkv, w_attn_out, w_in, b_in, w_down.T, (b_out, b_down),
        jnp.asarray(rotary_base()),
    )
    return output, grad_x, g_qkv.transpose(1, 0, 2), gb_qkv, g_out, g_in, gb_in, g_down.T, small


def solution(mesh):
    rows = P(("dp", "tensor"), None)
    placed = (
        rows, rows, P("dp"), P(), P(), P(), P(), P("dp", None, "tensor"), P(None, "tensor"),
        P("tensor", "dp"), P("dp", "tensor"), P("tensor"), P("tensor", "dp"), P(), P(),
    )
    return jax.shard_map(
        per_device,
        mesh=mesh,
        in_specs=placed,
        out_specs=(
            rows, rows, P("dp", None, "tensor"), P(None, "tensor"), P("tensor", "dp"),
            P("dp", "tensor"), P("tensor"), P("tensor", "dp"), P(),
        ),
        check_vma=False,
    )
```

time: 610 us -> 179 us (0.29)
  waiting for transfers between devices: 419 us -> 0 us
  Pallas kernels: 108 us -> 169 us
  blocking collectives: 47.5 us -> 0 us
  between operations: 15.2 us -> 1.35 us
  other arithmetic: 10.8 us -> 0 us
    reduce_scatter x5 -> x0, waiting for transfers between devices: 268 us -> none  [per_device(): lax.psum_scatter(a, axis, scatter_dimension=0, tiled=True).astype(f32)]
    all_gather x5 -> x0, waiting for transfers between devices: 147 us -> none  [per_device(): gather = lambda a, axis: lax.all_gather(a, axis, axis=0, tiled=True)]
    pallas_call x4 -> x1, Pallas kernels: 108 us -> 169 us  [layer(): pl.pallas_call(layer_kernel, name='layer', in_specs=[pl.BlockSpec(memory_...]
    psum x2 -> x0, blocking collectives: 47.5 us -> none  [the longest x1 37.1 us: per_device(): gb_qkv, gb_in, small = lax.psum((gb_qkv, gb_in, small), 'dp')]
    reduce_sum x4 -> x0, other arithmetic: 6.16 us -> none  [the longest x1 3.69 us: per_device(): jnp.sum(row_mask * cot, axis=0, keepdims=True)]
  transfers between devices with their start and end apart: 10 -> 0, of which waited for: 10 -> 0; matrix products, arithmetic and copies ran while one was open for 2% -> 0% of each run, Pallas kernels for 6% -> 0%
where the time goes in v4:
time: 179 us; the launch traced here: 178 us
  Pallas kernels  169 us (94%)
  local copies, waits for them, and re-layouts  8.52 us (5%)
    pallas_call x1, Pallas kernels, layer(): pl.pallas_call(layer_kernel, name='layer', in_specs=[pl.BlockSpec(memory_...  169 us
    unnamed x25, local copies, waits for them, and re-layouts  8.52 us

profile of v4, /device:TPU:0, one launch (start us, length us, event | category | flops | bytes accessed | tf_op | source)
XLA Modules:
  0.0 178.4 jit_solution(15868321783413216647)
XLA Ops:
  1.3 168.6 %layer.1 = (f32[512,768]{1,0:T(8,128)}, f32[512,768]{1,0:T(8,128)}, f32[3,96,192]{2,1,0:T(8,128)}, f32[3,192]{1,0:T(4,128)}, f32[192,96]{1,0:T(8,128)}, /*index=...) custom-call(s32[1]{0:T(128)S(6)} %copy.34.length_ref, bf16[512,768]{1,0:T(8,128)(2,1)} %tokens_ref.1, ...), custom_call_target="tpu_custom_call" | custom-call | tf_op jit(solution)/shard_map/layer/pallas_call | solution.py:834
  169.9 0.0 copy-start
  169.9 2.8 %copy.35 = f32[512,768]{1,0:T(8,128)} copy(f32[512,768]{1,0:T(8,128)} %get-tuple-element.36) | data formatting | bytes 3145728
  172.6 0.0 copy-done
  172.6 0.0 copy-start.3
  172.6 0.0 copy-start.7
  172.6 0.0 copy-start.4
  172.6 0.0 copy-start.2
  172.7 0.0 copy-start.6
  172.7 0.0 copy-start.1
  172.7 1.1 copy.36
  173.8 0.0 copy-done.3
  173.8 0.0 copy-start.5
  173.8 0.7 copy.37
  174.5 0.0 copy-done.7
  174.5 0.6 copy.38
  175.1 0.0 copy-done.4
  175.1 0.6 copy.39
  175.8 0.0 copy-done.2
  175.8 0.7 copy.40
  176.5 0.0 copy-done.6
  176.5 0.6 copy.41
  177.1 0.0 copy-done.1
  177.1 0.7 copy.42
  177.8 0.0 copy-done.5
  177.8 0.6 copy.43
Async XLA Ops:
  169.9 2.8 %copy-start = (f32[512,768]{1,0:T(8,128)S(1)}, f32[512,768]{1,0:T(8,128)}, u32[]{:S(2)}) copy-start(f32[512,768]{1,0:T(8,128)} %get-tuple-element.37) | copy-start | bytes 4718596
  172.6 1.2 copy-start.3
  172.6 1.9 %copy-start.7 = (f32[3,192]{1,0:T(4,128)S(1)}, f32[3,192]{1,0:T(4,128)}, u32[]{:S(2)}) copy-start(f32[3,192]{1,0:T(4,128)} %get-tuple-element.39) | copy-start | bytes 6916
  172.6 2.5 %copy-start.4 = (f32[192,96]{1,0:T(8,128)S(1)}, f32[192,96]{1,0:T(8,128)}, u32[]{:S(2)}) copy-start(f32[192,96]{1,0:T(8,128)} %get-tuple-element.40) | copy-start | bytes 221188
  172.6 3.1 %copy-start.2 = (f32[96,768]{1,0:T(8,128)S(1)}, f32[96,768]{1,0:T(8,128)}, u32[]{:S(2)}) copy-start(f32[96,768]{1,0:T(8,128)} %get-tuple-element.41) | copy-start | bytes 884740
  172.7 3.8 %copy-start.6 = (f32[768]{0:T(1024)S(1)}, f32[768]{0:T(1024)}, u32[]{:S(2)}) copy-start(f32[768]{0:T(1024)} %get-tuple-element.42) | copy-start | bytes 9220
  172.7 4.4 %copy-start.1 = (f32[96,768]{1,0:T(8,128)S(1)}, f32[96,768]{1,0:T(8,128)}, u32[]{:S(2)}) copy-start(f32[96,768]{1,0:T(8,128)} %get-tuple-element.25) | copy-start | bytes 884740
  173.8 4.0 %copy-start.5 = (f32[5,768]{1,0:T(8,128)S(1)}, f32[5,768]{1,0:T(8,128)}, u32[]{:S(2)}) copy-start(f32[5,768]{1,0:T(8,128)} %get-tuple-element.44) | copy-start | bytes 46084

commit v5 on v4

--- a/solution.py
+++ b/solution.py
@@ -137,28 +137,39 @@
     def first(self, k):
         p = self.p
         mine = self.mine.at[p.major(k)[0] * 2 + 1 - p.b]
-        return send(mine, self.got.at[k % p.majors], self.pairs, k % p.majors, p.beside)
+        return send(mine, self.got.at[k], self.pairs, k, p.beside)
 
     def second(self, k):
         to = (self.p.major(k)[1], self.p.t)
         return send(self.got.at[k], self.last.at[k - 1], self.lines, k - 1, to)
 
-    def start(self):
-        for k in range(1, self.p.majors + 1):
-            self.first(k).start()
-
-    def add(self, k):
+    def order(self, number):
+        p = self.p
+        half = p.majors // 2
+        if number <= half:
+            a = (1 - p.upper) * half + number - 1
+        else:
+            a = p.upper * half + (p.a % half + number - half) % half
+        return (a - p.a + p.majors) % p.majors
+
+    def start_half(self, turn):
+        half = self.p.majors // 2
+        for number in range(turn * half + 1, (turn + 1) * half + 1):
+            self.first(self.order(number)).start()
+
+    def add(self, number):
+        k = self.order(number)
         self.first(k).wait_recv()
         self.got[k] = plus(self.mine[self.p.major(k)[1]], self.got[k]).astype(self.got.dtype)
 
-    def forward(self, k):
-        self.second(k).start()
+    def forward(self, number):
+        self.second(self.order(number)).start()
 
     def finish(self):
         p = self.p
-        for k in range(1, p.majors + 1):
+        for k in range(p.majors):
             self.first(k).wait_send()
-        self.first(p.majors).wait_recv()
+        self.first(0).wait_recv()
         for k in range(1, p.majors):
             self.second(k).wait()
         return plus(self.mine[p.dp], self.got[0], *[self.last[k] for k in range(p.majors - 1)])
@@ -168,42 +179,89 @@
     def __init__(self, place, mine, whole, sems):
         self.p, self.mine, self.whole, self.lines, self.pairs = place, mine, whole, *sems
 
-    def line(self, k):
+    def line(self, way, hop):
         p = self.p
-        return send(self.mine, self.whole.at[p.dp], self.lines, k - 1, (p.major(k)[1], p.t))
-
-    def pair(self, k):
-        block = self.whole.at[self.p.major(self.p.majors - k)[1]]
-        return send(block, block, self.pairs, k, self.p.beside)
-
-    def own_pair(self):
-        return send(self.mine, self.whole.at[self.p.dp], self.pairs, 0, self.p.beside)
+        step = 1 - 2 * way
+        origin = (p.a - step * hop) * 2 + p.b
+        mine = self.mine if hop == 0 else self.whole.at[origin]
+        to = ((p.a + step) * 2 + p.b, p.t)
+        return send(mine, self.whole.at[origin], self.lines, way * (p.majors - 1) + hop, to)
+
+    def pair(self, way, hop):
+        p = self.p
+        origin = (p.a - (1 - 2 * way) * hop) * 2 + p.b
+        mine = self.mine if hop == 0 else self.whole.at[origin]
+        return send(mine, self.whole.at[origin], self.pairs, way * p.majors + hop, p.beside)
+
+    def came(self, way, hop):
+        p = self.p
+        return p.a >= hop if way == 0 else p.a <= p.majors - 1 - hop
+
+    def goes(self, way, hop):
+        p = self.p
+        return self.came(way, hop) & (p.a < p.majors - 1 if way == 0 else p.a > 0)
 
     def start(self):
+        for way in range(2):
+
+            @pl.when(self.goes(way, 0))
+            def _():
+                self.line(way, 0).start()
+
+        self.pair(0, 0).start()
+
+    def forward(self, hop):
+        for way in range(2):
+
+            @pl.when(self.came(way, hop))
+            def _():
+                self.arrival(way, hop).wait_recv()
+                if hop < self.p.majors - 1:
+
+                    @pl.when(self.goes(way, hop))
+                    def _():
+                        self.line(way, hop).start()
+
+                self.pair(way, hop).start()
+
+    def arrival(self, way, hop):
         p = self.p
-        for k in range(1, p.majors):
-            self.line(k + p.upper * (p.majors - 2 * k)).start()
-
-    def forward(self, number):
+        step = 1 - 2 * way
+        block = self.whole.at[(p.a - step * hop) * 2 + p.b]
+        back = ((p.a - step) * 2 + p.b, p.t)
+        return send(block, block, self.lines, way * (p.majors - 1) + hop - 1, back)
+
+    def arrived(self):
         p = self.p
-        k = p.majors - number + p.upper * (2 * number - p.majors)
-        self.line(k).wait_recv()
-        self.pair(k).start()
-
-    def arrived(self):
-        self.own_pair().wait_recv()
-        for k in range(1, self.p.majors):
-            self.pair(k).wait_recv()
+        for way in range(2):
+            for hop in range(way, p.majors):
+
+                @pl.when(self.came(way, hop))
+                def _():
+                    other = self.whole.at[(p.a - (1 - 2 * way) * hop) * 2 + 1 - p.b]
+                    send(other, other, self.pairs, way * p.majors + hop, p.beside).wait_recv()
 
     def finish(self):
-        self.own_pair().wait_send()
-        for k in range(1, self.p.majors):
-            self.pair(k).wait_send()
-            self.line(k).wait_send()
+        for way in range(2):
+            for hop in range(self.p.majors):
+                if hop < self.p.majors - 1:
+
+                    @pl.when(self.goes(way, hop))
+                    def _():
+                        self.line(way, hop).wait_send()
+
+                if way == 0 or hop > 0:
+
+                    @pl.when(self.came(way, hop))
+                    def _():
+                        self.pair(way, hop).wait_send()
 
 
 def gather_scratch(majors):
-    return [pltpu.SemaphoreType.DMA((2, majors - 1)), pltpu.SemaphoreType.DMA((2, majors))]
+    return [
+        pltpu.SemaphoreType.DMA((2, 2 * (majors - 1))),
+        pltpu.SemaphoreType.DMA((2, 2 * majors)),
+    ]
 
 
 class Rows:
@@ -295,12 +353,12 @@
 def layer_kernel(
     length_ref, tokens_ref, cot_ref, g1_ref, b1_ref, g2_ref, b2_ref, wq_ref, bq_ref, wo_ref, wi_ref,
     bi_ref, wd_ref, bo_ref, bd_ref, table_ref,
-    out_out, gx_out, gq_ref, gbq_ref, go_ref, gi_ref, gb_ref, gd_ref, small_ref,
+    out_out, gx_out, spill_out, gq_ref, gbq_ref, go_ref, gi_ref, gb_ref, gd_ref, small_ref,
     norm_ref, bias_ref, wq_mine, wd_mine, wq_all, wi_all, wd_all,
-    x_all, first_ref, second_ref, cot_all, qkv_ref, qx_ref, vm_ref, context_ref, pool_ref,
-    keyt_ref, gwi_sum, gwd_sum, gb_sum, gs_sum, gw_ref, own_sems, out_sems, x_sems, cot_sems,
+    x_all, first_ref, second_ref, cot_all, qkv_ref, qx_ref, dox_ref, context_ref, pool_ref,
+    keyt_ref, queryt_ref, valuet_ref, mixed_ref, top_ref, gwq_sum, stage_ref, gb_sum, gs_sum, gw_ref, own_sems, out_sems, x_sems, cot_sems,
     wq_lines, wq_pairs, wi_lines, wi_pairs, wd_lines, wd_pairs,
-    gn_near, gn_own, gn_far, gn_sem1, gn_sem2,
+    gn_near, gn_far, gn_sem1, gn_sem2,
     br_near, br_far, br_sem1, br_sem2,
     w_got, w_last, w_sem1, w_sem2,
     gq_low, q_got, q_last, q_sem1, q_sem2,
@@ -316,9 +374,10 @@
     hidden = wi_ref.shape[1]
     side = wi_ref.shape[0]
     scale = HD ** (-0.5)
+    to_power = scale * math.log2(math.e)
+    tall = valuet_ref.shape[1] // heads
     lane = lax.broadcasted_iota(jnp.int32, (BLOCK, padded), 1)
     of_head = [(lane >= h * HD) & (lane < (h + 1) * HD) for h in range(heads)]
-    inside = lane < width
     extra = (lane >= width) & (lane < width + 3)
 
     rows = Rows(here, tokens_ref, x_all, x_sems)
@@ -340,10 +399,7 @@
 
     here.greet()
     proj_w.start()
-    proj_w.own_pair().start()
     rows.start()
-    in_w.start()
-    down_w.start()
     own = [
         pltpu.make_async_copy(tokens_ref.at[pl.ds(c * BLOCK, BLOCK)], x_all.at[here.t * per + c], own_sems.at[c])
         for c in range(per)
@@ -369,17 +425,18 @@
         r = here.shard(kind) * per + c
         projected = dot(first_ref[r], flat(wq_all), NN) + bias_ref[...]
         tables = rotary_rows(table_ref, r)
-        qkv_ref[r, :, :padded] = rotate(projected[:, :padded], tables, 1).astype(low)
+        queries = rotate(projected[:, :padded], tables, 1)
+        queryt_ref[r] = queries.T[:width].astype(low)
+        qkv_ref[r, :, :padded] = queries.astype(low)
         keys = rotate(projected[:, padded : 2 * padded], tables, 1)
-        keys = jnp.where(extra, 1.0, keys)
         keyt_ref[r] = keys.T[:width].astype(low)
-        qkv_ref[r, :, padded : 2 * padded] = keys.astype(low)
+        qkv_ref[r, :, padded : 2 * padded] = jnp.where(extra, 1.0, keys).astype(low)
         values = projected[:, 2 * padded :]
         qkv_ref[r, :, 2 * padded :] = jnp.where(extra, 1.0, values).astype(low)
+        turned = values.T.astype(low)
         for h in range(heads):
-            vm_ref[r, h * BLOCK : (h + 1) * BLOCK, :] = jnp.where(
-                of_head[h], values, jnp.where(lane == width + h, 1.0, 0.0)
-            ).astype(low)
+            valuet_ref[r, h * tall : h * tall + HD, :] = turned[h * HD : (h + 1) * HD]
+            valuet_ref[r, h * tall + HD : (h + 1) * tall, :] = jnp.ones((tall - HD, BLOCK), low)
 
     for c in range(per):
         own[c].wait()
@@ -401,8 +458,7 @@
     for c in range(per - 1):
         rows.forward(c)
     proj_w.forward(here.majors - 1)
-    in_w.own_pair().start()
-    down_w.own_pair().start()
+    in_w.start()
     cots.start()
     for c in range(per - 1):
         norm(2, c)
@@ -418,6 +474,10 @@
         def _():
             rows.forward(per - 1)
 
+        @pl.when(number == per - 1)
+        def _():
+            in_w.forward(1)
+
         later = number // per
         project(1 + later + number % per * later, number % per * (1 - later))
 
@@ -425,19 +485,45 @@
     def _(c):
         project(0, c)
 
+    for k in range(2, here.majors - 1):
+        in_w.forward(k)
     norm(2, per - 1)
     project(2, per - 1)
     rows.arrived(2, per - 1)
     norm(3, per - 1)
     project(3, per - 1)
 
+    def spilled():
+        return pltpu.make_async_copy(first_ref, spill_out, out_sems.at[1 + per])
+
+    def restored():
+        return pltpu.make_async_copy(spill_out, first_ref, out_sems.at[1 + per])
+
+    spilled().start()
+
+    def in_fours(count, body):
+        @pl.loop(0, count // 4)
+        def _(number):
+            for k in range(4):
+                body(4 * number + k)
+
+        for size in (2, 1):
+
+            @pl.when(count // size % 2 == 1)
+            def _():
+                for k in range(size):
+                    body(count // (2 * size) * (2 * size) + k)
+
+    in_w.forward(here.majors - 1)
+    down_w.start()
+
     @pl.loop(0, blocks)
     def _(i):
         for k in range(1, here.majors):
 
-            @pl.when(i == min(blocks // 2 - 2 + k, blocks - 1))
+            @pl.when(i == min(2 * k, blocks - 1))
             def _():
-                in_w.forward(k)
+                down_w.forward(k)
 
         for c in range(per):
 
@@ -449,122 +535,100 @@
         for h in range(heads):
             qx_ref[i, h * BLOCK : (h + 1) * BLOCK, :] = jnp.where(of_head[h], q, 0.0).astype(low)
         query = qx_ref[i]
+        parts = [slice(h * BLOCK, (h + 1) * BLOCK) for h in range(heads)]
 
         def scores(j):
-            return dot(query, qkv_ref[j, :, padded : 2 * padded], NT)
-
-        def widest(s):
-            return functools.reduce(
-                jnp.maximum, [s[:, c : c + LANES] for c in range(0, BLOCK, LANES)]
-            )
+            return dot(qkv_ref[j, :, padded : 2 * padded], query, NT)
+
+        def highest(s):
+            return jnp.max(s.reshape(-1, 8, heads * BLOCK), axis=0)
+
+        def keep(j, s):
+            for h in range(heads):
+                pool_ref[j * heads + h] = s[:, parts[h]]
 
         diagonal = scores(i)
-        row = lax.broadcasted_iota(jnp.int32, diagonal.shape, 0) % BLOCK
-        col = lax.broadcasted_iota(jnp.int32, diagonal.shape, 1)
-        diagonal = jnp.where(col <= row, diagonal, -1e30)
-
-        def first_pass(j, top):
+        key_at = lax.broadcasted_iota(jnp.int32, diagonal.shape, 0)
+        query_at = lax.broadcasted_iota(jnp.int32, diagonal.shape, 1) % BLOCK
+        diagonal = jnp.where(key_at <= query_at, diagonal, -1e30)
+        keep(i, diagonal)
+        top_ref[...] = highest(diagonal)
+
+        def first_pass(j):
             s = scores(j)
-            pool_ref[pl.ds(j * heads, heads)] = s.reshape(heads, BLOCK, BLOCK)
-            return jnp.maximum(top, widest(s))
-
-        top = lax.fori_loop(0, i, first_pass, widest(diagonal))
-        top = jnp.max(top, axis=1, keepdims=True)
-
-        def weigh(s, j):
-            p = jnp.exp((s - top) * scale).astype(low)
-            parts = [slice(h * BLOCK, (h + 1) * BLOCK) for h in range(heads)]
-            return functools.reduce(jnp.add, [dot(p[at], vm_ref[j, at, :], NN) for at in parts])
-
-        def second_pass(j, total):
-            s = pool_ref[pl.ds(j * heads, heads)].reshape(heads * BLOCK, BLOCK)
-            return total + weigh(s, j)
-
-        mixed = lax.fori_loop(0, i, second_pass, weigh(diagonal, i))
-        inverse = jnp.zeros((BLOCK, padded), f32)
+            keep(j, s)
+            top_ref[...] = jnp.maximum(top_ref[...], highest(s))
+
+        in_fours(i, first_pass)
+        top = jnp.max(top_ref[...], axis=0, keepdims=True)
+        mixed_ref[...] = jnp.zeros_like(mixed_ref)
+
+        def second_pass(j):
+            for h in range(heads):
+                p = jnp.exp2((pool_ref[j * heads + h] - top[:, parts[h]]) * to_power).astype(low)
+                at = slice(h * tall, (h + 1) * tall)
+                mixed_ref[at, :] += dot(valuet_ref[j, at, :], p, NN)
+
+        in_fours(i + 1, second_pass)
+        mixed, terms = [], []
         for h in range(heads):
-            total = mixed[:, width + h : width + h + 1]
-            inverse = jnp.where(of_head[h], 1.0 / total, inverse)
-            log_total = top[h * BLOCK : (h + 1) * BLOCK] + jnp.log(total) / scale
-            extended = jnp.where(of_head[h], q, 0.0)
-            for k, term in enumerate(three_terms(-log_total)):
-                extended = jnp.where(lane == width + k, term, extended)
-            qx_ref[i, h * BLOCK : (h + 1) * BLOCK, :] = extended.astype(low)
-        context_ref[i] = (mixed * inverse).astype(low)
-
-    for k in range(1, here.majors):
-        down_w.forward(k)
+            total = mixed_ref[h * tall + HD : h * tall + HD + 1, :]
+            mixed.append(mixed_ref[h * tall : h * tall + HD, :] * (1.0 / total))
+            terms.append(jnp.concatenate(three_terms(-top[:, parts[h]] - jnp.log(total) / scale)))
+        terms = jnp.concatenate(terms, axis=1)
+        side_rows = width - (padded - LANES)
+        columns = jnp.concatenate(
+            [
+                jnp.zeros((side_rows, heads * BLOCK), f32),
+                terms,
+                jnp.zeros((LANES - side_rows - 3, heads * BLOCK), f32),
+            ]
+        ).T
+        for h in range(heads):
+            right = jnp.where(of_head[h], q, 0.0)[:, padded - LANES :]
+            qx_ref[i, parts[h], padded - LANES :] = (right + columns[parts[h]]).astype(low)
+        mixed.append(jnp.zeros((padded - width, BLOCK), f32))
+        context_ref[i] = jnp.concatenate(mixed).T.astype(low)
+
+    grad_ref, act_ref, hidden_ref, gradt_ref = cot_all, x_all, first_ref, valuet_ref
+    own[2 * per + 1].wait()
+    in_w.arrived()
+    rows.released()
+
+    @pl.loop(0, blocks)
+    def _(r):
+        u = dot(second_ref[r], flat(wi_all), NN) + norm_ref[6:7, :]
+        cdf = 0.5 * (1.0 + lax.erf(u * (1.0 / math.sqrt(2.0))))
+        act_ref[r] = (u * cdf).astype(low)
+        slope = cdf + u * (jnp.exp(-0.5 * u * u) * (1.0 / math.sqrt(2.0 * math.pi)))
+        for k in range(3):
+            pool_ref[3 * r + k] = slope[:, k * BLOCK : (k + 1) * BLOCK]
+
     for c in range(per):
         cots.arrived(0, c)
         cots.arrived(2, c)
-    for copy in own[per : 2 * per] + own[2 * per + 1 :]:
+    for copy in own[per : 2 * per] + own[2 * per + 2 :]:
         copy.wait()
-    in_w.arrived()
-    gwi_sum[...] = jnp.zeros_like(gwi_sum)
-    gwd_sum[...] = jnp.zeros_like(gwd_sum)
     gb_sum[...] = jnp.zeros_like(gb_sum)
     gs_sum[...] = jnp.zeros_like(gs_sum)
+    cots.released()
+    spilled().wait()
     down_w.arrived()
-    cots.released()
-    rows.released()
-
-    branch_ref, part_ref, dox_ref = cot_all, second_ref, vm_ref
-
-    def near_branch(chip):
-        owner = chip * 2 + 1 - here.core
-        return send(
-            branch_ref.at[pl.ds(owner * per, per)], br_near.at[chip], br_sem1, chip, here.near
-        )
-
-    def far_branch():
-        return send(br_near.at[1 - here.chip], br_far, br_sem2, 0, here.across)
 
     @pl.loop(0, blocks)
-    def _(number):
-        r = here.shard(3 - number // per) * per + number % per
-
-        @pl.when(number == per + 1)
-        def _():
-            near_branch(1 - here.chip).start()
-
-        @pl.when(number == 2 * per + 1)
-        def _():
-            near_branch(1 - here.chip).wait_recv()
-
-            @pl.loop(0, per)
-            def _(c):
-                mine = branch_ref[here.across[1] * per + c]
-                br_near[1 - here.chip, c] = plus(mine, br_near[1 - here.chip, c]).astype(low)
-
-        @pl.when(number == 3 * per + 1)
-        def _():
-            near_branch(here.chip).start()
-
-        second = second_ref[r]
-        context = context_ref[r]
-        row = lax.broadcasted_iota(jnp.int32, second.shape, 0) + r * BLOCK
+    def _(r):
+        row = lax.broadcasted_iota(jnp.int32, (BLOCK, d), 0) + r * BLOCK
         grad = jnp.where(row < length_ref[0], cot_all[r].astype(f32), 0.0).astype(low)
-
-        u = dot(second, flat(wi_all), NN) + norm_ref[6:7, :]
-        cdf = 0.5 * (1.0 + lax.erf(u * (1.0 / math.sqrt(2.0))))
-        act = (u * cdf).astype(low)
-        slope = cdf + u * (jnp.exp(-0.5 * u * u) * (1.0 / math.sqrt(2.0 * math.pi)))
-        both = jnp.concatenate([act, context], axis=1)
+        grad_ref[r] = grad
         back = dot(grad, flat(wd_all), NN)
-        branch_ref[r] = dot(both, flat(wd_all), NT).astype(low)
-
+        slope = jnp.concatenate([pool_ref[3 * r + k] for k in range(3)], axis=1)
         grad_hidden = back[:, :hidden] * slope
         gb_sum[1:2, :] += jnp.sum(grad_hidden, axis=0, keepdims=True)
-        hidden_low = grad_hidden.astype(low)
-        gwi_sum[...] += dot(second, hidden_low, TN)
-        gwd_sum[...] += dot(grad, both, TN)
-
-        @pl.when(number == 2 * per + 1)
-        def _():
-            far_branch().start()
+        hidden_ref[r] = grad_hidden.astype(low)
 
         grad_context = back[:, hidden:].astype(low).astype(f32)
-        product = grad_context * context.astype(f32)
+        gradt_ref[r, :width, :] = grad_context.T[:width].astype(low)
+        product = grad_context * context_ref[r].astype(f32)
         for h in range(heads):
             extended = jnp.where(of_head[h], grad_context, 0.0)
             delta = jnp.sum(jnp.where(of_head[h], product, 0.0), axis=1, keepdims=True)
@@ -572,21 +636,83 @@
                 extended = jnp.where(lane == width + k, term, extended)
             dox_ref[r, h * BLOCK : (h + 1) * BLOCK, :] = extended.astype(low)
 
-        part = dot(hidden_low, flat(wi_all), NT)
-        gs_sum[2:3, :] += jnp.sum(part * second.astype(f32), axis=0, keepdims=True)
+    weights = Scatter(here, gw_ref, w_got, w_last, (w_sem1, w_sem2))
+    final = Scatter(here, gq_low, q_got, q_last, (q_sem1, q_sem2))
+    half = d // 2
+    rows_total = blocks * BLOCK
+
+    @pl.loop(0, 2)
+    def _(turn):
+        which = (1 - turn) * (1 - here.upper) + turn * here.upper
+        at = pl.ds(pl.multiple_of(which * half, LANES), half)
+        all_rows = lambda ref: ref[...].reshape(rows_total, ref.shape[2])
+        mine = second_ref[:, :, at].reshape(rows_total, half)
+        first_block = which * (here.n // 2)
+        side_blocks = pl.ds(first_block, here.n // 2)
+        gwi = dot(mine, all_rows(hidden_ref), TN).reshape(here.n // 2, side, hidden)
+        gw_ref[side_blocks, :, :hidden] = gwi.astype(low)
+        @pl.when(turn == 1)
+        def _():
+            weights.start_half(0)
+
+        mine = grad_ref[:, :, at].reshape(rows_total, half)
+        gwd = dot(mine, all_rows(act_ref), TN).reshape(here.n // 2, side, hidden)
+        gw_ref[side_blocks, :, hidden : 2 * hidden] = gwd.astype(low)
+        gwd = dot(mine, all_rows(context_ref), TN).reshape(here.n // 2, side, padded)
+        gw_ref[side_blocks, :, 2 * hidden :] = gwd.astype(low)
+
+    branch_ref, part_ref = cot_all, second_ref
+
+    def near_branch(chip):
+        owner = chip * 2 + 1 - here.core
+        return send(
+            branch_ref.at[pl.ds(owner * per, per)], br_near.at[chip], br_sem1, chip, here.near
+        )
+
+    def far_branch():
+        return send(br_near.at[1 - here.chip], br_far, br_sem2, 0, here.across)
+
+    @pl.loop(0, blocks)
+    def _(number):
+        r = here.shard(3 - number // per) * per + number % per
+
+        @pl.when(number == per + 1)
+        def _():
+            near_branch(1 - here.chip).start()
+
+        @pl.when(number == 2 * per + 1)
+        def _():
+            near_branch(1 - here.chip).wait_recv()
+
+            @pl.loop(0, per)
+            def _(c):
+                mine = branch_ref[here.across[1] * per + c]
+                br_near[1 - here.chip, c] = plus(mine, br_near[1 - here.chip, c]).astype(low)
+
+        @pl.when(number == 3 * per + 1)
+        def _():
+            near_branch(here.chip).start()
+
+        second = second_ref[r].astype(f32)
+        part = dot(hidden_ref[r], flat(wi_all), NT)
+        both = jnp.concatenate([act_ref[r], context_ref[r]], axis=1)
+        branch_ref[r] = dot(both, flat(wd_all), NT).astype(low)
+        gs_sum[2:3, :] += jnp.sum(part * second, axis=0, keepdims=True)
         gs_sum[3:4, :] += jnp.sum(part, axis=0, keepdims=True)
         part_ref[r] = (part * norm_ref[2:3, :]).astype(low)
 
-    weights = Scatter(here, gw_ref, w_got, w_last, (w_sem1, w_sem2))
-    final = Scatter(here, gq_low, q_got, q_last, (q_sem1, q_sem2))
-    for block in range(here.n):
-        rows_of = slice(block * side, (block + 1) * side)
-        gw_ref[block, :, :hidden] = gwi_sum[rows_of, :].astype(low)
-        gw_ref[block, :, hidden:] = gwd_sum[rows_of, :].astype(low)
-    gwq_sum, gn_ref = gwi_sum, x_all
+        @pl.when(number == 0)
+        def _():
+            weights.start_half(1)
+
+        @pl.when(number == 2 * per + 1)
+        def _():
+            far_branch().start()
+
+    restored().start()
+    gn_ref = x_all
     gwq_sum[...] = jnp.zeros_like(gwq_sum)
     pool_ref[...] = jnp.zeros_like(pool_ref)
-    weights.start()
 
     last = blocks - 1
 
@@ -614,15 +740,10 @@
         @pl.when(owner % 2 == here.core)
         def _():
             near_block(r).wait_recv()
-            total = plus(gn_ref[r], gn_near[slot_of(r)])
-
-            @pl.when(owner // 2 == here.chip)
-            def _():
-                gn_own[r % per] = total
-
-            @pl.when(owner // 2 != here.chip)
-            def _():
-                gn_near[slot_of(r)] = total.astype(low)
+
+        @pl.when((owner % 2 == here.core) & (owner // 2 != here.chip))
+        def _():
+            gn_near[slot_of(r)] = plus(gn_ref[r], gn_near[slot_of(r)]).astype(low)
 
     def pass_on(r):
         owner = r // per
@@ -634,31 +755,31 @@
     def pair(i, j, own):
         keys, values = qkv_ref[j, :, padded : 2 * padded], qkv_ref[j, :, 2 * padded :]
         query, dout = qx_ref[i], dox_ref[i]
-        p = jnp.exp(dot(keys, query, NT) * scale)
+        p = jnp.exp2(dot(query, keys, NT) * to_power)
         if own:
-            key_at = lax.broadcasted_iota(jnp.int32, p.shape, 0)
-            query_at = lax.broadcasted_iota(jnp.int32, p.shape, 1) % BLOCK
+            query_at = lax.broadcasted_iota(jnp.int32, p.shape, 0) % BLOCK
+            key_at = lax.broadcasted_iota(jnp.int32, p.shape, 1)
             p = jnp.where(key_at <= query_at, p, 0.0)
-        ds = (p * dot(values, dout, NT)).astype(low)
-        pool_ref[blocks + j] += dot(p.astype(low), dout, NN)
-        pool_ref[j] += dot(ds, query, NN)
+        ds = (p * dot(dout, values, NT)).astype(low)
+        p = p.astype(low)
         for h in range(heads):
-            pool_ref[2 * blocks + i, h * HD : (h + 1) * HD, :] += dot(
-                keyt_ref[j, h * HD : (h + 1) * HD, :], ds[:, h * BLOCK : (h + 1) * BLOCK], NN
-            )
+            at, part = slice(h * HD, (h + 1) * HD), slice(h * BLOCK, (h + 1) * BLOCK)
+            pool_ref[blocks + j, at, :] += dot(gradt_ref[i, at, :], p[part], NN)
+            pool_ref[j, at, :] += dot(queryt_ref[i, at, :], ds[part], NN)
+            pool_ref[2 * blocks + i, at, :] += dot(keyt_ref[j, at, :], ds[part], NT)
 
     def kept(c, values):
         row = lax.broadcasted_iota(jnp.int32, (BLOCK, d), 0) + (here.t * per + c) * BLOCK
         return jnp.where(row < length_ref[0], values, 0.0)
 
     def output_copy():
-        return pltpu.make_async_copy(gwd_sum.at[:local, :d], out_out, out_sems.at[0])
+        return pltpu.make_async_copy(stage_ref.at[:], out_out, out_sems.at[0])
 
     @pl.loop(0, blocks)
     def _(step):
         for k in range(1, here.majors):
 
-            @pl.when(step == min(k, last - 2))
+            @pl.when(step == min(k - 1, last - 2))
             def _():
                 weights.add(k)
 
@@ -673,7 +794,7 @@
 
         for k in range(1, here.majors):
 
-            @pl.when(step == min(k, last - 2))
+            @pl.when(step == min(k - 1, last - 2))
             def _():
                 weights.forward(k)
 
@@ -681,10 +802,11 @@
         def _():
             collect(block_of(step - 1))
 
-        @pl.loop(0, last - step)
-        def _(number):
+        def next_pair(number):
             other = turn + 1 + number
             pair(other + odd * (last - turn - other), turn + odd * (other - turn), False)
+
+        in_fours(last - step, next_pair)
 
         @pl.when(step == last // 2)
         def _():
@@ -698,26 +820,28 @@
                 total = plus(branch_ref[here.t * per + c], br_near[here.chip, c], br_far[c])
                 total += norm_ref[4:5, :] + norm_ref[5:6, :]
                 at = pl.ds(pl.multiple_of(c * BLOCK, BLOCK), BLOCK)
-                gwd_sum[at, :d] = tokens_ref[at, :].astype(f32) + kept(c, total)
+                stage_ref[at, :] = tokens_ref[at, :].astype(f32) + kept(c, total)
 
         tables = rotary_rows(table_ref, now)
-        grad_query = jnp.concatenate(
-            [
-                pool_ref[2 * blocks + now, :width, :].T,
-                jnp.zeros((BLOCK, padded - width), f32),
-            ],
-            axis=1,
-        )
+        filler = jnp.zeros((BLOCK, padded - width), f32)
+        turned = [
+            jnp.concatenate([pool_ref[k * blocks + now, :width, :].T, filler], axis=1)
+            for k in range(3)
+        ]
         projected = jnp.concatenate(
             [
-                rotate(grad_query * scale, tables, -1),
-                rotate(jnp.where(inside, pool_ref[now] * scale, 0.0), tables, -1),
-                jnp.where(inside, pool_ref[blocks + now], 0.0),
+                rotate(turned[2] * scale, tables, -1),
+                rotate(turned[0] * scale, tables, -1),
+                turned[1],
             ],
             axis=1,
         )
         gb_sum[0:1, :] += jnp.sum(projected, axis=0, keepdims=True)
         proj_low = projected.astype(low)
+        @pl.when(step == 0)
+        def _():
+            restored().wait()
+
         first = first_ref[now]
         gwq_sum[...] += dot(first, proj_low, TN)
         part = dot(proj_low, flat(wq_all), NT)
@@ -743,7 +867,8 @@
     for c in range(per):
         cot = kept(c, cot_ref[c * BLOCK : (c + 1) * BLOCK, :].astype(f32))
         gs_sum[4:5, :] += jnp.sum(cot, axis=0, keepdims=True)
-    final.start()
+    final.start_half(0)
+    final.start_half(1)
     line_ref[here.dp] = jnp.concatenate(
         [gb_sum[0:2, :], gs_sum[0:5, :], jnp.zeros((1, d), f32)]
     )
@@ -768,15 +893,17 @@
     cross.start()
 
     def grad_copy(c):
-        return pltpu.make_async_copy(gn_own.at[c], gx_out.at[pl.ds(c * BLOCK, BLOCK)], out_sems.at[1 + c])
+        at = pl.ds(c * BLOCK, BLOCK)
+        return pltpu.make_async_copy(stage_ref.at[at], gx_out.at[at], out_sems.at[1 + c])
 
     for c in range(per):
         far_block(c).wait()
+    output_copy().wait()
     for c in range(per):
         at = slice(c * BLOCK, (c + 1) * BLOCK)
         normed, inv_std = norm_rows(tokens_ref[at, :].astype(f32))
-        grad_normed = gn_own[c] + gn_far[c].astype(f32)
-        gn_own[c] = cot_ref[at, :].astype(f32) + inv_std * (
+        grad_normed = plus(gn_ref[here.t * per + c], gn_near[here.chip * per + c], gn_far[c])
+        stage_ref[at, :] = cot_ref[at, :].astype(f32) + inv_std * (
             grad_normed
             - jnp.mean(grad_normed, axis=1, keepdims=True)
             - normed * jnp.mean(grad_normed * normed, axis=1, keepdims=True)
@@ -793,7 +920,6 @@
         near_block(slot // per * 2 * per + (1 - here.core) * per + slot % per).wait_send()
     for one in (rows, cots, proj_w, in_w, down_w, line, cross):
         one.finish()
-    output_copy().wait()
     for c in range(per):
         grad_copy(c).wait()
     total = final.finish()
@@ -822,6 +948,7 @@
     outs = [
         jax.ShapeDtypeStruct((local, d), f32),
         jax.ShapeDtypeStruct((local, d), f32),
+        jax.ShapeDtypeStruct((blocks, BLOCK, d), low),
         jax.ShapeDtypeStruct((3, side, width), f32),
         jax.ShapeDtypeStruct((3, width), f32),
         jax.ShapeDtypeStruct((width, side), f32),
@@ -835,7 +962,7 @@
         layer_kernel,
         name="layer",
         in_specs=[pl.BlockSpec(memory_space=pltpu.SMEM)] + [vmem] * len(args),
-        out_specs=[hbm, hbm] + [vmem] * (len(outs) - 2),
+        out_specs=[hbm] * 3 + [vmem] * (len(outs) - 3),
         out_shape=outs,
         scratch_shapes=[
             pltpu.VMEM((8, d), f32),
@@ -851,18 +978,21 @@
             pltpu.VMEM((blocks, BLOCK, padded), low),
             pltpu.VMEM((blocks * heads, BLOCK, BLOCK), f32),
             pltpu.VMEM((blocks, width, BLOCK), low),
+            pltpu.VMEM((blocks, width, BLOCK), low),
+            pltpu.VMEM((blocks, heads * (HD + 16), BLOCK), low),
+            pltpu.VMEM((heads * (HD + 16), BLOCK), f32),
+            pltpu.VMEM((8, heads * BLOCK), f32),
             pltpu.VMEM((d, hidden), f32),
-            pltpu.VMEM((d, hidden + padded), f32),
+            pltpu.VMEM((local, d), f32),
             pltpu.VMEM((8, d), f32),
             pltpu.VMEM((8, d), f32),
             pltpu.VMEM((n, side, columns), low),
             pltpu.SemaphoreType.DMA((2 * per + 3,)),
-            pltpu.SemaphoreType.DMA((1 + per,)),
+            pltpu.SemaphoreType.DMA((2 + per,)),
             pltpu.SemaphoreType.DMA((2, 3 * per)),
             pltpu.SemaphoreType.DMA((2, 3 * per)),
             *gather_scratch(majors), *gather_scratch(majors), *gather_scratch(majors),
             pltpu.VMEM((2 * per, BLOCK, d), low),
-            pltpu.VMEM((per, BLOCK, d), f32),
             pltpu.VMEM((per, BLOCK, d), low),
             pltpu.SemaphoreType.DMA((2, 2 * per)),
             pltpu.SemaphoreType.DMA((2, per)),
@@ -888,7 +1018,7 @@
     tokens, cotangent, seq_lengths, norm1_gain, norm1_bias, norm2_gain, norm2_bias,
     w_qkv, b_qkv, w_attn_out, w_in, b_in, w_down, b_out, b_down,
 ):
-    output, grad_x, g_qkv, gb_qkv, g_out, g_in, gb_in, g_down, small = layer(
+    output, grad_x, _, g_qkv, gb_qkv, g_out, g_in, gb_in, g_down, small = layer(
         seq_lengths, tokens, cotangent, (norm1_gain, norm1_bias, norm2_gain, norm2_bias),
         w_qkv.transpose(1, 0, 2), b_qkv, w_attn_out, w_in, b_in, w_down.T, (b_out, b_down),
         jnp.asarray(rotary_base()),

time: 179 us -> 153 us (0.85)
  Pallas kernels: 169 us -> 143 us
    pallas_call x1, Pallas kernels: 169 us -> 143 us  [layer(): pl.pallas_call(layer_kernel, name='layer', in_specs=[pl.BlockSpec(memory_...]
where the time goes in v5:
time: 153 us
  Pallas kernels  143 us (93%)
  local copies, waits for them, and re-layouts  8.52 us (6%)
    pallas_call x1, Pallas kernels, layer(): pl.pallas_call(layer_kernel, name='layer', in_specs=[pl.BlockSpec(memory_...  143 us
    unnamed x25, local copies, waits for them, and re-layouts  8.52 us

profile of v5, /device:TPU:0, one launch (start us, length us, event | category | flops | bytes accessed | tf_op | source)
XLA Modules:
  0.0 152.6 jit_solution(17319731634070212564)
XLA Ops:
  1.3 142.7 %layer.1 = (f32[512,768]{1,0:T(8,128)}, f32[512,768]{1,0:T(8,128)}, bf16[8,256,768]{2,1,0:T(8,128)(2,1)}, f32[3,96,192]{2,1,0:T(8,128)}, f32[3,192]{1,0:T(4,128)...) custom-call(s32[1]{0:T(128)S(6)} %copy.34.length_ref, ...), custom_call_target="tpu_custom_call" | custom-call | tf_op jit(solution)/shard_map/layer/pallas_call | solution.py:961
  144.0 0.0 copy-start
  144.0 2.8 %copy.35 = f32[512,768]{1,0:T(8,128)} copy(f32[512,768]{1,0:T(8,128)} %get-tuple-element.36) | data formatting | bytes 3145728
  146.8 0.0 copy-done
  146.8 0.0 copy-start.3
  146.8 0.0 copy-start.7
  146.8 0.0 copy-start.4
  146.8 0.0 copy-start.2
  146.8 0.0 copy-start.6
  146.8 0.0 copy-start.1
  146.8 1.1 copy.36
  148.0 0.0 copy-done.3
  148.0 0.0 copy-start.5
  148.0 0.7 copy.37
  148.7 0.0 copy-done.7
  148.7 0.6 copy.38
  149.3 0.0 copy-done.4
  149.3 0.6 copy.39
  149.9 0.0 copy-done.2
  149.9 0.7 copy.40
  150.7 0.0 copy-done.6
  150.7 0.6 copy.41
  151.3 0.0 copy-done.1
  151.3 0.7 copy.42
  152.0 0.0 copy-done.5
  152.0 0.6 copy.43
Async XLA Ops:
  144.0 2.8 %copy-start = (f32[512,768]{1,0:T(8,128)S(1)}, f32[512,768]{1,0:T(8,128)}, u32[]{:S(2)}) copy-start(f32[512,768]{1,0:T(8,128)} %get-tuple-element.37) | copy-start | bytes 4718596
  146.8 1.2 copy-start.3
  146.8 1.9 %copy-start.7 = (f32[3,192]{1,0:T(4,128)S(1)}, f32[3,192]{1,0:T(4,128)}, u32[]{:S(2)}) copy-start(f32[3,192]{1,0:T(4,128)} %get-tuple-element.39) | copy-start | bytes 6916
  146.8 2.5 %copy-start.4 = (f32[192,96]{1,0:T(8,128)S(1)}, f32[192,96]{1,0:T(8,128)}, u32[]{:S(2)}) copy-start(f32[192,96]{1,0:T(8,128)} %get-tuple-element.40) | copy-start | bytes 221188
  146.8 3.1 %copy-start.2 = (f32[96,768]{1,0:T(8,128)S(1)}, f32[96,768]{1,0:T(8,128)}, u32[]{:S(2)}) copy-start(f32[96,768]{1,0:T(8,128)} %get-tuple-element.41) | copy-start | bytes 884740
  146.8 3.8 %copy-start.6 = (f32[768]{0:T(1024)S(1)}, f32[768]{0:T(1024)}, u32[]{:S(2)}) copy-start(f32[768]{0:T(1024)} %get-tuple-element.42) | copy-start | bytes 9220
  146.8 4.4 %copy-start.1 = (f32[96,768]{1,0:T(8,128)S(1)}, f32[96,768]{1,0:T(8,128)}, u32[]{:S(2)}) copy-start(f32[96,768]{1,0:T(8,128)} %get-tuple-element.25) | copy-start | bytes 884740
  148.0 4.0 %copy-start.5 = (f32[5,768]{1,0:T(8,128)S(1)}, f32[5,768]{1,0:T(8,128)}, u32[]{:S(2)}) copy-start(f32[5,768]{1,0:T(8,128)} %get-tuple-element.44) | copy-start | bytes 46084

commit v6 on v5

--- a/solution.py
+++ b/solution.py
@@ -43,6 +43,13 @@
     return np.concatenate([np.cos(slow), np.sin(slow), np.cos(fast), np.sin(fast)]).astype(
         np.float32
     )
+
+
+def rotary_turned():
+    half = ROT // 2
+    inverse = np.exp(np.arange(half) * (-2.0 * math.log(10000.0) / ROT))
+    angles = inverse[:, None] * np.arange(LMAX)
+    return np.concatenate([np.cos(angles), np.sin(angles)]).astype(np.float32)
 
 
 def rotary_rows(table_ref, block):
@@ -352,7 +359,7 @@
 
 def layer_kernel(
     length_ref, tokens_ref, cot_ref, g1_ref, b1_ref, g2_ref, b2_ref, wq_ref, bq_ref, wo_ref, wi_ref,
-    bi_ref, wd_ref, bo_ref, bd_ref, table_ref,
+    bi_ref, wd_ref, bo_ref, bd_ref, table_ref, turned_ref,
     out_out, gx_out, spill_out, gq_ref, gbq_ref, go_ref, gi_ref, gb_ref, gd_ref, small_ref,
     norm_ref, bias_ref, wq_mine, wd_mine, wq_all, wi_all, wd_all,
     x_all, first_ref, second_ref, cot_all, qkv_ref, qx_ref, dox_ref, context_ref, pool_ref,
@@ -715,6 +722,7 @@
     pool_ref[...] = jnp.zeros_like(pool_ref)
 
     last = blocks - 1
+    half_rot = ROT // 2
 
     def block_of(number):
         return number // 2 + number % 2 * (last - number // 2 * 2)
@@ -772,6 +780,10 @@
         row = lax.broadcasted_iota(jnp.int32, (BLOCK, d), 0) + (here.t * per + c) * BLOCK
         return jnp.where(row < length_ref[0], values, 0.0)
 
+    for c in range(per):
+        cot = kept(c, cot_ref[c * BLOCK : (c + 1) * BLOCK, :].astype(f32))
+        gs_sum[4:5, :] += jnp.sum(cot, axis=0, keepdims=True)
+
     def output_copy():
         return pltpu.make_async_copy(stage_ref.at[:], out_out, out_sems.at[0])
 
@@ -822,20 +834,21 @@
                 at = pl.ds(pl.multiple_of(c * BLOCK, BLOCK), BLOCK)
                 stage_ref[at, :] = tokens_ref[at, :].astype(f32) + kept(c, total)
 
-        tables = rotary_rows(table_ref, now)
+        positions = pl.ds(pl.multiple_of(now * BLOCK, BLOCK), BLOCK)
+        cosine, sine = turned_ref[:half_rot, positions], turned_ref[half_rot:, positions]
+        for slab in (now, 2 * blocks + now):
+            for h in range(heads):
+                near_rows = slice(h * HD, h * HD + half_rot)
+                far_rows = slice(h * HD + half_rot, h * HD + 2 * half_rot)
+                near_part, far_part = pool_ref[slab, near_rows, :], pool_ref[slab, far_rows, :]
+                pool_ref[slab, near_rows, :] = near_part * cosine + far_part * sine
+                pool_ref[slab, far_rows, :] = far_part * cosine - near_part * sine
         filler = jnp.zeros((BLOCK, padded - width), f32)
         turned = [
             jnp.concatenate([pool_ref[k * blocks + now, :width, :].T, filler], axis=1)
             for k in range(3)
         ]
-        projected = jnp.concatenate(
-            [
-                rotate(turned[2] * scale, tables, -1),
-                rotate(turned[0] * scale, tables, -1),
-                turned[1],
-            ],
-            axis=1,
-        )
+        projected = jnp.concatenate([turned[2] * scale, turned[0] * scale, turned[1]], axis=1)
         gb_sum[0:1, :] += jnp.sum(projected, axis=0, keepdims=True)
         proj_low = projected.astype(low)
         @pl.when(step == 0)
@@ -864,9 +877,6 @@
             [gwq_sum[rows_of, k * padded : k * padded + width] for k in range(3)], axis=1
         ).astype(low)
     hand_over(now)
-    for c in range(per):
-        cot = kept(c, cot_ref[c * BLOCK : (c + 1) * BLOCK, :].astype(f32))
-        gs_sum[4:5, :] += jnp.sum(cot, axis=0, keepdims=True)
     final.start_half(0)
     final.start_half(1)
     line_ref[here.dp] = jnp.concatenate(
@@ -927,7 +937,7 @@
         gq_ref[k] = total[:, k * width : (k + 1) * width]
 
 
-def layer(length, tokens, cot, norms, wq, bq, wo, wi, bi, wd, biases, table):
+def layer(length, tokens, cot, norms, wq, bq, wo, wi, bi, wd, biases, table, turned):
     local, d = tokens.shape
     _, side, width = wq.shape
     hidden = wi.shape[1]
@@ -957,7 +967,7 @@
         jax.ShapeDtypeStruct((side, hidden), f32),
         jax.ShapeDtypeStruct((5, d), f32),
     ]
-    args = (tokens, cot, *norms, wq, bq, wo, wi, bi, wd, *biases, table)
+    args = (tokens, cot, *norms, wq, bq, wo, wi, bi, wd, *biases, table, turned)
     return pl.pallas_call(
         layer_kernel,
         name="layer",
@@ -1014,14 +1024,51 @@
     )(length, *args)
 
 
+def settle_kernel(*refs):
+    count = len(refs) // 3
+    sources, targets, held, sems = refs[:count], refs[count : 2 * count], refs[2 * count : -1], refs[-1]
+    taken = [
+        pltpu.make_async_copy(source, buffer, sems.at[0, k])
+        for k, (source, buffer) in enumerate(zip(sources, held))
+    ]
+    put = [
+        pltpu.make_async_copy(buffer, target, sems.at[1, k])
+        for k, (buffer, target) in enumerate(zip(held, targets))
+    ]
+    for copy in taken:
+        copy.start()
+    for before, after in zip(taken, put):
+        before.wait()
+        after.start()
+    for copy in put:
+        copy.wait()
+
+
+def settle(arrays):
+    hbm = pl.BlockSpec(memory_space=pl.ANY)
+    return pl.pallas_call(
+        settle_kernel,
+        name="settle",
+        in_specs=[hbm] * len(arrays),
+        out_specs=[hbm] * len(arrays),
+        out_shape=[jax.ShapeDtypeStruct(a.shape, a.dtype) for a in arrays],
+        scratch_shapes=[pltpu.VMEM(a.shape, a.dtype) for a in arrays]
+        + [pltpu.SemaphoreType.DMA((2, len(arrays)))],
+        compiler_params=pltpu.CompilerParams(vmem_limit_bytes=VMEM),
+    )(*arrays)
+
+
 def per_device(
     tokens, cotangent, seq_lengths, norm1_gain, norm1_bias, norm2_gain, norm2_bias,
     w_qkv, b_qkv, w_attn_out, w_in, b_in, w_down, b_out, b_down,
 ):
-    output, grad_x, _, g_qkv, gb_qkv, g_out, g_in, gb_in, g_down, small = layer(
+    output, grad_x, _, *rest = layer(
         seq_lengths, tokens, cotangent, (norm1_gain, norm1_bias, norm2_gain, norm2_bias),
         w_qkv.transpose(1, 0, 2), b_qkv, w_attn_out, w_in, b_in, w_down.T, (b_out, b_down),
-        jnp.asarray(rotary_base()),
+        jnp.asarray(rotary_base()), jnp.asarray(rotary_turned()),
+    )
+    output, grad_x, g_qkv, gb_qkv, g_out, g_in, gb_in, g_down, small = settle(
+        [output, grad_x, *rest]
     )
     return output, grad_x, g_qkv.transpose(1, 0, 2), gb_qkv, g_out, g_in, gb_in, g_down.T, small
 

time: 153 us -> 145 us (0.948)
  local copies, waits for them, and re-layouts: 8.52 us -> 0 us
    unnamed x25 -> x0, local copies, waits for them, and re-layouts: 8.52 us -> none
    pallas_call x0 -> x1, Pallas kernels: none -> 3.56 us  [settle(): pl.pallas_call(settle_kernel, name='settle', in_specs=[hbm] * len(arrays)...]
    pallas_call x1, Pallas kernels: 143 us -> 140 us  [layer(): pl.pallas_call(layer_kernel, name='layer', in_specs=[pl.BlockSpec(memory_...]
where the time goes in v6:
time: 145 us
  Pallas kernels  144 us (99%)
  between operations  1.46 us (1%)
    pallas_call x1, Pallas kernels, layer(): pl.pallas_call(layer_kernel, name='layer', in_specs=[pl.BlockSpec(memory_...  140 us
    pallas_call x1, Pallas kernels, settle(): pl.pallas_call(settle_kernel, name='settle', in_specs=[hbm] * len(arrays)...  3.56 us

profile of v6, /device:TPU:0, one launch (start us, length us, event | category | flops | bytes accessed | tf_op | source)
XLA Modules:
  0.0 145.3 jit_solution(4716219830909706196)
XLA Ops:
  1.3 140.3 %layer.1 = (f32[512,768]{1,0:T(8,128)}, f32[512,768]{1,0:T(8,128)}, bf16[8,256,768]{2,1,0:T(8,128)(2,1)}, f32[3,96,192]{2,1,0:T(8,128)}, f32[3,192]{1,0:T(4,128)...) custom-call(s32[1]{0:T(128)S(6)} %copy.26.length_ref, ...), custom_call_target="tpu_custom_call" | custom-call | tf_op jit(solution)/shard_map/layer/pallas_call | solution.py:971
  141.6 3.6 %settle.1 = (f32[512,768]{1,0:T(8,128)}, f32[512,768]{1,0:T(8,128)}, f32[3,96,192]{2,1,0:T(8,128)}, f32[3,192]{1,0:T(4,128)}, f32[192,96]{1,0:T(8,128)}, /*index...) custom-call(f32[512,768]{1,0:T(8,128)} %get-tuple-element.27.refs_0_, ...), custom_call_target="tpu_custom_call" | custom-call | tf_op jit(solution)/shard_map/settle/pallas_call | solution.py:1049

commit v7 on v6

--- a/solution.py
+++ b/solution.py
@@ -466,6 +466,7 @@
         rows.forward(c)
     proj_w.forward(here.majors - 1)
     in_w.start()
+    down_w.start()
     cots.start()
     for c in range(per - 1):
         norm(2, c)
@@ -492,10 +493,10 @@
     def _(c):
         project(0, c)
 
+    norm(2, per - 1)
+    project(2, per - 1)
     for k in range(2, here.majors - 1):
         in_w.forward(k)
-    norm(2, per - 1)
-    project(2, per - 1)
     rows.arrived(2, per - 1)
     norm(3, per - 1)
     project(3, per - 1)
@@ -522,13 +523,12 @@
                     body(count // (2 * size) * (2 * size) + k)
 
     in_w.forward(here.majors - 1)
-    down_w.start()
 
     @pl.loop(0, blocks)
     def _(i):
         for k in range(1, here.majors):
 
-            @pl.when(i == min(2 * k, blocks - 1))
+            @pl.when(i == min(2 * k + 1, blocks - 1))
             def _():
                 down_w.forward(k)
 
@@ -791,7 +791,7 @@
     def _(step):
         for k in range(1, here.majors):
 
-            @pl.when(step == min(k - 1, last - 2))
+            @pl.when(step == min(k, last - 2))
             def _():
                 weights.add(k)
 
@@ -806,7 +806,7 @@
 
         for k in range(1, here.majors):
 
-            @pl.when(step == min(k - 1, last - 2))
+            @pl.when(step == min(k, last - 2))
             def _():
                 weights.forward(k)
 

time: 145 us -> 139 us (0.959)
  Pallas kernels: 144 us -> 138 us
    pallas_call x1, Pallas kernels: 140 us -> 134 us  [layer(): pl.pallas_call(layer_kernel, name='layer', in_specs=[pl.BlockSpec(memory_...]
where the time goes in v7:
time: 139 us
  Pallas kernels  138 us (99%)
  between operations  1.46 us (1%)
    pallas_call x1, Pallas kernels, layer(): pl.pallas_call(layer_kernel, name='layer', in_specs=[pl.BlockSpec(memory_...  134 us
    pallas_call x1, Pallas kernels, settle(): pl.pallas_call(settle_kernel, name='settle', in_specs=[hbm] * len(arrays)...  3.56 us

profile of v7, /device:TPU:0, one launch (start us, length us, event | category | flops | bytes accessed | tf_op | source)
XLA Modules:
  0.0 139.0 jit_solution(14384963358410189756)
XLA Ops:
  1.3 134.0 %layer.1 = (f32[512,768]{1,0:T(8,128)}, f32[512,768]{1,0:T(8,128)}, bf16[8,256,768]{2,1,0:T(8,128)(2,1)}, f32[3,96,192]{2,1,0:T(8,128)}, f32[3,192]{1,0:T(4,128)...) custom-call(s32[1]{0:T(128)S(6)} %copy.26.length_ref, ...), custom_call_target="tpu_custom_call" | custom-call | tf_op jit(solution)/shard_map/layer/pallas_call | solution.py:971
  135.3 3.6 %settle.1 = (f32[512,768]{1,0:T(8,128)}, f32[512,768]{1,0:T(8,128)}, f32[3,96,192]{2,1,0:T(8,128)}, f32[3,192]{1,0:T(4,128)}, f32[192,96]{1,0:T(8,128)}, /*index...) custom-call(f32[512,768]{1,0:T(8,128)} %get-tuple-element.27.refs_0_, ...), custom_call_target="tpu_custom_call" | custom-call | tf_op jit(solution)/shard_map/settle/pallas_call | solution.py:1049
